TPU v7x, 512 devices: a whole 4x8x8 slice. The times are simulated.
512 devices in a mesh: ctx: 64 (over z, y), head: 2 (over core), pair: 4 (over x).
Axes of the slice: x: 4, y: 8, z: 8, core: 2. Of those that a mesh axis runs over, the one named last changes fastest.
Arguments:
- tokens_in: bfloat16 [2, 4096, 2048], P(None, ('ctx', 'pair')), may hold values from -6 to 6
- attn_gain: float32 [2048], replicated, may hold values from 0.1 to 1.9
- query_matrix: bfloat16 [2048, 2048], P(None, ('head', 'pair')), may hold values from -20 to 20
- key_matrix: bfloat16 [256, 2048], P(('head', 'pair')), may hold values from -1 to 1
- value_matrix: bfloat16 [256, 2048], P(('head', 'pair')), may hold values from -0.125 to 0.125
- output_matrix: bfloat16 [2048, 2048], P(None, ('head', 'pair')), may hold values from -0.125 to 0.125
- moe_gain: float32 [2048], replicated, may hold values from 0.1 to 1.9
- chosen_experts: int32 [2, 4096, 8], P('head', ('ctx', 'pair')), may hold values from 0 to 127, all different within a row; in each aligned block of 16 rows (0 to 15, 16 to 31, ..., all dimensions but the last counted through in order) at most 2 rows name the same one
- combine_weights: float32 [2, 4096, 8], P('head', ('ctx', 'pair')), may hold values from 0.02 to 0.5
- gate_weight: bfloat16 [128, 768, 2048], P(('ctx', 'head'), 'pair'), may hold values from -0.125 to 0.125
- up_weight: bfloat16 [128, 768, 2048], P(('ctx', 'head'), 'pair'), may hold values from -0.125 to 0.125
- down_weight: bfloat16 [128, 768, 2048], P(('ctx', 'head'), 'pair'), may hold values from -0.21875 to 0.21875
Outputs:
- layer_out: bfloat16 [2, 4096, 2048], P('head', ('ctx', 'pair'))
Inputs may be any that keep to these rules, and one draw needn't show every extreme that they name: `chosen_experts`: each token names 8 different experts; among the 16 tokens of one sequence that one device holds, no expert is named more than 2 times.
All inputs are finite; a program needn't handle non-finite values.
Results may differ from a plain program's by a relative error of at most 0.013.
Values may be sent and summed in bfloat16 or wider, within the bound.
No kernel may reach another device: no remote copies, remote signals or barrier semaphores. Data moves between devices by JAX's collectives and lax.ppermute only.
A program may use at most 64 MiB of HBM per device.

v0:
```python
import jax
import jax.numpy as jnp
from jax import lax
from jax.sharding import PartitionSpec as P

ROPE_BASE = 1000000.0
EPSILON = 1e-06
MASKED = -1e30


def in_order(tiles, dim):
    lengths = list(tiles.shape[1:])
    lengths[dim] *= tiles.shape[0]
    return jnp.moveaxis(tiles, 0, dim).reshape(lengths)


def copy_for_each(shard, axis):
    size = lax.axis_size(axis)
    return lax.all_to_all(
        jnp.broadcast_to(shard[None], (size, *shard.shape)), axis, 0, 0, tiled=True
    )


def collect(shard, axis, dim):
    return in_order(copy_for_each(shard, axis), dim)


def rows_first(arrays, axis, dims):
    turned = [jnp.moveaxis(a, dim, 0) for a, dim in zip(arrays, dims)]
    both = jnp.concatenate([t.reshape(len(t), -1) for t in turned], axis=1)
    whole, at, done = (lax.all_gather(both, axis, axis=0, tiled=True), 0, [])
    for t, dim in zip(turned, dims):
        slab = whole[:, at : at + t[0].size].reshape(-1, *t.shape[1:])
        done.append(jnp.moveaxis(slab, 0, dim))
        at += t[0].size
    return tuple(done)


def in_one_piece(arrays, axis, dim, along):
    ends, at = ([], 0)
    for a in arrays[:-1]:
        at += a.shape[along]
        ends.append(at)
    both = jnp.concatenate(arrays, axis=along)
    return tuple(jnp.split(lax.all_gather(both, axis, axis=dim, tiled=True), ends, axis=along))


def normalize(values, gain_vector):
    wide = values.astype(jnp.float32)
    mean_square = jnp.mean(wide * wide, axis=-1, keepdims=True)
    return (wide * lax.rsqrt(mean_square + EPSILON) * gain_vector).astype(jnp.bfloat16)


def rotate(values, positions):
    half_dim = values.shape[-1] // 2
    frequency = ROPE_BASE ** (-(jnp.arange(half_dim).astype(jnp.float32) * 2.0) / values.shape[-1])
    angles = positions[:, None] * frequency[None, :]
    cosine_part = jnp.cos(angles)[:, None, :]
    sine_part = jnp.sin(angles)[:, None, :]
    lower_half = values[..., :half_dim]
    upper_half = values[..., half_dim:]
    return jnp.concatenate(
        [
            lower_half * cosine_part - upper_half * sine_part,
            upper_half * cosine_part + lower_half * sine_part,
        ],
        axis=-1,
    )


def body(
    tokens_in,
    attn_gain,
    query_matrix,
    key_matrix,
    value_matrix,
    output_matrix,
    moe_gain,
    chosen_experts,
    combine_weights,
    gate_weight,
    up_weight,
    down_weight,
):
    pair_count = lax.axis_size("pair")
    head_count = lax.axis_size("head")
    ctx_count = lax.axis_size("ctx")
    seq_count, own_len, model_width = tokens_in.shape
    block_len = own_len * pair_count
    normalized_input = normalize(tokens_in, attn_gain)
    block_rows = collect(normalized_input, "pair", 1)
    block_start = lax.axis_index("ctx") * block_len
    query_pos = block_start + jnp.arange(block_len)
    positions = query_pos.astype(jnp.float32)
    key_part = jnp.einsum("spd,hd->sph", block_rows, key_matrix, preferred_element_type=jnp.float32)
    value_part = jnp.einsum(
        "spd,hd->sph", block_rows, value_matrix, preferred_element_type=jnp.float32
    )
    key_full, value_full = tuple(
        (
            part.astype(jnp.float32)
            for part in rows_first(
                (key_part.astype(jnp.bfloat16), value_part.astype(jnp.bfloat16)), "pair", (2, 2)
            )
        )
    )
    head_dim = key_full.shape[2]
    local_heads = query_matrix.shape[1] // head_dim
    query_unrotated = jnp.einsum(
        "spd,dh->sph", block_rows, query_matrix, preferred_element_type=jnp.float32
    )
    queries = rotate(
        query_unrotated.reshape(seq_count, block_len, local_heads, head_dim), positions
    ).astype(jnp.bfloat16)
    rotated_keys = rotate(key_full.reshape(seq_count, block_len, 1, head_dim), positions)[
        :, :, 0
    ].astype(jnp.bfloat16)
    every_value_row = value_full.astype(jnp.bfloat16)
    scaling = head_dim ** (-0.5)
    last_query = block_start + block_len - 1
    start_state = (
        jnp.full((seq_count, block_len, local_heads), MASKED, jnp.float32),
        jnp.zeros((seq_count, block_len, local_heads), jnp.float32),
        jnp.zeros((seq_count, block_len, local_heads, head_dim), jnp.float32),
    )
    key_rows, value_rows = in_one_piece((rotated_keys, every_value_row), "ctx", 1, 0)
    key_span = key_rows.shape[1]

    def compute(running_state):
        row_peak, denominator, accumulated = running_state
        key_pos = jnp.arange(key_span)
        allowed = (key_pos[None, :] <= query_pos[:, None])[None, :, None, :]
        scores = (
            jnp.einsum("sphd,skd->sphk", queries, key_rows, preferred_element_type=jnp.float32)
            * scaling
        )
        scores = jnp.where(allowed, scores, MASKED)
        new_peak = jnp.maximum(row_peak, jnp.max(scores, axis=-1))
        weights = jnp.where(allowed, jnp.exp(scores - new_peak[..., None]), 0.0)
        denominator = jnp.sum(weights, axis=-1)
        accumulated = jnp.einsum(
            "sphk,skd->sphd",
            weights.astype(jnp.bfloat16),
            value_rows,
            preferred_element_type=jnp.float32,
        )
        return (new_peak, denominator, accumulated)

    row_peak, denominator, accumulated = lax.cond(
        jnp.int32(0) > last_query, lambda skipped: skipped, compute, start_state
    )
    attended = (
        (accumulated / denominator[..., None])
        .astype(jnp.bfloat16)
        .reshape(seq_count, block_len, local_heads * head_dim)
    )
    projected = jnp.einsum(
        "sph,hc->spc",
        collect(attended, ("head", "pair"), 2),
        output_matrix,
        preferred_element_type=jnp.float32,
    )
    projected = projected.astype(jnp.bfloat16).reshape(
        seq_count * pair_count, own_len, output_matrix.shape[1]
    )
    owned_rows = lax.all_to_all(
        projected, ("head", "pair"), split_axis=0, concat_axis=2, tiled=True
    )[0]
    own_tokens = lax.dynamic_index_in_dim(tokens_in, lax.axis_index("head"), 0, keepdims=False)
    residual = (own_tokens.astype(jnp.float32) + owned_rows.astype(jnp.float32)).astype(
        jnp.bfloat16
    )
    moe_in = normalize(residual, moe_gain)
    expert_total = ctx_count * head_count
    top_count = chosen_experts.shape[-1]
    capacity = max(2, (own_len * top_count + expert_total - 1) // expert_total + 1)
    picked = chosen_experts.reshape(own_len, top_count)
    member = (picked[..., None] == jnp.arange(expert_total)[None, None, :]).astype(jnp.int32)
    running = jnp.cumsum(member.reshape(own_len * top_count, expert_total), axis=0).reshape(
        own_len, top_count, expert_total
    )
    slot_rank = jnp.sum((running - 1) * member, axis=-1)
    slot_ids = picked * capacity + slot_rank
    placing = jnp.any(
        slot_ids[..., None] == jnp.arange(expert_total * capacity)[None, None, :], axis=1
    ).astype(jnp.bfloat16)
    outgoing = jnp.einsum("ts,td->sd", placing, moe_in, preferred_element_type=jnp.float32).astype(
        jnp.bfloat16
    )
    incoming = lax.all_to_all(
        outgoing.reshape(expert_total, capacity, model_width),
        ("ctx", "head"),
        split_axis=0,
        concat_axis=0,
        tiled=True,
    )
    incoming = incoming.reshape(expert_total * capacity, model_width)
    slot_rows = incoming.shape[0]
    gate_local = gate_weight[0]
    up_local = up_weight[0]
    down_local = down_weight[0]
    quarter = gate_local.shape[0]
    totals = jnp.zeros((slot_rows, model_width), jnp.float32)
    gate_rows_w, up_rows_w, down_rows_w = in_one_piece(
        (gate_local, up_local, down_local), "pair", 0, 1
    )
    for part_id in range(gate_rows_w.shape[0] // quarter):
        lower_row = part_id * quarter
        gate_part = lax.dot_general(
            gate_rows_w[lower_row : lower_row + quarter],
            incoming,
            (((1,), (1,)), ((), ())),
            preferred_element_type=jnp.float32,
        )
        up_part = lax.dot_general(
            up_rows_w[lower_row : lower_row + quarter],
            incoming,
            (((1,), (1,)), ((), ())),
            preferred_element_type=jnp.float32,
        )
        hidden = (jax.nn.silu(gate_part) * up_part).astype(jnp.bfloat16)
        partial_value = lax.dot_general(
            hidden,
            down_rows_w[lower_row : lower_row + quarter],
            (((0,), (0,)), ((), ())),
            preferred_element_type=jnp.float32,
        )
        totals = totals + lax.optimization_barrier(partial_value.astype(jnp.bfloat16)).astype(
            jnp.float32
        )
    expert_out = totals
    expert_out = expert_out.astype(jnp.bfloat16)
    returned = lax.all_to_all(
        expert_out.reshape(expert_total, capacity, model_width),
        ("ctx", "head"),
        split_axis=0,
        concat_axis=0,
        tiled=True,
    )
    returned = returned.reshape(expert_total * capacity, model_width)
    gathered = returned[slot_ids.reshape(-1)].reshape(own_len, top_count, model_width)
    weights_here = combine_weights.reshape(own_len, top_count)
    mixture = jnp.sum(weights_here[..., None] * gathered.astype(jnp.float32), axis=1)
    layer_out = (residual.astype(jnp.float32) + mixture).astype(jnp.bfloat16)
    return layer_out[None]


def solution(mesh):
    return jax.shard_map(
        body,
        mesh=mesh,
        in_specs=(
            P(None, ("ctx", "pair"), None),
            P(),
            P(None, ("head", "pair")),
            P(("head", "pair"), None),
            P(("head", "pair"), None),
            P(None, ("head", "pair")),
            P(),
            P("head", ("ctx", "pair"), None),
            P("head", ("ctx", "pair"), None),
            P(("ctx", "head"), "pair", None),
            P(("ctx", "head"), "pair", None),
            P(("ctx", "head"), "pair", None),
        ),
        out_specs=P("head", ("ctx", "pair"), None),
        check_vma=False,
    )
```

profile of v0, /device:TPU:1, one launch (start us, length us, event | category | flops | bytes accessed | tf_op | source)
XLA Modules:
  0.0 309.3 jit_solution(10895587120673009331)
XLA Ops:
  6.5 1.1 fusion.41
  7.7 1.0 fusion.43
  8.7 0.9 broadcast_in_dim.37
  9.6 4.8 %all-to-all-start = ((bf16[4,2,16,2048]{3,2,1,0:T(8,128)(2,1)}), bf16[4,2,16,2048]{3,2,1,0:T(8,128)(2,1)S(1)}, u32[]{:S(2)}, u32[]{:S(2)}) async-start(bf16[4,2,16,2048]{3,2,1,0:T(8,128)(2,1)} %broadcast_in_dim.37), calls=%async_computation | async-start | bytes 1048576 | tf_op jit(solution)/shard_map/all_to_all | solution.py:19
  14.4 0.2 multiply_cosine_fusion
  14.6 6.7 %all-to-all-done = bf16[4,2,16,2048]{3,2,1,0:T(8,128)(2,1)S(1)} async-done(((bf16[4,2,16,2048]{3,2,1,0:T(8,128)(2,1)}), bf16[4,2,16,2048]{3,2,1,0:T(8,128)(2,1)S(1)}, u32[]{:S(2)}, u32[]{:S(2)}) %all-to-all-start) | async-done | bytes 524320 | tf_op jit(solution)/shard_map/all_to_all | solution.py:19
  21.4 1.3 fusion.17
  22.8 1.3 fusion.18
  24.1 9.0 %all_gather.9 = bf16[128,256]{1,0:T(8,128)(2,1)S(1)} all-gather(bf16[32,256]{1,0:T(8,128)(2,1)S(1)} %pad_maximum_fusion.3), channel_id=1, replica_groups=mesh['ctx'=64,'head'=2,'pair'=4] {'pair'}, dimensions={0}, use_global_device_ids=true | all-gather | bytes 81920 | tf_op jit(solution)/shard_map/all_gather | solution.py:31
  33.5 0.6 pad_maximum_fusion.1
  34.3 3.0 pad_maximum_fusion
  37.3 1.5 copy.83
  38.9 0.5 fusion.90
  39.6 86.1 %all-gather.3.cloned.1.call-done = bf16[4,4096,128]{2,1,0:T(8,128)(2,1)} async-done(((bf16[4,64,128]{2,1,0:T(8,128)(2,1)}), bf16[4,4096,128]{2,1,0:T(8,128)(2,1)}) %all-gather.3.cloned.1.call-update) | async-done | bytes 4194320 | tf_op jit(solution)/shard_map/all_gather | solution.py:45
  125.7 5.0 %conditional.1 = (f32[2,64,2]{1,2,0:T(2,128)S(1)}, f32[2,64,2,128]{3,1,2,0:T(8,128)S(1)}) conditional(s32[]{:T(128)} %convert_element_type.170, (s32[]{:T(128)}, s32[64]{0:T(128)S(1)}, bf16[4,4096,128]{2,1,0:T(8,128)(2,1)}, bf16[2,64,2,128]{3,1,2,0:T(8,128)(2,1)S(1)}) %tuple.13, () %tuple.14), branch_computations={%region_1.4_spmd, %region_4.5_spmd} | conditional | flops 546570048 | bytes 34807600 | solution.py:149
  125.7 0.2 iota_compare_fusion
  126.0 2.8 fusion.89
  128.7 0.9 fusion.3
  129.7 1.0 fusion.2
  130.8 0.8 broadcast_in_dim.39
  131.7 9.2 %all-to-all-start.1 = ((bf16[8,2,64,256]{3,2,1,0:T(8,128)(2,1)}), bf16[8,2,64,256]{3,2,1,0:T(8,128)(2,1)S(1)}, u32[]{:S(2)}, u32[]{:S(2)}) async-start(bf16[8,2,64,256]{3,2,1,0:T(8,128)(2,1)} %broadcast_in_dim.39), calls=%async_computation.1 | async-start | bytes 1048576 | tf_op jit(solution)/shard_map/all_to_all | solution.py:19
  140.9 0.2 reduce_window_sum.11
  141.1 0.2 select_reduce_fusion
  141.5 10.2 %all-to-all-done.1 = bf16[8,2,64,256]{3,2,1,0:T(8,128)(2,1)S(1)} async-done(((bf16[8,2,64,256]{3,2,1,0:T(8,128)(2,1)}), bf16[8,2,64,256]{3,2,1,0:T(8,128)(2,1)S(1)}, u32[]{:S(2)}, u32[]{:S(2)}) %all-to-all-start.1) | async-done | bytes 524320 | tf_op jit(solution)/shard_map/all_to_all | solution.py:19
  151.8 1.0 convolution_convert_fusion.5
  152.7 3.3 %all-to-all-start.2 = ((bf16[8,16,256]{2,1,0:T(8,128)(2,1)}), bf16[8,16,256]{2,1,0:T(8,128)(2,1)S(1)}, u32[]{:S(2)}, u32[]{:S(2)}) async-start(bf16[8,16,256]{2,1,0:T(8,128)(2,1)} %bitcast.25), calls=%async_computation.2 | async-start | bytes 131072 | tf_op jit(solution)/shard_map/all_to_all | solution.py:166
  156.2 4.8 %all-to-all-done.2 = bf16[8,16,256]{2,1,0:T(8,128)(2,1)S(1)} async-done(((bf16[8,16,256]{2,1,0:T(8,128)(2,1)}), bf16[8,16,256]{2,1,0:T(8,128)(2,1)S(1)}, u32[]{:S(2)}, u32[]{:S(2)}) %all-to-all-start.2) | async-done | bytes 65568 | tf_op jit(solution)/shard_map/all_to_all | solution.py:166
  161.1 0.5 convolution_convert_fusion
  161.6 0.7 reshape.215
  162.4 38.9 %all_to_all.29 = bf16[128,2,2048]{2,1,0:T(2,128)(2,1)S(1)} all-to-all(bf16[128,2,2048]{2,1,0:T(2,128)(2,1)S(1)} %reshape.215), channel_id=1, replica_groups=mesh['ctx'=64,'head'=2,'pair'=4] {'ctx','head'}, dimensions={0} | all-to-all | bytes 2097152 | tf_op jit(solution)/shard_map/all_to_all | solution.py:190
  201.3 0.4 reshape.216
  201.7 25.5 %all-gather.5.cloned.1.call-done = bf16[768,6144]{1,0:T(8,128)(2,1)} async-done(((bf16[192,6144]{1,0:T(8,128)(2,1)}), bf16[768,6144]{1,0:T(8,128)(2,1)}) %all-gather.5.cloned.1.call-update) | async-done | bytes 9437200 | tf_op jit(solution)/shard_map/all_gather | solution.py:45
  227.2 2.3 fusion.39
  229.5 3.3 %convolution_convert_fusion.4 = bf16[256,2048]{1,0:T(8,128)(2,1)S(1)} fusion(bf16[256,2048]{1,0:T(8,128)(2,1)} %copy-done.2, bf16[768,6144]{1,0:T(8,128)(2,1)} %all-gather.5.cloned.1.call-done, f32[192,256]{1,0:T(8,128)} %fusion.39), kind=kOutput, calls=%fused_computation.22 | convolution fusion | flops 403472384 | bytes 3866624 | tf_op jit(solution)/shard_map/dot_general | solution.py:222
  232.8 2.3 fusion.34
  235.1 3.9 %convolution_convert_fusion.3 = bf16[256,2048]{1,0:T(8,128)(2,1)} fusion(bf16[256,2048]{1,0:T(8,128)(2,1)S(1)} %copy-done.3, bf16[768,6144]{1,0:T(8,128)(2,1)} %all-gather.5.cloned.1.call-done, f32[192,256]{1,0:T(8,128)} %fusion.34), kind=kOutput, calls=%fused_computation.21 | convolution fusion | flops 403472384 | bytes 3866624 | tf_op jit(solution)/shard_map/dot_general | solution.py:222
  239.0 2.3 fusion.29
  241.3 3.9 %convolution_convert_fusion.2 = bf16[256,2048]{1,0:T(8,128)(2,1)} fusion(bf16[256,2048]{1,0:T(8,128)(2,1)S(1)} %copy-done.3, bf16[768,6144]{1,0:T(8,128)(2,1)} %all-gather.5.cloned.1.call-done, f32[192,256]{1,0:T(8,128)} %fusion.29), kind=kOutput, calls=%fused_computation.20 | convolution fusion | flops 403472384 | bytes 3866624 | tf_op jit(solution)/shard_map/dot_general | solution.py:222
  245.2 2.3 fusion.24
  247.5 3.9 %convolution_convert_fusion.1 = bf16[256,2048]{1,0:T(8,128)(2,1)} fusion(bf16[256,2048]{1,0:T(8,128)(2,1)S(1)} %copy-done.3, bf16[768,6144]{1,0:T(8,128)(2,1)} %all-gather.5.cloned.1.call-done, f32[192,256]{1,0:T(8,128)} %fusion.24), kind=kOutput, calls=%fused_computation.19 | convolution fusion | flops 403472384 | bytes 3866624 | tf_op jit(solution)/shard_map/dot_general | solution.py:222
  251.4 2.6 add_convert_fusion
  254.0 1.5 reshape.217
  255.5 13.5 %all-to-all-start.4 = ((bf16[128,2,2048]{2,1,0:T(2,128)(2,1)}), bf16[128,2,2048]{2,1,0:T(2,128)(2,1)S(1)}, u32[]{:S(2)}, u32[]{:S(2)}) async-start(bf16[128,2,2048]{2,1,0:T(2,128)(2,1)} %reshape.217), calls=%async_computation.4 | async-start | bytes 2097152 | tf_op jit(solution)/shard_map/all_to_all | solution.py:233
  269.3 30.7 %all-to-all-done.4 = bf16[128,2,2048]{2,1,0:T(2,128)(2,1)S(1)} async-done(((bf16[128,2,2048]{2,1,0:T(2,128)(2,1)}), bf16[128,2,2048]{2,1,0:T(2,128)(2,1)S(1)}, u32[]{:S(2)}, u32[]{:S(2)}) %all-to-all-start.4) | async-done | bytes 1048608 | tf_op jit(solution)/shard_map/all_to_all | solution.py:233
  300.0 0.4 reshape.218
  300.4 0.9 gather_fusion
  301.4 0.4 fusion.19
  301.8 0.7 fusion.70
  (62 shorter events, 2.2 us)
Async XLA Ops:
  6.5 145.2 %copy-start = (bf16[2048,256]{1,0:T(8,128)(2,1)S(1)}, bf16[2048,256]{1,0:T(8,128)(2,1)}, u32[]{:S(2)}) copy-start(bf16[2048,256]{1,0:T(8,128)(2,1)} %param.19) | copy-start | bytes 3145732
  6.5 27.7 %copy-start.4 = (bf16[1,192,2048]{2,1,0:T(8,128)(2,1)S(1)}, bf16[1,192,2048]{2,1,0:T(8,128)(2,1)}, u32[]{:S(2)}) copy-start(bf16[1,192,2048]{2,1,0:T(8,128)(2,1)} %param.25) | copy-start | bytes 2359300
  9.6 11.8 %all-to-all-start = ((bf16[4,2,16,2048]{3,2,1,0:T(8,128)(2,1)}), bf16[4,2,16,2048]{3,2,1,0:T(8,128)(2,1)S(1)}, u32[]{:S(2)}, u32[]{:S(2)}) async-start(bf16[4,2,16,2048]{3,2,1,0:T(8,128)(2,1)} %broadcast_in_dim.37), calls=%async_computation | async-start | bytes 1048576 | tf_op jit(solution)/shard_map/all_to_all | solution.py:19
  14.4 111.3 %all-gather.3.cloned.1.call-start = ((), (), s32[]{:S(2)}) async-start(), calls=%async_computation.5 | async-start | bytes 4259840 | tf_op jit(solution)/shard_map/all_gather | solution.py:45
  34.2 193.0 %all-gather.5.cloned.1.call-start = ((), (), s32[]{:S(2)}) async-start(), calls=%async_computation.6 | async-start | bytes 11796480 | tf_op jit(solution)/shard_map/all_gather | solution.py:45
  34.3 4.5 %copy-start.5 = (s32[1,16,8]{1,2,0:T(8,128)S(1)}, s32[1,16,8]{1,2,0:T(8,128)}, u32[]{:S(2)}) copy-start(s32[1,16,8]{1,2,0:T(8,128)} %param.21) | copy-start | bytes 1540
  125.7 3.0 copy-start.8
  130.7 30.3 %copy-start.1 = (bf16[2,16,2048]{2,1,0:T(8,128)(2,1)S(1)}, bf16[2,16,2048]{2,1,0:T(8,128)(2,1)}, u32[]{:S(2)}) copy-start(bf16[2,16,2048]{2,1,0:T(8,128)(2,1)} %param.14) | copy-start | bytes 393220
  130.7 30.4 %copy-start.6 = (f32[2048]{0:T(1024)S(1)}, f32[2048]{0:T(1024)}, u32[]{:S(2)}) copy-start(f32[2048]{0:T(1024)} %param.20) | copy-start | bytes 24580
  131.7 20.0 %all-to-all-start.1 = ((bf16[8,2,64,256]{3,2,1,0:T(8,128)(2,1)}), bf16[8,2,64,256]{3,2,1,0:T(8,128)(2,1)S(1)}, u32[]{:S(2)}, u32[]{:S(2)}) async-start(bf16[8,2,64,256]{3,2,1,0:T(8,128)(2,1)} %broadcast_in_dim.39), calls=%async_computation.1 | async-start | bytes 1048576 | tf_op jit(solution)/shard_map/all_to_all | solution.py:19
  152.7 8.2 %all-to-all-start.2 = ((bf16[8,16,256]{2,1,0:T(8,128)(2,1)}), bf16[8,16,256]{2,1,0:T(8,128)(2,1)S(1)}, u32[]{:S(2)}, u32[]{:S(2)}) async-start(bf16[8,16,256]{2,1,0:T(8,128)(2,1)} %bitcast.25), calls=%async_computation.2 | async-start | bytes 131072 | tf_op jit(solution)/shard_map/all_to_all | solution.py:166
  201.7 25.5 %copy-start.2 = (bf16[256,2048]{1,0:T(8,128)(2,1)}, bf16[256,2048]{1,0:T(8,128)(2,1)S(1)}, u32[]{:S(2)}) copy-start(bf16[256,2048]{1,0:T(8,128)(2,1)S(1)} %reshape.216) | copy-start | bytes 3145732
  229.5 3.3 %copy-start.3 = (bf16[256,2048]{1,0:T(8,128)(2,1)S(1)}, bf16[256,2048]{1,0:T(8,128)(2,1)}, u32[]{:S(2)}) copy-start(bf16[256,2048]{1,0:T(8,128)(2,1)} %copy-done.2) | copy-start | bytes 3145732
  251.4 17.8 %copy-start.7 = (f32[1,16,8]{1,2,0:T(8,128)S(1)}, f32[1,16,8]{1,2,0:T(8,128)}, u32[]{:S(2)}) copy-start(f32[1,16,8]{1,2,0:T(8,128)} %param.22) | copy-start | bytes 1540
  255.5 44.5 %all-to-all-start.4 = ((bf16[128,2,2048]{2,1,0:T(2,128)(2,1)}), bf16[128,2,2048]{2,1,0:T(2,128)(2,1)S(1)}, u32[]{:S(2)}, u32[]{:S(2)}) async-start(bf16[128,2,2048]{2,1,0:T(2,128)(2,1)} %reshape.217), calls=%async_computation.4 | async-start | bytes 2097152 | tf_op jit(solution)/shard_map/all_to_all | solution.py:233
Sparse Core Ops, SparseCore 0:
  34.3 91.3 all-gather.2
  127.8 99.3 all-gather.4
where the time goes:
time: 310 us; the launch traced here: 309 us
  waiting for transfers between devices  164 us (53%)
  blocking collectives  47.9 us (15%)
  matrix products  32.3 us (10%)
  starting transfers between devices  30.9 us (10%)
  between operations  13.7 us (4%)
  other arithmetic  12.1 us (4%)
  local copies, waits for them, and re-layouts  8.36 us (3%)
    all_gather x2, waiting for transfers between devices, in_one_piece(): lax.all_gather(both, axis, axis=dim, tiled=True)  112 us
    all_to_all x1, blocking collectives, body(): lax.all_to_all(outgoing.reshape(expert_total, capacity, model_width), ('c...  38.9 us
    all_to_all x1, waiting for transfers between devices, body(): lax.all_to_all(expert_out.reshape(expert_total, capacity, model_width), (...  30.7 us
    all_to_all x2, waiting for transfers between devices, copy_for_each(): lax.all_to_all(jnp.broadcast_to(shard[None], (size, *shard.shape)), axis,...  16.9 us
    dot_general x4, matrix products, body(): lax.dot_general(hidden, down_rows_w[lower_row:lower_row + quarter], (((0,...  14.9 us
    all_to_all x2, starting transfers between devices, copy_for_each(): lax.all_to_all(jnp.broadcast_to(shard[None], (size, *shard.shape)), axis,...  14 us
    all_to_all x1, starting transfers between devices, body(): lax.all_to_all(expert_out.reshape(expert_total, capacity, model_width), (...  13.5 us
    dot_general x4, matrix products, body(): lax.dot_general(gate_rows_w[lower_row:lower_row + quarter], incoming, (((...  9.26 us
  transfers between devices with their start and end apart: 6, of which 6 were waited for; matrix products, arithmetic and copies ran while one was open for 5% of the time, Pallas kernels for 0%

commit v1 on v0

v1 whole, which is shorter than its diff:
```python
import jax
import jax.numpy as jnp
from jax import lax
from jax.sharding import PartitionSpec as P

ROPE_BASE = 1000000.0
EPSILON = 1e-06
MASKED = -1e30
F32 = jnp.float32
BF16 = jnp.bfloat16


def exchange(tiles, axis):
    return lax.all_to_all(tiles, axis, 0, 0, tiled=True)


def for_each(shard, count):
    return jnp.broadcast_to(shard[None], (count, *shard.shape))


def dot(a, b, a_dim, b_dim):
    return lax.dot_general(a, b, (((a_dim,), (b_dim,)), ((), ())), preferred_element_type=F32)


def normalize(values, gain_vector):
    wide = values.astype(F32)
    mean_square = jnp.mean(wide * wide, axis=-1, keepdims=True)
    return (wide * lax.rsqrt(mean_square + EPSILON) * gain_vector).astype(BF16)


def rope_tables(positions, head_dim):
    half_dim = head_dim // 2
    frequency = ROPE_BASE ** (-(jnp.arange(half_dim).astype(F32) * 2.0) / head_dim)
    angles = positions[:, None] * frequency[None, :]
    return jnp.cos(angles), jnp.sin(angles)


def rotate(values, tables):
    cosine_part, sine_part = tables
    half_dim = values.shape[-1] // 2
    lower_half = values[..., :half_dim]
    upper_half = values[..., half_dim:]
    return jnp.concatenate(
        [
            lower_half * cosine_part - upper_half * sine_part,
            upper_half * cosine_part + lower_half * sine_part,
        ],
        axis=-1,
    ).astype(BF16)


def rounded(values):
    return lax.reduce_precision(values, 8, 7)


def pieces(values):
    high = rounded(values)
    middle = rounded(values - high)
    return [high, middle, rounded(values - high - middle)]


def body(
    tokens_in,
    attn_gain,
    query_matrix,
    key_matrix,
    value_matrix,
    output_matrix,
    moe_gain,
    chosen_experts,
    combine_weights,
    gate_weight,
    up_weight,
    down_weight,
):
    pairs = lax.axis_size("pair")
    heads = lax.axis_size("head")
    blocks = lax.axis_size("ctx")
    seqs, own_len, width = tokens_in.shape
    own_rows = seqs * own_len
    rows = pairs * own_rows
    block_len = own_len * pairs
    q_cols = query_matrix.shape[1]
    part_cols = key_matrix.shape[0]
    head_dim = part_cols * pairs
    local_heads = q_cols // head_dim
    group = local_heads * pairs

    weights = lax.all_gather(
        jnp.concatenate([gate_weight[0], up_weight[0], down_weight[0]], axis=1),
        "pair",
        axis=0,
        tiled=True,
    )

    normed = normalize(tokens_in, attn_gain)
    block_rows = exchange(for_each(normed, pairs), "pair").reshape(rows, width)
    block_start = lax.axis_index("ctx") * block_len
    own_start = block_start + lax.axis_index("pair") * own_len
    places = jnp.arange(own_len)
    row_pos = block_start + (
        jnp.arange(pairs)[:, None, None] * own_len + jnp.zeros((seqs, 1), jnp.int32) + places
    ).reshape(rows)
    q_tables = rope_tables(row_pos.astype(F32), head_dim)
    key_value = dot(
        block_rows, jnp.concatenate([key_matrix, value_matrix], axis=0), 1, 1
    ).astype(BF16)
    query_raw = dot(block_rows, query_matrix, 1, 0)
    query = jnp.concatenate(
        [
            rotate(query_raw[:, j * head_dim : (j + 1) * head_dim], q_tables)
            for j in range(local_heads)
        ],
        axis=1,
    )
    swapped = exchange(
        jnp.concatenate(
            [
                for_each(query, pairs),
                jnp.pad(
                    key_value.reshape(pairs, own_rows, 2 * part_cols),
                    ((0, 0), (0, 0), (0, q_cols - 2 * part_cols)),
                ),
            ],
            axis=1,
        ),
        "pair",
    )
    own_pos = (own_start + jnp.zeros((seqs, 1), jnp.int32) + places).reshape(own_rows)
    key_own = jnp.concatenate([swapped[p, rows:, :part_cols] for p in range(pairs)], axis=1)
    value_own = jnp.concatenate(
        [swapped[p, rows:, part_cols : 2 * part_cols] for p in range(pairs)], axis=1
    )
    key_own = rotate(key_own.astype(F32), rope_tables(own_pos.astype(F32), head_dim))
    both = jnp.concatenate([key_own, value_own], axis=1)
    spread = exchange(for_each(both, blocks), "ctx").reshape(blocks, seqs, own_len, 2 * head_dim)
    spread = jnp.moveaxis(spread, 1, 0).reshape(seqs, blocks * own_len, 2 * head_dim)
    keys = spread[..., :head_dim]
    values = spread[..., head_dim:]

    queries = (
        swapped[:, :rows]
        .reshape(pairs, pairs, seqs, own_len, local_heads, head_dim)
        .transpose(2, 0, 4, 1, 3, 5)
        .reshape(seqs, group * block_len, head_dim)
    )
    key_pos = (
        jnp.arange(blocks)[:, None] * block_len + lax.axis_index("pair") * own_len + places
    ).reshape(1, blocks * own_len)
    query_pos = (jnp.zeros((group, 1), jnp.int32) + block_start + jnp.arange(block_len)).reshape(
        group * block_len, 1
    )
    allowed = (key_pos <= query_pos)[None]
    scores = jnp.einsum("sqd,skd->sqk", queries, keys, preferred_element_type=F32) * (
        head_dim ** (-0.5)
    )
    scores = jnp.where(allowed, scores, MASKED)
    peak = jnp.max(scores, axis=-1)
    probs = jnp.where(allowed, jnp.exp(scores - peak[..., None]), 0.0)
    total = jnp.sum(probs, axis=-1)
    mixed = jnp.einsum("sqk,skd->sqd", probs.astype(BF16), values, preferred_element_type=F32)

    stats = jnp.stack(pieces(peak) + pieces(total), axis=-1).astype(BF16)
    stats = stats.reshape(seqs, group, pairs, own_len, 6).transpose(2, 0, 3, 1, 4)
    stats = stats.reshape(pairs, own_rows, group * 6)
    mixed = (
        mixed.astype(BF16)
        .reshape(seqs, group, pairs, own_len, head_dim)
        .transpose(2, 0, 3, 1, 4)
        .reshape(pairs, own_rows, group * head_dim)
    )
    merged = exchange(
        jnp.concatenate(
            [mixed, jnp.pad(stats, ((0, 0), (0, 0), (0, head_dim - group * 6)))], axis=2
        ),
        "pair",
    )
    part_stats = (
        merged[..., group * head_dim : group * head_dim + group * 6]
        .astype(F32)
        .reshape(pairs, own_rows, group, 6)
    )
    part_peak = jnp.sum(part_stats[..., :3], axis=-1)
    part_total = jnp.sum(part_stats[..., 3:], axis=-1)
    scale = jnp.exp(part_peak - jnp.max(part_peak, axis=0))
    scale = scale / jnp.sum(scale * part_total, axis=0)
    part_mixed = merged[..., : group * head_dim].reshape(pairs, own_rows, group, head_dim)
    attended = jnp.sum(scale[..., None] * part_mixed.astype(F32), axis=0).astype(BF16)
    attended = attended.reshape(own_rows, group * head_dim)

    gathered_heads = exchange(for_each(attended, heads * pairs), ("head", "pair"))
    gathered_heads = gathered_heads.reshape(heads, rows, group * head_dim)
    projected = sum(
        dot(
            gathered_heads[h],
            output_matrix[h * group * head_dim : (h + 1) * group * head_dim],
            1,
            0,
        )
        for h in range(heads)
    ).astype(BF16)
    out_cols = output_matrix.shape[1]
    projected = (
        projected.reshape(pairs, seqs, own_len, out_cols)
        .transpose(1, 0, 2, 3)
        .reshape(seqs * pairs, own_len, out_cols)
    )
    owned = exchange(projected, ("head", "pair"))
    owned = jnp.moveaxis(owned, 0, 1).reshape(own_len, width)
    own_tokens = lax.dynamic_index_in_dim(tokens_in, lax.axis_index("head"), 0, keepdims=False)
    residual = (own_tokens.astype(F32) + owned.astype(F32)).astype(BF16)
    moe_in = normalize(residual, moe_gain)

    experts = blocks * heads
    top = chosen_experts.shape[-1]
    capacity = max(2, (own_len * top + experts - 1) // experts + 1)
    slots = experts * capacity
    picked = chosen_experts.reshape(own_len * top)
    earlier = jnp.tril(jnp.ones((own_len * top, own_len * top), jnp.bool_), -1)
    same = (picked[:, None] == picked[None, :]) & earlier
    slot_ids = picked * capacity + jnp.sum(same.astype(jnp.int32), axis=1)
    slot_ids = slot_ids.reshape(own_len, top)
    chosen_slot = slot_ids[..., None] == jnp.arange(slots)[None, None, :]
    placing = jnp.any(chosen_slot, axis=1).astype(BF16)
    outgoing = dot(placing, moe_in, 0, 0).astype(BF16)
    incoming = exchange(outgoing.reshape(experts, capacity, width), ("ctx", "head"))
    incoming = incoming.reshape(slots, width)
    gate_rows, up_rows, down_rows = jnp.split(weights, 3, axis=1)
    gate_part = dot(incoming, gate_rows, 1, 1)
    up_part = dot(incoming, up_rows, 1, 1)
    hidden = (jax.nn.silu(gate_part) * up_part).astype(BF16)
    expert_out = dot(hidden, down_rows, 1, 0).astype(BF16)
    returned = exchange(expert_out.reshape(experts, capacity, width), ("ctx", "head"))
    returned = returned.reshape(slots, width)
    gathered = returned[slot_ids.reshape(-1)].reshape(own_len, top, width)
    mixture = jnp.sum(
        combine_weights.reshape(own_len, top, 1) * gathered.astype(F32), axis=1
    )
    return (residual.astype(F32) + mixture).astype(BF16)[None]


def solution(mesh):
    return jax.shard_map(
        body,
        mesh=mesh,
        in_specs=(
            P(None, ("ctx", "pair"), None),
            P(),
            P(None, ("head", "pair")),
            P(("head", "pair"), None),
            P(("head", "pair"), None),
            P(None, ("head", "pair")),
            P(),
            P("head", ("ctx", "pair"), None),
            P("head", ("ctx", "pair"), None),
            P(("ctx", "head"), "pair", None),
            P(("ctx", "head"), "pair", None),
            P(("ctx", "head"), "pair", None),
        ),
        out_specs=P("head", ("ctx", "pair"), None),
        check_vma=False,
    )
```

time: 310 us -> 240 us (0.77)
  waiting for transfers between devices: 164 us -> 81.3 us
  starting transfers between devices: 30.9 us -> 50.8 us
  matrix products: 32.3 us -> 18.3 us
  blocking collectives: 47.9 us -> 52.9 us
    all_gather x2 -> x1, waiting for transfers between devices: 112 us -> 0.02 us  [body(): lax.all_gather(jnp.concatenate([gate_weight[0], up_weight[0], down_weight...]
    all_to_all x4 -> x6, waiting for transfers between devices: 52.3 us -> 81.3 us  [exchange(): return lax.all_to_all(tiles, axis, 0, 0, tiled=True)]
    all_to_all x4 -> x6, starting transfers between devices: 30.8 us -> 50.8 us  [exchange(): return lax.all_to_all(tiles, axis, 0, 0, tiled=True)]
    dot_general x15 -> x9, matrix products: 32.3 us -> 18.3 us  [the longest x7 11.9 us: dot(): lax.dot_general(a, b, (((a_dim,), (b_dim,)), ((), ())), preferred_element...]
    all_to_all x1 -> x2, blocking collectives: 38.9 us -> 52.9 us  [exchange(): return lax.all_to_all(tiles, axis, 0, 0, tiled=True)]
    all_gather x1 -> x0, blocking collectives: 8.97 us -> none  [rows_first(): whole, at, done = (lax.all_gather(both, axis, axis=0, tiled=True), 0, [])]
    convert_element_type x6, other arithmetic: 4.39 us -> 0.95 us  [the longest x1 0.66 us: body(): return (residual.astype(F32) + mixture).astype(BF16)[None]]
  transfers between devices with their start and end apart: 6 -> 7, of which waited for: 6 -> 6; matrix products, arithmetic and copies ran while one was open for 5% -> 10% of each run, Pallas kernels for 0% -> 0%
where the time goes in v1:
time: 240 us; the launch traced here: 239 us
  waiting for transfers between devices  81.3 us (34%)
  blocking collectives  52.9 us (22%)
  starting transfers between devices  50.8 us (21%)
  matrix products  18.3 us (8%)
  between operations  13.9 us (6%)
  local copies, waits for them, and re-layouts  11.4 us (5%)
  other arithmetic  10.8 us (4%)
    all_to_all x6, waiting for transfers between devices, exchange(): return lax.all_to_all(tiles, axis, 0, 0, tiled=True)  81.3 us
    all_to_all x2, blocking collectives, exchange(): return lax.all_to_all(tiles, axis, 0, 0, tiled=True)  52.9 us
    all_to_all x6, starting transfers between devices, exchange(): return lax.all_to_all(tiles, axis, 0, 0, tiled=True)  50.8 us
    dot_general x7, matrix products, dot(): lax.dot_general(a, b, (((a_dim,), (b_dim,)), ((), ())), preferred_element...  11.9 us
  transfers between devices with their start and end apart: 7, of which 6 were waited for; matrix products, arithmetic and copies ran while one was open for 10% of the time, Pallas kernels for 0%

profile of v1, /device:TPU:1, one launch (start us, length us, event | category | flops | bytes accessed | tf_op | source)
XLA Modules:
  0.0 239.5 jit_solution(7271052385379495477)
XLA Ops:
  6.5 3.3 %pad_maximum_fusion = bf16[192,6144]{1,0:T(8,128)(2,1)} fusion(bf16[192,2048]{1,0:T(8,128)(2,1)} %bitcast.92, bf16[192,2048]{1,0:T(8,128)(2,1)} %bitcast.93, bf16[192,2048]{1,0:T(8,128)(2,1)} %bitcast.94), kind=kLoop, calls=%fused_computation.15 | loop fusion | flops 7077888 | bytes 4718592 | tf_op jit(solution)/shard_map/concatenate | solution.py:90
  10.1 0.8 broadcast_in_dim.24
  11.0 4.8 %all-to-all-start = ((bf16[4,2,16,2048]{3,2,1,0:T(8,128)(2,1)}), bf16[4,2,16,2048]{3,2,1,0:T(8,128)(2,1)S(1)}, u32[]{:S(2)}, u32[]{:S(2)}) async-start(bf16[4,2,16,2048]{3,2,1,0:T(8,128)(2,1)} %broadcast_in_dim.24), calls=%async_computation | async-start | bytes 1048576 | tf_op jit(solution)/shard_map/all_to_all | solution.py:14
  16.0 6.8 %all-to-all-done = bf16[4,2,16,2048]{3,2,1,0:T(8,128)(2,1)S(1)} async-done(((bf16[4,2,16,2048]{3,2,1,0:T(8,128)(2,1)}), bf16[4,2,16,2048]{3,2,1,0:T(8,128)(2,1)S(1)}, u32[]{:S(2)}, u32[]{:S(2)}) %all-to-all-start) | async-done | bytes 524320 | tf_op jit(solution)/shard_map/all_to_all | solution.py:14
  22.8 0.5 fusion.107
  23.3 0.2 fusion.78
  23.6 0.3 convolution_convert_fusion.1
  24.0 0.1 copy.83
  24.1 0.8 fusion.45
  24.9 3.5 %all-to-all-start.1 = ((bf16[4,160,256]{2,1,0:T(8,128)(2,1)}), bf16[4,160,256]{2,1,0:T(8,128)(2,1)S(1)}, u32[]{:S(2)}, u32[]{:S(2)}) async-start(bf16[4,160,256]{2,1,0:T(8,128)(2,1)} %fusion.45), calls=%async_computation.1 | async-start | bytes 655360 | tf_op jit(solution)/shard_map/all_to_all | solution.py:14
  28.4 5.7 %all-to-all-done.1 = bf16[4,160,256]{2,1,0:T(8,128)(2,1)S(1)} async-done(((bf16[4,160,256]{2,1,0:T(8,128)(2,1)}), bf16[4,160,256]{2,1,0:T(8,128)(2,1)S(1)}, u32[]{:S(2)}, u32[]{:S(2)}) %all-to-all-start.1) | async-done | bytes 327712 | tf_op jit(solution)/shard_map/all_to_all | solution.py:14
  34.3 0.1 fusion.92
  34.6 1.1 broadcast_in_dim.26
  35.7 22.6 %all-to-all-start.2 = ((bf16[64,32,256]{2,1,0:T(8,128)(2,1)}), bf16[64,32,256]{2,1,0:T(8,128)(2,1)S(1)}, u32[]{:S(2)}, u32[]{:S(2)}) async-start(bf16[64,32,256]{2,1,0:T(8,128)(2,1)} %broadcast_in_dim.26), calls=%async_computation.2 | async-start | bytes 2097152 | tf_op jit(solution)/shard_map/all_to_all | solution.py:14
  58.5 0.4 broadcast_compare_fusion
  59.1 24.6 %all-to-all-done.2 = bf16[64,32,256]{2,1,0:T(8,128)(2,1)S(1)} async-done(((bf16[64,32,256]{2,1,0:T(8,128)(2,1)}), bf16[64,32,256]{2,1,0:T(8,128)(2,1)S(1)}, u32[]{:S(2)}, u32[]{:S(2)}) %all-to-all-start.2) | async-done | bytes 1048608 | tf_op jit(solution)/shard_map/all_to_all | solution.py:14
  83.8 1.0 copy-done.3
  84.8 3.0 %fusion.1 = (f32[2,512]{1,0:T(2,128)S(1)}, f32[2,512,1024]{2,1,0:T(8,128)}) fusion(pred[512,1024]{1,0:T(8,128)(4,1)S(1)} %broadcast_compare_fusion, bf16[2,512,128]{2,1,0:T(8,128)(2,1)S(1)} %bitcast.97, bf16[2,1024,256]{2,1,0:T(8,128)(2,1)S(1)} %bitcast.86), kind=kOutput, calls=%fused_computation.4 | convolution fusion | flops 271580160 | bytes 5509120 | tf_op jit(solution)/shard_map/sqd,skd->sqk/dot_general | solution.py:154
  87.9 3.4 %fusion.22 = bf16[2,512,128]{2,1,0:T(8,128)(2,1)S(1)} fusion(f32[2,512,1024]{2,1,0:T(8,128)} %get-tuple-element.28, f32[2,512]{1,0:T(2,128)S(1)} %get-tuple-element.27, pred[512,1024]{1,0:T(8,128)(4,1)S(1)} %broadcast_compare_fusion, bf16[2,1024,256]{2,1,0:T(8,128)(2,1)} %bitcast.87), kind=kOutput, calls=%fused_computation.20 | convolution fusion | flops 273809408 | bytes 5509120 | tf_op jit(solution)/shard_map/sqk,skd->sqd/dot_general | solution.py:161
  91.3 0.2 copy.102
  91.5 0.1 reshape.338
  91.6 3.7 %fusion.8 = f32[2,512]{1,0:T(2,128)S(1)} fusion(f32[2,512,1024]{2,1,0:T(8,128)} %get-tuple-element.28, f32[2,512]{1,0:T(2,128)S(1)} %get-tuple-element.27, pred[512,1024]{1,0:T(8,128)(4,1)S(1)} %broadcast_compare_fusion), kind=kLoop, calls=%fused_computation.11 | loop fusion | flops 5241856 | bytes 4726784 | tf_op jit(solution)/shard_map/reduce_sum | solution.py:160
  95.8 11.4 %all_to_all.40 = bf16[4,32,1152]{2,1,0:T(8,128)(2,1)S(1)} all-to-all(bf16[4,32,1152]{2,1,0:T(8,128)(2,1)S(1)} %fusion.46), channel_id=1, replica_groups=mesh['ctx'=64,'head'=2,'pair'=4] {'pair'}, dimensions={0} | all-to-all | bytes 589824 | tf_op jit(solution)/shard_map/all_to_all | solution.py:14
  107.5 0.2 mul.228
  107.9 0.9 broadcast_in_dim.29
  108.8 10.0 %all-to-all-start.4 = ((bf16[8,32,1024]{2,1,0:T(8,128)(2,1)}), bf16[8,32,1024]{2,1,0:T(8,128)(2,1)S(1)}, u32[]{:S(2)}, u32[]{:S(2)}) async-start(bf16[8,32,1024]{2,1,0:T(8,128)(2,1)} %broadcast_in_dim.29), calls=%async_computation.4 | async-start | bytes 1048576 | tf_op jit(solution)/shard_map/all_to_all | solution.py:14
  118.9 0.2 convert_reduce_fusion
  119.3 8.8 %all-to-all-done.4 = bf16[8,32,1024]{2,1,0:T(8,128)(2,1)S(1)} async-done(((bf16[8,32,1024]{2,1,0:T(8,128)(2,1)}), bf16[8,32,1024]{2,1,0:T(8,128)(2,1)S(1)}, u32[]{:S(2)}, u32[]{:S(2)}) %all-to-all-start.4) | async-done | bytes 524320 | tf_op jit(solution)/shard_map/all_to_all | solution.py:14
  128.1 1.3 fusion.42
  129.4 0.2 fusion.27
  129.6 0.6 copy.91
  130.3 3.6 %all-to-all-start.5 = ((bf16[8,16,256]{2,1,0:T(8,128)(2,1)}), bf16[8,16,256]{2,1,0:T(8,128)(2,1)S(1)}, u32[]{:S(2)}, u32[]{:S(2)}) async-start(bf16[8,16,256]{2,1,0:T(8,128)(2,1)} %bitcast.23), calls=%async_computation.5 | async-start | bytes 131072 | tf_op jit(solution)/shard_map/all_to_all | solution.py:14
  133.9 0.1 fusion.60
  134.0 4.8 %all-to-all-done.5 = bf16[8,16,256]{2,1,0:T(8,128)(2,1)S(1)} async-done(((bf16[8,16,256]{2,1,0:T(8,128)(2,1)}), bf16[8,16,256]{2,1,0:T(8,128)(2,1)S(1)}, u32[]{:S(2)}, u32[]{:S(2)}) %all-to-all-start.5) | async-done | bytes 65568 | tf_op jit(solution)/shard_map/all_to_all | solution.py:14
  138.9 0.1 fusion.56
  139.0 0.5 convolution_convert_fusion
  139.5 0.7 reshape.344
  140.2 41.5 %all_to_all.41 = bf16[128,2,2048]{2,1,0:T(2,128)(2,1)S(1)} all-to-all(bf16[128,2,2048]{2,1,0:T(2,128)(2,1)S(1)} %reshape.344), channel_id=1, replica_groups=mesh['ctx'=64,'head'=2,'pair'=4] {'ctx','head'}, dimensions={0} | all-to-all | bytes 2097152 | tf_op jit(solution)/shard_map/all_to_all | solution.py:14
  181.7 0.4 reshape.345
  182.2 3.8 %fusion.6 = f32[256,768]{1,0:T(8,128)} fusion(bf16[256,2048]{1,0:T(8,128)(2,1)S(1)} %reshape.345, bf16[768,6144]{1,0:T(8,128)(2,1)} %all-gather.2.cloned.1.call-done), kind=kOutput, calls=%fused_computation.9 | convolution fusion | flops 805306368 | bytes 4980736 | tf_op jit(solution)/shard_map/dot_general | solution.py:22
  186.0 5.3 %fusion.10 = bf16[256,2048]{1,0:T(8,128)(2,1)S(1)} fusion(bf16[768,6144]{1,0:T(8,128)(2,1)} %all-gather.2.cloned.1.call-done, bf16[256,2048]{1,0:T(8,128)(2,1)S(1)} %reshape.345, f32[256,768]{1,0:T(8,128)} %fusion.6), kind=kOutput, calls=%fused_computation.14 | convolution fusion | flops 1612316672 | bytes 9175040 | tf_op jit(solution)/shard_map/dot_general | solution.py:22
  191.3 1.5 reshape.346
  192.8 6.4 %all-to-all-start.7 = ((bf16[128,2,2048]{2,1,0:T(2,128)(2,1)}), bf16[128,2,2048]{2,1,0:T(2,128)(2,1)S(1)}, u32[]{:S(2)}, u32[]{:S(2)}) async-start(bf16[128,2,2048]{2,1,0:T(2,128)(2,1)} %reshape.346), calls=%async_computation.7 | async-start | bytes 2097152 | tf_op jit(solution)/shard_map/all_to_all | solution.py:14
  199.6 30.6 %all-to-all-done.7 = bf16[128,2,2048]{2,1,0:T(2,128)(2,1)S(1)} async-done(((bf16[128,2,2048]{2,1,0:T(2,128)(2,1)}), bf16[128,2,2048]{2,1,0:T(2,128)(2,1)S(1)}, u32[]{:S(2)}, u32[]{:S(2)}) %all-to-all-start.7) | async-done | bytes 1048608 | tf_op jit(solution)/shard_map/all_to_all | solution.py:14
  230.2 0.4 reshape.347
  230.6 0.9 gather_fusion
  231.5 0.4 fusion.30
  232.0 0.7 fusion.59
  (87 shorter events, 3.2 us)
Async XLA Ops:
  6.5 16.2 %copy-start = (bf16[2048,256]{1,0:T(8,128)(2,1)S(1)}, bf16[2048,256]{1,0:T(8,128)(2,1)}, u32[]{:S(2)}) copy-start(bf16[2048,256]{1,0:T(8,128)(2,1)} %param.14) | copy-start | bytes 3145732
  6.5 3.4 %copy-start.1 = (bf16[2,16,2048]{2,1,0:T(8,128)(2,1)S(1)}, bf16[2,16,2048]{2,1,0:T(8,128)(2,1)}, u32[]{:S(2)}) copy-start(bf16[2,16,2048]{2,1,0:T(8,128)(2,1)} %param.12) | copy-start | bytes 393220
  6.5 3.5 %copy-start.6 = (f32[2048]{0:T(1024)S(1)}, f32[2048]{0:T(1024)}, u32[]{:S(2)}) copy-start(f32[2048]{0:T(1024)} %param.13) | copy-start | bytes 24580
  6.5 175.6 %all-gather.2.cloned.1.call-start = ((), (), s32[]{:S(2)}) async-start(), calls=%async_computation.8 | async-start | bytes 11796480 | tf_op jit(solution)/shard_map/all_gather | solution.py:89
  9.9 13.8 %copy-start.8 = (bf16[32,2048]{1,0:T(8,128)(2,1)S(1)}, bf16[32,2048]{1,0:T(8,128)(2,1)}, u32[]{:S(2)}) copy-start(bf16[32,2048]{1,0:T(8,128)(2,1)} %param.16) | copy-start | bytes 393220
  9.9 13.8 %copy-start.9 = (bf16[32,2048]{1,0:T(8,128)(2,1)S(1)}, bf16[32,2048]{1,0:T(8,128)(2,1)}, u32[]{:S(2)}) copy-start(bf16[32,2048]{1,0:T(8,128)(2,1)} %param.15) | copy-start | bytes 393220
  11.0 11.8 %all-to-all-start = ((bf16[4,2,16,2048]{3,2,1,0:T(8,128)(2,1)}), bf16[4,2,16,2048]{3,2,1,0:T(8,128)(2,1)S(1)}, u32[]{:S(2)}, u32[]{:S(2)}) async-start(bf16[4,2,16,2048]{3,2,1,0:T(8,128)(2,1)} %broadcast_in_dim.24), calls=%async_computation | async-start | bytes 1048576 | tf_op jit(solution)/shard_map/all_to_all | solution.py:14
  24.9 9.3 %all-to-all-start.1 = ((bf16[4,160,256]{2,1,0:T(8,128)(2,1)}), bf16[4,160,256]{2,1,0:T(8,128)(2,1)S(1)}, u32[]{:S(2)}, u32[]{:S(2)}) async-start(bf16[4,160,256]{2,1,0:T(8,128)(2,1)} %fusion.45), calls=%async_computation.1 | async-start | bytes 655360 | tf_op jit(solution)/shard_map/all_to_all | solution.py:14
  35.7 48.0 %all-to-all-start.2 = ((bf16[64,32,256]{2,1,0:T(8,128)(2,1)}), bf16[64,32,256]{2,1,0:T(8,128)(2,1)S(1)}, u32[]{:S(2)}, u32[]{:S(2)}) async-start(bf16[64,32,256]{2,1,0:T(8,128)(2,1)} %broadcast_in_dim.26), calls=%async_computation.2 | async-start | bytes 2097152 | tf_op jit(solution)/shard_map/all_to_all | solution.py:14
  83.8 1.0 copy-start.3
  95.3 23.5 %copy-start.4 = (s32[1,16,8]{1,2,0:T(8,128)S(1)}, s32[1,16,8]{1,2,0:T(8,128)}, u32[]{:S(2)}) copy-start(s32[1,16,8]{1,2,0:T(8,128)} %param.19) | copy-start | bytes 1540
  107.4 31.6 %copy-start.5 = (f32[2048]{0:T(1024)S(1)}, f32[2048]{0:T(1024)}, u32[]{:S(2)}) copy-start(f32[2048]{0:T(1024)} %param.18) | copy-start | bytes 24580
  107.8 21.6 %copy-start.2 = (bf16[2048,256]{1,0:T(8,128)(2,1)S(1)}, bf16[2048,256]{1,0:T(8,128)(2,1)}, u32[]{:S(2)}) copy-start(bf16[2048,256]{1,0:T(8,128)(2,1)} %param.17) | copy-start | bytes 3145732
  108.8 19.3 %all-to-all-start.4 = ((bf16[8,32,1024]{2,1,0:T(8,128)(2,1)}), bf16[8,32,1024]{2,1,0:T(8,128)(2,1)S(1)}, u32[]{:S(2)}, u32[]{:S(2)}) async-start(bf16[8,32,1024]{2,1,0:T(8,128)(2,1)} %broadcast_in_dim.29), calls=%async_computation.4 | async-start | bytes 1048576 | tf_op jit(solution)/shard_map/all_to_all | solution.py:14
  130.3 8.5 %all-to-all-start.5 = ((bf16[8,16,256]{2,1,0:T(8,128)(2,1)}), bf16[8,16,256]{2,1,0:T(8,128)(2,1)S(1)}, u32[]{:S(2)}, u32[]{:S(2)}) async-start(bf16[8,16,256]{2,1,0:T(8,128)(2,1)} %bitcast.23), calls=%async_computation.5 | async-start | bytes 131072 | tf_op jit(solution)/shard_map/all_to_all | solution.py:14
  191.3 8.1 %copy-start.7 = (f32[1,16,8]{1,2,0:T(8,128)S(1)}, f32[1,16,8]{1,2,0:T(8,128)}, u32[]{:S(2)}) copy-start(f32[1,16,8]{1,2,0:T(8,128)} %param.20) | copy-start | bytes 1540
  192.8 37.4 %all-to-all-start.7 = ((bf16[128,2,2048]{2,1,0:T(2,128)(2,1)}), bf16[128,2,2048]{2,1,0:T(2,128)(2,1)S(1)}, u32[]{:S(2)}, u32[]{:S(2)}) async-start(bf16[128,2,2048]{2,1,0:T(2,128)(2,1)} %reshape.346), calls=%async_computation.7 | async-start | bytes 2097152 | tf_op jit(solution)/shard_map/all_to_all | solution.py:14
Sparse Core Ops, SparseCore 0:
  10.0 107.4 all-gather.1

commit v2 on v1

--- a/solution.py
+++ b/solution.py
@@ -1,7 +1,10 @@
 import jax
 import jax.numpy as jnp
 from jax import lax
+from jax.experimental import pallas as pl
+from jax.experimental.pallas import tpu as pltpu
 from jax.sharding import PartitionSpec as P
+
 
 ROPE_BASE = 1000000.0
 EPSILON = 1e-06
@@ -49,14 +52,125 @@
     ).astype(BF16)
 
 
-def rounded(values):
-    return lax.reduce_precision(values, 8, 7)
-
-
-def pieces(values):
-    high = rounded(values)
-    middle = rounded(values - high)
-    return [high, middle, rounded(values - high - middle)]
+STATS = 6
+
+
+def attend_part(where, query_slots, spread, seqs, own_len, block_len, local_heads, head_dim):
+    pairs = len(query_slots)
+    own_rows = seqs * own_len
+    blocks = spread.shape[0]
+    lanes = pairs * local_heads * head_dim
+    scaling = head_dim ** (-0.5)
+
+    def kernel(where_ref, *refs):
+        query_refs = refs[:pairs]
+        spread_ref, out_ref = refs[pairs:]
+        start = where_ref[0]
+        me = where_ref[1]
+        key_shape = (own_len, blocks * own_len)
+        key_index = lax.broadcasted_iota(jnp.int32, key_shape, 1)
+        place = lax.broadcasted_iota(jnp.int32, key_shape, 0)
+        lag = (
+            (key_index // own_len) * block_len + me * own_len + key_index % own_len - place
+        )
+        lane = lax.broadcasted_iota(jnp.int32, (own_len, head_dim), 1)
+        for seq in range(seqs):
+            low = seq * own_len
+            keys = spread_ref[:, low : low + own_len, :head_dim].reshape(-1, head_dim)
+            values = spread_ref[:, low : low + own_len, head_dim:].reshape(-1, head_dim)
+            stats = {}
+            for t in range(pairs):
+                owners = [lax.rem(me - t - s + 2 * pairs, pairs) for s in range(pairs)]
+                allowed = jnp.concatenate([lag <= start + o * own_len for o in owners], axis=0)
+                for j in range(local_heads):
+                    head = t * local_heads + j
+                    query = jnp.concatenate(
+                        [
+                            query_refs[t][
+                                s, low : low + own_len, j * head_dim : (j + 1) * head_dim
+                            ]
+                            for s in range(pairs)
+                        ],
+                        axis=0,
+                    )
+                    scores = dot(query, keys, 1, 1) * scaling
+                    scores = jnp.where(allowed, scores, MASKED)
+                    peak = jnp.max(scores, axis=1, keepdims=True)
+                    probs = jnp.where(allowed, jnp.exp(scores - peak), 0.0)
+                    total = jnp.sum(probs, axis=1, keepdims=True)
+                    mixed = dot(probs.astype(BF16), values, 1, 0).astype(BF16)
+                    terms = []
+                    for number in (peak, total):
+                        high = number.astype(BF16).astype(F32)
+                        middle = (number - high).astype(BF16).astype(F32)
+                        terms += [high, middle, number - high - middle]
+                    for s in range(pairs):
+                        span = slice(s * own_len, (s + 1) * own_len)
+                        out_ref[
+                            owners[s],
+                            low : low + own_len,
+                            head * head_dim : (head + 1) * head_dim,
+                        ] = mixed[span]
+                        at = (t + s) % pairs
+                        row = stats.get(at, jnp.zeros((own_len, head_dim), F32))
+                        for n, term in enumerate(terms):
+                            row = jnp.where(lane == head * STATS + n, term[span], row)
+                        stats[at] = row
+            for at in range(pairs):
+                out_ref[lax.rem(me - at + pairs, pairs), low : low + own_len, lanes:] = stats[
+                    at
+                ].astype(BF16)
+
+    vmem = pl.BlockSpec(memory_space=pltpu.VMEM)
+    return pl.pallas_call(
+        kernel,
+        out_shape=jax.ShapeDtypeStruct((pairs, own_rows, lanes + head_dim), BF16),
+        in_specs=[pl.BlockSpec(memory_space=pltpu.SMEM)] + [vmem] * (pairs + 1),
+        out_specs=vmem,
+        name="attend_part",
+    )(where, *query_slots, spread)
+
+
+def merge_parts(merged, own_rows, local_heads, head_dim):
+    pairs = merged.shape[0]
+    lanes = pairs * local_heads * head_dim
+
+    def kernel(in_ref, out_ref):
+        stats = [in_ref[p, :, lanes:].astype(F32) for p in range(pairs)]
+        for g in range(pairs):
+            for j in range(local_heads):
+                heads = [((p - g) % pairs) * local_heads + j for p in range(pairs)]
+
+                def number(p, first):
+                    at = heads[p] * STATS + first
+                    return (
+                        stats[p][:, at : at + 1]
+                        + stats[p][:, at + 1 : at + 2]
+                        + stats[p][:, at + 2 : at + 3]
+                    )
+
+                peaks = [number(p, 0) for p in range(pairs)]
+                top = peaks[0]
+                for peak in peaks[1:]:
+                    top = jnp.maximum(top, peak)
+                scales = [jnp.exp(peak - top) for peak in peaks]
+                total = sum(scales[p] * number(p, 3) for p in range(pairs))
+                mix = sum(
+                    scales[p]
+                    * in_ref[p, :, heads[p] * head_dim : (heads[p] + 1) * head_dim].astype(F32)
+                    for p in range(pairs)
+                )
+                head = g * local_heads + j
+                out_ref[:, head * head_dim : (head + 1) * head_dim] = (mix / total).astype(BF16)
+
+    vmem = pl.BlockSpec(memory_space=pltpu.VMEM)
+    return pl.pallas_call(
+        kernel,
+        out_shape=jax.ShapeDtypeStruct((own_rows, lanes), BF16),
+        in_specs=[vmem],
+        out_specs=vmem,
+        name="merge_parts",
+    )(merged)
 
 
 def body(
@@ -86,26 +200,43 @@
     local_heads = q_cols // head_dim
     group = local_heads * pairs
 
-    weights = lax.all_gather(
-        jnp.concatenate([gate_weight[0], up_weight[0], down_weight[0]], axis=1),
-        "pair",
-        axis=0,
-        tiled=True,
-    )
-
-    normed = normalize(tokens_in, attn_gain)
-    block_rows = exchange(for_each(normed, pairs), "pair").reshape(rows, width)
+    places = jnp.arange(own_len)
     block_start = lax.axis_index("ctx") * block_len
-    own_start = block_start + lax.axis_index("pair") * own_len
-    places = jnp.arange(own_len)
-    row_pos = block_start + (
-        jnp.arange(pairs)[:, None, None] * own_len + jnp.zeros((seqs, 1), jnp.int32) + places
+    me = lax.axis_index("pair")
+    own_pos = (block_start + me * own_len + jnp.zeros((seqs, 1), jnp.int32) + places).reshape(
+        own_rows
+    )
+    own_tables = rope_tables(own_pos.astype(F32), head_dim)
+    normed = normalize(tokens_in, attn_gain).reshape(own_rows, width)
+    kv_send = for_each(jnp.concatenate([key_matrix, value_matrix], axis=0), pairs)
+    kv_rows = exchange(kv_send, "pair")
+
+    joined = jnp.concatenate([gate_weight[0], up_weight[0], down_weight[0]], axis=1)
+    weights = lax.all_gather(joined, "pair", axis=0, tiled=True)
+    key_own = dot(normed, kv_rows[:, :part_cols].reshape(head_dim, width), 1, 1)
+    value_own = dot(normed, kv_rows[:, part_cols:].reshape(head_dim, width), 1, 1)
+    both = jnp.concatenate([rotate(key_own, own_tables), value_own.astype(BF16)], axis=1)
+    to_send = for_each(both, blocks)
+    spread = exchange(to_send, "ctx")
+
+    normed, _ = lax.optimization_barrier((normed, to_send))
+
+    def from_below(shard):
+        return [shard] + [
+            lax.ppermute(shard, "pair", [(i, (i + t) % pairs) for i in range(pairs)])
+            for t in range(1, pairs)
+        ]
+
+    token_slots = jnp.concatenate(from_below(normed), axis=0)
+    slot_pair = (me - jnp.arange(pairs)) % pairs
+    row_pos = (
+        block_start
+        + slot_pair[:, None, None] * own_len
+        + jnp.zeros((seqs, 1), jnp.int32)
+        + places
     ).reshape(rows)
     q_tables = rope_tables(row_pos.astype(F32), head_dim)
-    key_value = dot(
-        block_rows, jnp.concatenate([key_matrix, value_matrix], axis=0), 1, 1
-    ).astype(BF16)
-    query_raw = dot(block_rows, query_matrix, 1, 0)
+    query_raw = dot(token_slots, query_matrix, 1, 0)
     query = jnp.concatenate(
         [
             rotate(query_raw[:, j * head_dim : (j + 1) * head_dim], q_tables)
@@ -113,80 +244,19 @@
         ],
         axis=1,
     )
-    swapped = exchange(
-        jnp.concatenate(
-            [
-                for_each(query, pairs),
-                jnp.pad(
-                    key_value.reshape(pairs, own_rows, 2 * part_cols),
-                    ((0, 0), (0, 0), (0, q_cols - 2 * part_cols)),
-                ),
-            ],
-            axis=1,
-        ),
-        "pair",
-    )
-    own_pos = (own_start + jnp.zeros((seqs, 1), jnp.int32) + places).reshape(own_rows)
-    key_own = jnp.concatenate([swapped[p, rows:, :part_cols] for p in range(pairs)], axis=1)
-    value_own = jnp.concatenate(
-        [swapped[p, rows:, part_cols : 2 * part_cols] for p in range(pairs)], axis=1
-    )
-    key_own = rotate(key_own.astype(F32), rope_tables(own_pos.astype(F32), head_dim))
-    both = jnp.concatenate([key_own, value_own], axis=1)
-    spread = exchange(for_each(both, blocks), "ctx").reshape(blocks, seqs, own_len, 2 * head_dim)
-    spread = jnp.moveaxis(spread, 1, 0).reshape(seqs, blocks * own_len, 2 * head_dim)
-    keys = spread[..., :head_dim]
-    values = spread[..., head_dim:]
-
-    queries = (
-        swapped[:, :rows]
-        .reshape(pairs, pairs, seqs, own_len, local_heads, head_dim)
-        .transpose(2, 0, 4, 1, 3, 5)
-        .reshape(seqs, group * block_len, head_dim)
-    )
-    key_pos = (
-        jnp.arange(blocks)[:, None] * block_len + lax.axis_index("pair") * own_len + places
-    ).reshape(1, blocks * own_len)
-    query_pos = (jnp.zeros((group, 1), jnp.int32) + block_start + jnp.arange(block_len)).reshape(
-        group * block_len, 1
-    )
-    allowed = (key_pos <= query_pos)[None]
-    scores = jnp.einsum("sqd,skd->sqk", queries, keys, preferred_element_type=F32) * (
-        head_dim ** (-0.5)
-    )
-    scores = jnp.where(allowed, scores, MASKED)
-    peak = jnp.max(scores, axis=-1)
-    probs = jnp.where(allowed, jnp.exp(scores - peak[..., None]), 0.0)
-    total = jnp.sum(probs, axis=-1)
-    mixed = jnp.einsum("sqk,skd->sqd", probs.astype(BF16), values, preferred_element_type=F32)
-
-    stats = jnp.stack(pieces(peak) + pieces(total), axis=-1).astype(BF16)
-    stats = stats.reshape(seqs, group, pairs, own_len, 6).transpose(2, 0, 3, 1, 4)
-    stats = stats.reshape(pairs, own_rows, group * 6)
-    mixed = (
-        mixed.astype(BF16)
-        .reshape(seqs, group, pairs, own_len, head_dim)
-        .transpose(2, 0, 3, 1, 4)
-        .reshape(pairs, own_rows, group * head_dim)
-    )
-    merged = exchange(
-        jnp.concatenate(
-            [mixed, jnp.pad(stats, ((0, 0), (0, 0), (0, head_dim - group * 6)))], axis=2
-        ),
-        "pair",
-    )
-    part_stats = (
-        merged[..., group * head_dim : group * head_dim + group * 6]
-        .astype(F32)
-        .reshape(pairs, own_rows, group, 6)
-    )
-    part_peak = jnp.sum(part_stats[..., :3], axis=-1)
-    part_total = jnp.sum(part_stats[..., 3:], axis=-1)
-    scale = jnp.exp(part_peak - jnp.max(part_peak, axis=0))
-    scale = scale / jnp.sum(scale * part_total, axis=0)
-    part_mixed = merged[..., : group * head_dim].reshape(pairs, own_rows, group, head_dim)
-    attended = jnp.sum(scale[..., None] * part_mixed.astype(F32), axis=0).astype(BF16)
-    attended = attended.reshape(own_rows, group * head_dim)
+    query_slots = [q.reshape(pairs, own_rows, q_cols) for q in from_below(query)]
+    parts = attend_part(
+        jnp.stack([block_start, me]).astype(jnp.int32),
+        query_slots,
+        spread,
+        seqs,
+        own_len,
+        block_len,
+        local_heads,
+        head_dim,
+    )
+    merged = exchange(parts, "pair")
+    attended = merge_parts(merged, own_rows, local_heads, head_dim)
 
     gathered_heads = exchange(for_each(attended, heads * pairs), ("head", "pair"))
     gathered_heads = gathered_heads.reshape(heads, rows, group * head_dim)

time: 240 us -> 245 us (1.021)
  starting transfers between devices: 50.8 us -> 61.9 us
  Pallas kernels: 0 us -> 10.2 us
  waiting for transfers between devices: 81.3 us -> 71.4 us
  matrix products: 18.3 us -> 10.9 us
  blocking collectives: 52.9 us -> 57.9 us
  other arithmetic: 10.8 us -> 7.33 us
    all_to_all x6 -> x5, waiting for transfers between devices: 81.3 us -> 57.2 us  [exchange(): return lax.all_to_all(tiles, axis, 0, 0, tiled=True)]
    ppermute x0 -> x6, starting transfers between devices: none -> 16.4 us  [from_below(): lax.ppermute(shard, 'pair', [(i, (i + t) % pairs) for i in range(pairs)])]
    ppermute x0 -> x6, waiting for transfers between devices: none -> 14.2 us  [from_below(): lax.ppermute(shard, 'pair', [(i, (i + t) % pairs) for i in range(pairs)])]
    pallas_call x0 -> x2, Pallas kernels: none -> 10.2 us  [the longest x1 7.89 us: attend_part(): pl.pallas_call(kernel, out_shape=jax.ShapeDtypeStruct((pairs, own_rows, l...]
    dot_general x2 -> x0, matrix products: 6.43 us -> none  [the longest x1 3.38 us: body(): jnp.einsum('sqk,skd->sqd', probs.astype(BF16), values, preferred_element_...]
    all_to_all x6 -> x5, starting transfers between devices: 50.8 us -> 45.5 us  [exchange(): return lax.all_to_all(tiles, axis, 0, 0, tiled=True)]
    all_to_all x2, blocking collectives: 52.9 us -> 57.9 us  [exchange(): return lax.all_to_all(tiles, axis, 0, 0, tiled=True)]
    reduce_sum x3 -> x0, other arithmetic: 3.77 us -> none  [the longest x1 3.68 us: body(): total = jnp.sum(probs, axis=-1)]
  transfers between devices with their start and end apart: 7 -> 12, of which waited for: 6 -> 9; matrix products, arithmetic and copies ran while one was open for 10% -> 5% of each run, Pallas kernels for 0% -> 4%
where the time goes in v2:
time: 245 us; the launch traced here: 244 us
  waiting for transfers between devices  71.4 us (29%)
  starting transfers between devices  61.9 us (25%)
  blocking collectives  57.9 us (24%)
  between operations  13.7 us (6%)
  matrix products  10.9 us (4%)
  local copies, waits for them, and re-layouts  10.8 us (4%)
  Pallas kernels  10.2 us (4%)
  other arithmetic  7.33 us (3%)
    all_to_all x2, blocking collectives, exchange(): return lax.all_to_all(tiles, axis, 0, 0, tiled=True)  57.9 us
    all_to_all x5, waiting for transfers between devices, exchange(): return lax.all_to_all(tiles, axis, 0, 0, tiled=True)  57.2 us
    all_to_all x5, starting transfers between devices, exchange(): return lax.all_to_all(tiles, axis, 0, 0, tiled=True)  45.5 us
    ppermute x6, starting transfers between devices, from_below(): lax.ppermute(shard, 'pair', [(i, (i + t) % pairs) for i in range(pairs)])  16.4 us
    ppermute x6, waiting for transfers between devices, from_below(): lax.ppermute(shard, 'pair', [(i, (i + t) % pairs) for i in range(pairs)])  14.2 us
    dot_general x8, matrix products, dot(): lax.dot_general(a, b, (((a_dim,), (b_dim,)), ((), ())), preferred_element...  10.9 us
    pallas_call x1, Pallas kernels, attend_part(): pl.pallas_call(kernel, out_shape=jax.ShapeDtypeStruct((pairs, own_rows, l...  7.89 us
  transfers between devices with their start and end apart: 12, of which 9 were waited for; matrix products, arithmetic and copies ran while one was open for 5% of the time, Pallas kernels for 4%

profile of v2, /device:TPU:1, one launch (start us, length us, event | category | flops | bytes accessed | tf_op | source)
XLA Modules:
  0.0 244.1 jit_solution(7902275554912000007)
XLA Ops:
  6.5 3.3 %pad_maximum_fusion = bf16[192,6144]{1,0:T(8,128)(2,1)} fusion(bf16[192,2048]{1,0:T(8,128)(2,1)} %bitcast.69, bf16[192,2048]{1,0:T(8,128)(2,1)} %bitcast.70, bf16[192,2048]{1,0:T(8,128)(2,1)} %bitcast.71), kind=kLoop, calls=%fused_computation.9 | loop fusion | flops 7077888 | bytes 4718592 | tf_op jit(solution)/shard_map/concatenate | solution.py:214
  9.9 1.1 broadcast_in_dim.7
  11.1 4.8 %all-to-all-start = ((bf16[4,64,2048]{2,1,0:T(8,128)(2,1)}), bf16[4,64,2048]{2,1,0:T(8,128)(2,1)S(1)}, u32[]{:S(2)}, u32[]{:S(2)}) async-start(bf16[4,64,2048]{2,1,0:T(8,128)(2,1)} %broadcast_in_dim.7), calls=%async_computation | async-start | bytes 2097152 | tf_op jit(solution)/shard_map/all_to_all | solution.py:17
  16.3 9.4 %all-to-all-done = bf16[4,64,2048]{2,1,0:T(8,128)(2,1)S(1)} async-done(((bf16[4,64,2048]{2,1,0:T(8,128)(2,1)}), bf16[4,64,2048]{2,1,0:T(8,128)(2,1)S(1)}, u32[]{:S(2)}, u32[]{:S(2)}) %all-to-all-start) | async-done | bytes 1048608 | tf_op jit(solution)/shard_map/all_to_all | solution.py:17
  25.8 0.3 fusion.84
  26.2 0.3 convolution_convert_fusion.1
  26.6 1.2 broadcast_in_dim.8
  27.7 20.8 %all-to-all-start.1 = ((bf16[64,32,256]{2,1,0:T(8,128)(2,1)}), bf16[64,32,256]{2,1,0:T(8,128)(2,1)S(1)}, u32[]{:S(2)}, u32[]{:S(2)}) async-start(bf16[64,32,256]{2,1,0:T(8,128)(2,1)} %broadcast_in_dim.8), calls=%async_computation.1 | async-start | bytes 2097152 | tf_op jit(solution)/shard_map/all_to_all | solution.py:17
  48.6 2.8 %collective-permute-start.2 = (bf16[32,2048]{1,0:T(8,128)(2,1)S(1)}, bf16[32,2048]{1,0:T(8,128)(2,1)S(1)}, u32[]{:S(2)}, u32[]{:S(2)}) collective-permute-start(bf16[32,2048]{1,0:T(8,128)(2,1)S(1)} %bitcast.63), channel_id=1, source_target_pairs={{0,3},{1,0},{2,1},{3,2},{4,7},{5,4},{6,5},{7,6},{8,11},{9,8},{10,9... | collective-permute-start | bytes 393224 | tf_op jit(solution)/shard_map/ppermute | solution.py:226
  51.4 3.1 %collective-permute-start.1 = (bf16[32,2048]{1,0:T(8,128)(2,1)S(1)}, bf16[32,2048]{1,0:T(8,128)(2,1)S(1)}, u32[]{:S(2)}, u32[]{:S(2)}) collective-permute-start(bf16[32,2048]{1,0:T(8,128)(2,1)S(1)} %bitcast.64), channel_id=1, source_target_pairs={{0,2},{1,3},{2,0},{3,1},{4,6},{5,7},{6,4},{7,5},{8,10},{9,11},{10,... | collective-permute-start | bytes 393224 | tf_op jit(solution)/shard_map/ppermute | solution.py:226
  54.5 1.9 collective-permute-start
  56.6 0.7 pad_add_fusion.where_ref
  57.2 1.0 collective-permute-done.2
  58.2 4.1 %collective-permute-done.1 = bf16[32,2048]{1,0:T(8,128)(2,1)S(1)} collective-permute-done((bf16[32,2048]{1,0:T(8,128)(2,1)S(1)}, bf16[32,2048]{1,0:T(8,128)(2,1)S(1)}, u32[]{:S(2)}, u32[]{:S(2)}) %collective-permute-start.1) | collective-permute-done | bytes 131104 | tf_op jit(solution)/shard_map/ppermute | solution.py:226
  62.3 5.2 %collective-permute-done = bf16[32,2048]{1,0:T(8,128)(2,1)S(1)} collective-permute-done((bf16[32,2048]{1,0:T(8,128)(2,1)S(1)}, bf16[32,2048]{1,0:T(8,128)(2,1)S(1)}, u32[]{:S(2)}, u32[]{:S(2)}) %collective-permute-start) | collective-permute-done | bytes 131104 | tf_op jit(solution)/shard_map/ppermute | solution.py:226
  67.5 0.3 fusion.24
  67.8 0.3 fusion.56
  68.3 2.1 collective-permute-start.3
  70.4 3.7 %collective-permute-start.4 = (bf16[128,256]{1,0:T(8,128)(2,1)S(1)}, bf16[128,256]{1,0:T(8,128)(2,1)S(1)}, u32[]{:S(2)}, u32[]{:S(2)}) collective-permute-start(bf16[128,256]{1,0:T(8,128)(2,1)S(1)} %pad_maximum_fusion.3), channel_id=1, source_target_pairs={{0,2},{1,3},{2,0},{3,1},{4,6},{5,7},{6,4},{7,5},{8,10},{9,11},{10,... | collective-permute-start | bytes 196616 | tf_op jit(solution)/shard_map/ppermute | solution.py:226
  74.1 2.7 %collective-permute-start.5 = (bf16[128,256]{1,0:T(8,128)(2,1)S(1)}, bf16[128,256]{1,0:T(8,128)(2,1)S(1)}, u32[]{:S(2)}, u32[]{:S(2)}) collective-permute-start(bf16[128,256]{1,0:T(8,128)(2,1)S(1)} %pad_maximum_fusion.3), channel_id=1, source_target_pairs={{0,3},{1,0},{2,1},{3,2},{4,7},{5,4},{6,5},{7,6},{8,11},{9,8},{10,9... | collective-permute-start | bytes 196616 | tf_op jit(solution)/shard_map/ppermute | solution.py:226
  76.9 0.7 pad_maximum_fusion.2.refs_0_
  77.6 1.5 collective-permute-done.4
  79.2 2.4 collective-permute-done.5
  81.6 0.6 copy-done.8
  82.2 0.4 copy-done.1
  82.6 7.9 %attend_part.1 = bf16[4,32,1152]{2,1,0:T(8,128)(2,1)} custom-call(s32[2]{0:T(128)} %pad_add_fusion.where_ref, bf16[4,32,256]{2,1,0:T(8,128)(2,1)} %pad_maximum_fusion.2.refs_0_, bf16[4,32,256]{2,1,0:T(8,128)(2,1)} %bitcast.78, bf16[4,32,256]{2,1,0:T(8,128)(2,1)} %bitcast.79, bf16[4,32,256]{2,1,0:T(8,128)(2,1)} %bitcast.80, bf16[64,32,256]{2,1,0:T(8,128)(2,1)} %copy-done.1), custom_call_target="tpu_custom_call" | custom-call | tf_op jit(solution)/shard_map/attend_part/pallas_call | solution.py:125
  90.5 13.3 %all_to_all.35.in_ref = bf16[4,32,1152]{2,1,0:T(8,128)(2,1)} all-to-all(bf16[4,32,1152]{2,1,0:T(8,128)(2,1)} %attend_part.1), channel_id=1, replica_groups=mesh['ctx'=64,'head'=2,'pair'=4] {'pair'}, dimensions={0} | all-to-all | bytes 589824 | tf_op jit(solution)/shard_map/all_to_all | solution.py:17
  103.9 2.3 merge_parts.1
  106.2 1.7 broadcast_in_dim.9
  107.9 8.3 %all-to-all-start.3 = ((bf16[8,32,1024]{2,1,0:T(8,128)(2,1)}), bf16[8,32,1024]{2,1,0:T(8,128)(2,1)S(1)}, u32[]{:S(2)}, u32[]{:S(2)}) async-start(bf16[8,32,1024]{2,1,0:T(8,128)(2,1)} %broadcast_in_dim.9), calls=%async_computation.3 | async-start | bytes 1048576 | tf_op jit(solution)/shard_map/all_to_all | solution.py:17
  116.7 12.3 %all-to-all-done.3 = bf16[8,32,1024]{2,1,0:T(8,128)(2,1)S(1)} async-done(((bf16[8,32,1024]{2,1,0:T(8,128)(2,1)}), bf16[8,32,1024]{2,1,0:T(8,128)(2,1)S(1)}, u32[]{:S(2)}, u32[]{:S(2)}) %all-to-all-start.3) | async-done | bytes 524320 | tf_op jit(solution)/shard_map/all_to_all | solution.py:17
  129.4 0.2 fusion.17
  129.6 0.6 copy.32
  130.2 5.2 %all-to-all-start.4 = ((bf16[8,16,256]{2,1,0:T(8,128)(2,1)}), bf16[8,16,256]{2,1,0:T(8,128)(2,1)S(1)}, u32[]{:S(2)}, u32[]{:S(2)}) async-start(bf16[8,16,256]{2,1,0:T(8,128)(2,1)} %bitcast.16), calls=%async_computation.4 | async-start | bytes 131072 | tf_op jit(solution)/shard_map/all_to_all | solution.py:17
  135.6 4.8 %all-to-all-done.4 = bf16[8,16,256]{2,1,0:T(8,128)(2,1)S(1)} async-done(((bf16[8,16,256]{2,1,0:T(8,128)(2,1)}), bf16[8,16,256]{2,1,0:T(8,128)(2,1)S(1)}, u32[]{:S(2)}, u32[]{:S(2)}) %all-to-all-start.4) | async-done | bytes 65568 | tf_op jit(solution)/shard_map/all_to_all | solution.py:17
  140.6 0.5 convolution_convert_fusion
  141.1 0.7 reshape.196
  141.8 44.5 %all_to_all.36 = bf16[128,2,2048]{2,1,0:T(2,128)(2,1)S(1)} all-to-all(bf16[128,2,2048]{2,1,0:T(2,128)(2,1)S(1)} %reshape.196), channel_id=1, replica_groups=mesh['ctx'=64,'head'=2,'pair'=4] {'ctx','head'}, dimensions={0} | all-to-all | bytes 2097152 | tf_op jit(solution)/shard_map/all_to_all | solution.py:17
  186.3 0.4 reshape.197
  186.8 3.8 %fusion.4 = f32[256,768]{1,0:T(8,128)} fusion(bf16[256,2048]{1,0:T(8,128)(2,1)S(1)} %reshape.197, bf16[768,6144]{1,0:T(8,128)(2,1)} %all-gather.2.cloned.1.call-done), kind=kOutput, calls=%fused_computation.5 | convolution fusion | flops 805306368 | bytes 4980736 | tf_op jit(solution)/shard_map/dot_general | solution.py:25
  190.6 5.3 %fusion.6 = bf16[256,2048]{1,0:T(8,128)(2,1)S(1)} fusion(bf16[768,6144]{1,0:T(8,128)(2,1)} %all-gather.2.cloned.1.call-done, bf16[256,2048]{1,0:T(8,128)(2,1)S(1)} %reshape.197, f32[256,768]{1,0:T(8,128)} %fusion.4), kind=kOutput, calls=%fused_computation.8 | convolution fusion | flops 1612316672 | bytes 9175040 | tf_op jit(solution)/shard_map/dot_general | solution.py:25
  195.9 1.5 reshape.198
  197.4 6.4 %all-to-all-start.6 = ((bf16[128,2,2048]{2,1,0:T(2,128)(2,1)}), bf16[128,2,2048]{2,1,0:T(2,128)(2,1)S(1)}, u32[]{:S(2)}, u32[]{:S(2)}) async-start(bf16[128,2,2048]{2,1,0:T(2,128)(2,1)} %reshape.198), calls=%async_computation.6 | async-start | bytes 2097152 | tf_op jit(solution)/shard_map/all_to_all | solution.py:17
  204.2 30.6 %all-to-all-done.6 = bf16[128,2,2048]{2,1,0:T(2,128)(2,1)S(1)} async-done(((bf16[128,2,2048]{2,1,0:T(2,128)(2,1)}), bf16[128,2,2048]{2,1,0:T(2,128)(2,1)S(1)}, u32[]{:S(2)}, u32[]{:S(2)}) %all-to-all-start.6) | async-done | bytes 1048608 | tf_op jit(solution)/shard_map/all_to_all | solution.py:17
  234.8 0.4 reshape.199
  235.2 0.9 gather_fusion
  236.1 0.4 fusion.18
  236.6 0.7 fusion.45
  (67 shorter events, 2.6 us)
Async XLA Ops:
  6.5 61.0 %copy-start = (bf16[2048,256]{1,0:T(8,128)(2,1)S(1)}, bf16[2048,256]{1,0:T(8,128)(2,1)}, u32[]{:S(2)}) copy-start(bf16[2048,256]{1,0:T(8,128)(2,1)} %param.14) | copy-start | bytes 3145732
  6.5 180.3 %all-gather.2.cloned.1.call-start = ((), (), s32[]{:S(2)}) async-start(), calls=%async_computation.7 | async-start | bytes 11796480 | tf_op jit(solution)/shard_map/all_gather | solution.py:215
  6.5 3.4 %copy-start.4 = (bf16[32,2048]{1,0:T(8,128)(2,1)S(1)}, bf16[32,2048]{1,0:T(8,128)(2,1)}, u32[]{:S(2)}) copy-start(bf16[32,2048]{1,0:T(8,128)(2,1)} %param.16) | copy-start | bytes 393220
  6.5 3.4 %copy-start.5 = (bf16[32,2048]{1,0:T(8,128)(2,1)S(1)}, bf16[32,2048]{1,0:T(8,128)(2,1)}, u32[]{:S(2)}) copy-start(bf16[32,2048]{1,0:T(8,128)(2,1)} %param.15) | copy-start | bytes 393220
  9.9 6.2 %copy-start.2 = (bf16[2,16,2048]{2,1,0:T(8,128)(2,1)S(1)}, bf16[2,16,2048]{2,1,0:T(8,128)(2,1)}, u32[]{:S(2)}) copy-start(bf16[2,16,2048]{2,1,0:T(8,128)(2,1)} %param.12) | copy-start | bytes 393220
  9.9 6.3 %copy-start.11 = (f32[2048]{0:T(1024)S(1)}, f32[2048]{0:T(1024)}, u32[]{:S(2)}) copy-start(f32[2048]{0:T(1024)} %param.13) | copy-start | bytes 24580
  11.1 14.6 %all-to-all-start = ((bf16[4,64,2048]{2,1,0:T(8,128)(2,1)}), bf16[4,64,2048]{2,1,0:T(8,128)(2,1)S(1)}, u32[]{:S(2)}, u32[]{:S(2)}) async-start(bf16[4,64,2048]{2,1,0:T(8,128)(2,1)} %broadcast_in_dim.7), calls=%async_computation | async-start | bytes 2097152 | tf_op jit(solution)/shard_map/all_to_all | solution.py:17
  27.7 53.8 %all-to-all-start.1 = ((bf16[64,32,256]{2,1,0:T(8,128)(2,1)}), bf16[64,32,256]{2,1,0:T(8,128)(2,1)S(1)}, u32[]{:S(2)}, u32[]{:S(2)}) async-start(bf16[64,32,256]{2,1,0:T(8,128)(2,1)} %broadcast_in_dim.8), calls=%async_computation.1 | async-start | bytes 2097152 | tf_op jit(solution)/shard_map/all_to_all | solution.py:17
  48.6 9.6 %collective-permute-start.2 = (bf16[32,2048]{1,0:T(8,128)(2,1)S(1)}, bf16[32,2048]{1,0:T(8,128)(2,1)S(1)}, u32[]{:S(2)}, u32[]{:S(2)}) collective-permute-start(bf16[32,2048]{1,0:T(8,128)(2,1)S(1)} %bitcast.63), channel_id=1, source_target_pairs={{0,3},{1,0},{2,1},{3,2},{4,7},{5,4},{6,5},{7,6},{8,11},{9,8},{10,9... | collective-permute-start | bytes 393224 | tf_op jit(solution)/shard_map/ppermute | solution.py:226
  51.4 10.9 %collective-permute-start.1 = (bf16[32,2048]{1,0:T(8,128)(2,1)S(1)}, bf16[32,2048]{1,0:T(8,128)(2,1)S(1)}, u32[]{:S(2)}, u32[]{:S(2)}) collective-permute-start(bf16[32,2048]{1,0:T(8,128)(2,1)S(1)} %bitcast.64), channel_id=1, source_target_pairs={{0,2},{1,3},{2,0},{3,1},{4,6},{5,7},{6,4},{7,5},{8,10},{9,11},{10,... | collective-permute-start | bytes 393224 | tf_op jit(solution)/shard_map/ppermute | solution.py:226
  54.5 13.0 %collective-permute-start = (bf16[32,2048]{1,0:T(8,128)(2,1)S(1)}, bf16[32,2048]{1,0:T(8,128)(2,1)S(1)}, u32[]{:S(2)}, u32[]{:S(2)}) collective-permute-start(bf16[32,2048]{1,0:T(8,128)(2,1)S(1)} %bitcast.65), channel_id=1, source_target_pairs={{0,1},{1,2},{2,3},{3,0},{4,5},{5,6},{6,7},{7,4},{8,9},{9,10},{10,1... | collective-permute-start | bytes 393224 | tf_op jit(solution)/shard_map/ppermute | solution.py:226
  67.8 48.3 %copy-start.9 = (s32[1,16,8]{1,2,0:T(8,128)S(1)}, s32[1,16,8]{1,2,0:T(8,128)}, u32[]{:S(2)}) copy-start(s32[1,16,8]{1,2,0:T(8,128)} %param.19) | copy-start | bytes 1540
  67.8 61.3 %copy-start.3 = (bf16[2048,256]{1,0:T(8,128)(2,1)S(1)}, bf16[2048,256]{1,0:T(8,128)(2,1)}, u32[]{:S(2)}) copy-start(bf16[2048,256]{1,0:T(8,128)(2,1)} %param.17) | copy-start | bytes 3145732
  68.3 9.3 %collective-permute-start.3 = (bf16[128,256]{1,0:T(8,128)(2,1)S(1)}, bf16[128,256]{1,0:T(8,128)(2,1)S(1)}, u32[]{:S(2)}, u32[]{:S(2)}) collective-permute-start(bf16[128,256]{1,0:T(8,128)(2,1)S(1)} %pad_maximum_fusion.3), channel_id=1, source_target_pairs={{0,1},{1,2},{2,3},{3,0},{4,5},{5,6},{6,7},{7,4},{8,9},{9,10},{10,1... | collective-permute-start | bytes 196616 | tf_op jit(solution)/shard_map/ppermute | solution.py:226
  70.4 8.7 %collective-permute-start.4 = (bf16[128,256]{1,0:T(8,128)(2,1)S(1)}, bf16[128,256]{1,0:T(8,128)(2,1)S(1)}, u32[]{:S(2)}, u32[]{:S(2)}) collective-permute-start(bf16[128,256]{1,0:T(8,128)(2,1)S(1)} %pad_maximum_fusion.3), channel_id=1, source_target_pairs={{0,2},{1,3},{2,0},{3,1},{4,6},{5,7},{6,4},{7,5},{8,10},{9,11},{10,... | collective-permute-start | bytes 196616 | tf_op jit(solution)/shard_map/ppermute | solution.py:226
  74.1 7.4 %collective-permute-start.5 = (bf16[128,256]{1,0:T(8,128)(2,1)S(1)}, bf16[128,256]{1,0:T(8,128)(2,1)S(1)}, u32[]{:S(2)}, u32[]{:S(2)}) collective-permute-start(bf16[128,256]{1,0:T(8,128)(2,1)S(1)} %pad_maximum_fusion.3), channel_id=1, source_target_pairs={{0,3},{1,0},{2,1},{3,2},{4,7},{5,4},{6,5},{7,6},{8,11},{9,8},{10,9... | collective-permute-start | bytes 196616 | tf_op jit(solution)/shard_map/ppermute | solution.py:226
  77.6 4.0 %copy-start.6 = (bf16[128,256]{1,0:T(8,128)(2,1)}, bf16[128,256]{1,0:T(8,128)(2,1)S(1)}, u32[]{:S(2)}) copy-start(bf16[128,256]{1,0:T(8,128)(2,1)S(1)} %collective-permute-done.3) | copy-start | bytes 196612
  79.2 2.4 copy-start.7
  81.6 0.6 copy-start.8
  81.6 1.0 copy-start.1
  103.8 36.8 %copy-start.10 = (f32[2048]{0:T(1024)S(1)}, f32[2048]{0:T(1024)}, u32[]{:S(2)}) copy-start(f32[2048]{0:T(1024)} %param.18) | copy-start | bytes 24580
  107.9 21.2 %all-to-all-start.3 = ((bf16[8,32,1024]{2,1,0:T(8,128)(2,1)}), bf16[8,32,1024]{2,1,0:T(8,128)(2,1)S(1)}, u32[]{:S(2)}, u32[]{:S(2)}) async-start(bf16[8,32,1024]{2,1,0:T(8,128)(2,1)} %broadcast_in_dim.9), calls=%async_computation.3 | async-start | bytes 1048576 | tf_op jit(solution)/shard_map/all_to_all | solution.py:17
  130.2 10.2 %all-to-all-start.4 = ((bf16[8,16,256]{2,1,0:T(8,128)(2,1)}), bf16[8,16,256]{2,1,0:T(8,128)(2,1)S(1)}, u32[]{:S(2)}, u32[]{:S(2)}) async-start(bf16[8,16,256]{2,1,0:T(8,128)(2,1)} %bitcast.16), calls=%async_computation.4 | async-start | bytes 131072 | tf_op jit(solution)/shard_map/all_to_all | solution.py:17
  195.9 8.1 %copy-start.12 = (f32[1,16,8]{1,2,0:T(8,128)S(1)}, f32[1,16,8]{1,2,0:T(8,128)}, u32[]{:S(2)}) copy-start(f32[1,16,8]{1,2,0:T(8,128)} %param.20) | copy-start | bytes 1540
  197.4 37.4 %all-to-all-start.6 = ((bf16[128,2,2048]{2,1,0:T(2,128)(2,1)}), bf16[128,2,2048]{2,1,0:T(2,128)(2,1)S(1)}, u32[]{:S(2)}, u32[]{:S(2)}) async-start(bf16[128,2,2048]{2,1,0:T(2,128)(2,1)} %reshape.198), calls=%async_computation.6 | async-start | bytes 2097152 | tf_op jit(solution)/shard_map/all_to_all | solution.py:17
Sparse Core Ops, SparseCore 0:
  10.0 119.6 all-gather.1

commit v3 on v1

--- a/solution.py
+++ b/solution.py
@@ -1,7 +1,10 @@
 import jax
 import jax.numpy as jnp
 from jax import lax
+from jax.experimental import pallas as pl
+from jax.experimental.pallas import tpu as pltpu
 from jax.sharding import PartitionSpec as P
+
 
 ROPE_BASE = 1000000.0
 EPSILON = 1e-06
@@ -53,10 +56,123 @@
     return lax.reduce_precision(values, 8, 7)
 
 
-def pieces(values):
-    high = rounded(values)
-    middle = rounded(values - high)
-    return [high, middle, rounded(values - high - middle)]
+STATS = 6
+LOG2_E = 1.4426950408889634
+GROUP_ROWS = 256
+
+
+def attend_part(where, swapped, spread, seqs, own_len, local_heads, head_dim):
+    pairs = swapped.shape[0]
+    own_rows = seqs * own_len
+    block_len = pairs * own_len
+    blocks = spread.shape[0]
+    group = pairs * local_heads
+    lanes = group * head_dim
+    scaling = head_dim ** (-0.5)
+    heads_each = GROUP_ROWS // block_len
+
+    def kernel(where_ref, swapped_ref, spread_ref, out_ref):
+        start = where_ref[0]
+        me = where_ref[1]
+        key_index = lax.broadcasted_iota(jnp.int32, (1, blocks * own_len), 1)
+        key_pos = (key_index // own_len) * block_len + me * own_len + key_index % own_len
+        row = lax.broadcasted_iota(jnp.int32, (GROUP_ROWS, 1), 0)
+        allowed = key_pos <= start + row % block_len
+        lane = lax.broadcasted_iota(jnp.int32, (block_len, head_dim), 1)
+        for seq in range(seqs):
+            low = seq * own_len
+            keys = spread_ref[:, low : low + own_len, :head_dim].reshape(-1, head_dim)
+            values = spread_ref[:, low : low + own_len, head_dim:].reshape(-1, head_dim)
+            stats = jnp.zeros((block_len, head_dim), F32)
+            for first in range(0, group, heads_each):
+                query = jnp.concatenate(
+                    [
+                        swapped_ref[
+                            g // local_heads,
+                            p * own_rows + low : p * own_rows + low + own_len,
+                            (g % local_heads) * head_dim : (g % local_heads + 1) * head_dim,
+                        ]
+                        for g in range(first, first + heads_each)
+                        for p in range(pairs)
+                    ],
+                    axis=0,
+                )
+                scores = jnp.where(allowed, dot(query, keys, 1, 1), MASKED)
+                peak = jnp.maximum(jnp.max(scores, axis=1, keepdims=True), 0.1 * MASKED)
+                probs = jnp.exp2((scores - peak) * (scaling * LOG2_E))
+                total = jnp.sum(probs, axis=1, keepdims=True)
+                mixed = dot(probs.astype(BF16), values, 1, 0).astype(BF16)
+                terms = []
+                for number in (peak * scaling, total):
+                    high = number.astype(BF16).astype(F32)
+                    middle = (number - high).astype(BF16).astype(F32)
+                    terms += [high, middle, number - high - middle]
+                for g in range(first, first + heads_each):
+                    top = (g - first) * block_len
+                    for p in range(pairs):
+                        at = top + p * own_len
+                        out_ref[
+                            p, low : low + own_len, g * head_dim : (g + 1) * head_dim
+                        ] = mixed[at : at + own_len]
+                    for n, term in enumerate(terms):
+                        stats = jnp.where(
+                            lane == g * STATS + n, term[top : top + block_len], stats
+                        )
+            for p in range(pairs):
+                out_ref[p, low : low + own_len, lanes:] = stats[
+                    p * own_len : (p + 1) * own_len
+                ].astype(BF16)
+
+    vmem = pl.BlockSpec(memory_space=pltpu.VMEM)
+    return pl.pallas_call(
+        kernel,
+        out_shape=jax.ShapeDtypeStruct((pairs, own_rows, lanes + head_dim), BF16),
+        in_specs=[pl.BlockSpec(memory_space=pltpu.SMEM), vmem, vmem],
+        out_specs=vmem,
+        name="attend_part",
+    )(where, swapped, spread)
+
+
+def experts_forward(incoming, weights):
+    slots, width = incoming.shape
+    hidden_units = weights.shape[0]
+    step_units = 256 if hidden_units % 256 == 0 else hidden_units
+
+    def kernel(rows_ref, gate_ref, up_ref, down_ref, out_ref, sum_ref):
+        step = pl.program_id(0)
+        gate_part = dot(rows_ref[...], gate_ref[...], 1, 1)
+        up_part = dot(rows_ref[...], up_ref[...], 1, 1)
+        hidden = (gate_part / (1.0 + jnp.exp(-gate_part)) * up_part).astype(BF16)
+        part = dot(hidden, down_ref[...], 1, 0)
+
+        @pl.when(step == 0)
+        def _():
+            sum_ref[...] = part
+
+        @pl.when(step > 0)
+        def _():
+            sum_ref[...] += part
+
+        @pl.when(step == pl.num_programs(0) - 1)
+        def _():
+            out_ref[...] = sum_ref[...].astype(BF16)
+
+    whole = pl.BlockSpec((slots, width), lambda i: (0, 0))
+    return pl.pallas_call(
+        kernel,
+        grid=(hidden_units // step_units,),
+        out_shape=jax.ShapeDtypeStruct((slots, width), BF16),
+        in_specs=[
+            whole,
+            pl.BlockSpec((step_units, width), lambda i: (i, 0)),
+            pl.BlockSpec((step_units, width), lambda i: (i, 1)),
+            pl.BlockSpec((step_units, width), lambda i: (i, 2)),
+        ],
+        out_specs=whole,
+        scratch_shapes=[pltpu.VMEM((slots, width), F32)],
+        compiler_params=pltpu.CompilerParams(dimension_semantics=("arbitrary",)),
+        name="experts_forward",
+    )(incoming, weights, weights, weights)
 
 
 def body(
@@ -86,15 +202,12 @@
     local_heads = q_cols // head_dim
     group = local_heads * pairs
 
-    weights = lax.all_gather(
-        jnp.concatenate([gate_weight[0], up_weight[0], down_weight[0]], axis=1),
-        "pair",
-        axis=0,
-        tiled=True,
-    )
+    joined = jnp.concatenate([gate_weight[0], up_weight[0], down_weight[0]], axis=1)
+    weights = lax.all_gather(joined, "pair", axis=0, tiled=True)
 
     normed = normalize(tokens_in, attn_gain)
-    block_rows = exchange(for_each(normed, pairs), "pair").reshape(rows, width)
+    token_send = for_each(normed, pairs)
+    block_rows = exchange(token_send, "pair").reshape(rows, width)
     block_start = lax.axis_index("ctx") * block_len
     own_start = block_start + lax.axis_index("pair") * own_len
     places = jnp.arange(own_len)
@@ -133,48 +246,29 @@
     )
     key_own = rotate(key_own.astype(F32), rope_tables(own_pos.astype(F32), head_dim))
     both = jnp.concatenate([key_own, value_own], axis=1)
-    spread = exchange(for_each(both, blocks), "ctx").reshape(blocks, seqs, own_len, 2 * head_dim)
-    spread = jnp.moveaxis(spread, 1, 0).reshape(seqs, blocks * own_len, 2 * head_dim)
-    keys = spread[..., :head_dim]
-    values = spread[..., head_dim:]
-
-    queries = (
-        swapped[:, :rows]
-        .reshape(pairs, pairs, seqs, own_len, local_heads, head_dim)
-        .transpose(2, 0, 4, 1, 3, 5)
-        .reshape(seqs, group * block_len, head_dim)
-    )
-    key_pos = (
-        jnp.arange(blocks)[:, None] * block_len + lax.axis_index("pair") * own_len + places
-    ).reshape(1, blocks * own_len)
-    query_pos = (jnp.zeros((group, 1), jnp.int32) + block_start + jnp.arange(block_len)).reshape(
-        group * block_len, 1
-    )
-    allowed = (key_pos <= query_pos)[None]
-    scores = jnp.einsum("sqd,skd->sqk", queries, keys, preferred_element_type=F32) * (
-        head_dim ** (-0.5)
-    )
-    scores = jnp.where(allowed, scores, MASKED)
-    peak = jnp.max(scores, axis=-1)
-    probs = jnp.where(allowed, jnp.exp(scores - peak[..., None]), 0.0)
-    total = jnp.sum(probs, axis=-1)
-    mixed = jnp.einsum("sqk,skd->sqd", probs.astype(BF16), values, preferred_element_type=F32)
-
-    stats = jnp.stack(pieces(peak) + pieces(total), axis=-1).astype(BF16)
-    stats = stats.reshape(seqs, group, pairs, own_len, 6).transpose(2, 0, 3, 1, 4)
-    stats = stats.reshape(pairs, own_rows, group * 6)
-    mixed = (
-        mixed.astype(BF16)
-        .reshape(seqs, group, pairs, own_len, head_dim)
-        .transpose(2, 0, 3, 1, 4)
-        .reshape(pairs, own_rows, group * head_dim)
-    )
-    merged = exchange(
-        jnp.concatenate(
-            [mixed, jnp.pad(stats, ((0, 0), (0, 0), (0, head_dim - group * 6)))], axis=2
-        ),
-        "pair",
-    )
+    kv_send = for_each(both, blocks)
+    spread = exchange(kv_send, "ctx")
+
+    head = lax.axis_index("head")
+    group_cols = group * head_dim
+    out_mine = lax.dynamic_slice_in_dim(output_matrix, head * group_cols, group_cols, 0)
+    out_theirs = lax.dynamic_slice_in_dim(
+        output_matrix, (heads - 1 - head) * group_cols, group_cols, 0
+    )
+    out_other = lax.ppermute(
+        out_theirs, "head", [(h, heads - 1 - h) for h in range(heads)]
+    )
+
+    parts = attend_part(
+        jnp.stack([block_start, lax.axis_index("pair")]).astype(jnp.int32),
+        swapped,
+        spread,
+        seqs,
+        own_len,
+        local_heads,
+        head_dim,
+    )
+    merged = exchange(parts, "pair")
     part_stats = (
         merged[..., group * head_dim : group * head_dim + group * 6]
         .astype(F32)
@@ -188,27 +282,23 @@
     attended = jnp.sum(scale[..., None] * part_mixed.astype(F32), axis=0).astype(BF16)
     attended = attended.reshape(own_rows, group * head_dim)
 
-    gathered_heads = exchange(for_each(attended, heads * pairs), ("head", "pair"))
-    gathered_heads = gathered_heads.reshape(heads, rows, group * head_dim)
-    projected = sum(
-        dot(
-            gathered_heads[h],
-            output_matrix[h * group * head_dim : (h + 1) * group * head_dim],
-            1,
-            0,
-        )
-        for h in range(heads)
+    gathered_heads = exchange(for_each(attended, pairs), "pair").reshape(rows, group_cols)
+    projected = jnp.stack(
+        [dot(gathered_heads, out_mine, 1, 0), dot(gathered_heads, out_other, 1, 0)]
     ).astype(BF16)
     out_cols = output_matrix.shape[1]
     projected = (
-        projected.reshape(pairs, seqs, own_len, out_cols)
-        .transpose(1, 0, 2, 3)
-        .reshape(seqs * pairs, own_len, out_cols)
-    )
-    owned = exchange(projected, ("head", "pair"))
+        projected.reshape(2, pairs, seqs, own_len, out_cols)
+        .transpose(2, 1, 0, 3, 4)
+        .reshape(seqs * pairs, 2 * own_len, out_cols)
+    )
+    owned = exchange(projected, ("head", "pair")).reshape(
+        heads, pairs, 2, own_len, out_cols
+    ).astype(F32)
+    owned = (owned[:, :, 0] + owned[::-1, :, 1]).reshape(heads * pairs, own_len, out_cols)
     owned = jnp.moveaxis(owned, 0, 1).reshape(own_len, width)
     own_tokens = lax.dynamic_index_in_dim(tokens_in, lax.axis_index("head"), 0, keepdims=False)
-    residual = (own_tokens.astype(F32) + owned.astype(F32)).astype(BF16)
+    residual = (own_tokens.astype(F32) + rounded(owned)).astype(BF16)
     moe_in = normalize(residual, moe_gain)
 
     experts = blocks * heads
@@ -225,17 +315,15 @@
     outgoing = dot(placing, moe_in, 0, 0).astype(BF16)
     incoming = exchange(outgoing.reshape(experts, capacity, width), ("ctx", "head"))
     incoming = incoming.reshape(slots, width)
-    gate_rows, up_rows, down_rows = jnp.split(weights, 3, axis=1)
-    gate_part = dot(incoming, gate_rows, 1, 1)
-    up_part = dot(incoming, up_rows, 1, 1)
-    hidden = (jax.nn.silu(gate_part) * up_part).astype(BF16)
-    expert_out = dot(hidden, down_rows, 1, 0).astype(BF16)
+    expert_out = experts_forward(incoming, weights)
     returned = exchange(expert_out.reshape(experts, capacity, width), ("ctx", "head"))
     returned = returned.reshape(slots, width)
-    gathered = returned[slot_ids.reshape(-1)].reshape(own_len, top, width)
-    mixture = jnp.sum(
-        combine_weights.reshape(own_len, top, 1) * gathered.astype(F32), axis=1
-    )
+    share = jnp.sum(
+        jnp.where(chosen_slot, combine_weights.reshape(own_len, top, 1), 0.0), axis=1
+    )
+    high = rounded(share)
+    mixture = dot(jnp.concatenate([high, share - high], axis=0).astype(BF16), returned, 1, 0)
+    mixture = mixture[:own_len] + mixture[own_len:]
     return (residual.astype(F32) + mixture).astype(BF16)[None]
 
 

time: 240 us -> 231 us (0.963)
  matrix products: 18.3 us -> 3.09 us
  blocking collectives: 52.9 us -> 38.9 us
  Pallas kernels: 0 us -> 12.3 us
  starting transfers between devices: 50.8 us -> 59.2 us
  other arithmetic: 10.8 us -> 6.93 us
  waiting for transfers between devices: 81.3 us -> 84.9 us
    all_to_all x2 -> x1, blocking collectives: 52.9 us -> 38.9 us  [exchange(): return lax.all_to_all(tiles, axis, 0, 0, tiled=True)]
    pallas_call x0 -> x2, Pallas kernels: none -> 12.3 us  [the longest x1 8 us: experts_forward(): pl.pallas_call(kernel, grid=(hidden_units // step_units,), out_shape=jax....]
    dot_general x7 -> x6, matrix products: 11.9 us -> 3.09 us  [dot(): lax.dot_general(a, b, (((a_dim,), (b_dim,)), ((), ())), preferred_element...]
    dot_general x2 -> x0, matrix products: 6.43 us -> none  [the longest x1 3.38 us: body(): jnp.einsum('sqk,skd->sqd', probs.astype(BF16), values, preferred_element_...]
    ppermute x0 -> x1, starting transfers between devices: none -> 5.02 us  [body(): lax.ppermute(out_theirs, 'head', [(h, heads - 1 - h) for h in range(heads)])]
    reduce_sum x2 -> x1, other arithmetic: 4.13 us -> 0.12 us  [body(): jnp.sum(jnp.where(chosen_slot, combine_weights.reshape(own_len, top, 1),...]
    all_to_all x6 -> x7, waiting for transfers between devices: 81.3 us -> 84.9 us  [exchange(): return lax.all_to_all(tiles, axis, 0, 0, tiled=True)]
    all_to_all x6 -> x7, starting transfers between devices: 50.8 us -> 54.1 us  [exchange(): return lax.all_to_all(tiles, axis, 0, 0, tiled=True)]
  transfers between devices with their start and end apart: 7 -> 9, of which waited for: 6 -> 7; matrix products, arithmetic and copies ran while one was open for 10% -> 5% of each run, Pallas kernels for 0% -> 2%
where the time goes in v3:
time: 231 us; the launch traced here: 230 us
  waiting for transfers between devices  84.9 us (37%)
  starting transfers between devices  59.2 us (26%)
  blocking collectives  38.9 us (17%)
  between operations  13.8 us (6%)
  Pallas kernels  12.3 us (5%)
  local copies, waits for them, and re-layouts  10.9 us (5%)
  other arithmetic  6.93 us (3%)
  matrix products  3.09 us (1%)
    all_to_all x7, waiting for transfers between devices, exchange(): return lax.all_to_all(tiles, axis, 0, 0, tiled=True)  84.9 us
    all_to_all x7, starting transfers between devices, exchange(): return lax.all_to_all(tiles, axis, 0, 0, tiled=True)  54.1 us
    all_to_all x1, blocking collectives, exchange(): return lax.all_to_all(tiles, axis, 0, 0, tiled=True)  38.9 us
    pallas_call x1, Pallas kernels, experts_forward(): pl.pallas_call(kernel, grid=(hidden_units // step_units,), out_shape=jax....  8 us
    ppermute x1, starting transfers between devices, body(): lax.ppermute(out_theirs, 'head', [(h, heads - 1 - h) for h in range(heads)])  5.02 us
  transfers between devices with their start and end apart: 9, of which 7 were waited for; matrix products, arithmetic and copies ran while one was open for 5% of the time, Pallas kernels for 2%

profile of v3, /device:TPU:1, one launch (start us, length us, event | category | flops | bytes accessed | tf_op | source)
XLA Modules:
  0.0 229.9 jit_solution(17911887674676238507)
XLA Ops:
  6.6 3.4 %pad_maximum_fusion = bf16[192,6144]{1,0:T(8,128)(2,1)} fusion(bf16[192,2048]{1,0:T(8,128)(2,1)} %bitcast.75, bf16[192,2048]{1,0:T(8,128)(2,1)} %bitcast.76, bf16[192,2048]{1,0:T(8,128)(2,1)} %bitcast.77), kind=kLoop, calls=%fused_computation.2 | loop fusion | flops 7077888 | bytes 4718592 | tf_op jit(solution)/shard_map/concatenate | solution.py:205
  10.0 0.1 fusion.10
  10.1 0.1 fusion.12
  10.2 0.9 broadcast_in_dim.21
  11.1 4.8 %all-to-all-start = ((bf16[4,2,16,2048]{3,2,1,0:T(8,128)(2,1)}), bf16[4,2,16,2048]{3,2,1,0:T(8,128)(2,1)S(1)}, u32[]{:S(2)}, u32[]{:S(2)}) async-start(bf16[4,2,16,2048]{3,2,1,0:T(8,128)(2,1)} %broadcast_in_dim.21), calls=%async_computation | async-start | bytes 1048576 | tf_op jit(solution)/shard_map/all_to_all | solution.py:17
  16.1 6.8 %all-to-all-done = bf16[4,2,16,2048]{3,2,1,0:T(8,128)(2,1)S(1)} async-done(((bf16[4,2,16,2048]{3,2,1,0:T(8,128)(2,1)}), bf16[4,2,16,2048]{3,2,1,0:T(8,128)(2,1)S(1)}, u32[]{:S(2)}, u32[]{:S(2)}) %all-to-all-start) | async-done | bytes 524320 | tf_op jit(solution)/shard_map/all_to_all | solution.py:17
  22.9 0.5 fusion.61
  23.4 0.2 fusion.37
  23.6 0.1 copy.48
  23.8 0.3 convolution_convert_fusion.3
  24.1 0.1 copy.49
  24.2 0.8 fusion.9
  25.0 3.5 %all-to-all-start.1 = ((bf16[4,160,256]{2,1,0:T(8,128)(2,1)}), bf16[4,160,256]{2,1,0:T(8,128)(2,1)S(1)}, u32[]{:S(2)}, u32[]{:S(2)}) async-start(bf16[4,160,256]{2,1,0:T(8,128)(2,1)} %fusion.9), calls=%async_computation.1 | async-start | bytes 655360 | tf_op jit(solution)/shard_map/all_to_all | solution.py:17
  28.5 5.7 %all-to-all-done.1.swapped_ref = bf16[4,160,256]{2,1,0:T(8,128)(2,1)S(1)} async-done(((bf16[4,160,256]{2,1,0:T(8,128)(2,1)}), bf16[4,160,256]{2,1,0:T(8,128)(2,1)S(1)}, u32[]{:S(2)}, u32[]{:S(2)}) %all-to-all-start.1) | async-done | bytes 327712 | tf_op jit(solution)/shard_map/all_to_all | solution.py:17
  34.4 0.1 fusion.51
  34.7 1.1 broadcast_in_dim.23
  35.8 22.6 %all-to-all-start.2 = ((bf16[64,32,256]{2,1,0:T(8,128)(2,1)}), bf16[64,32,256]{2,1,0:T(8,128)(2,1)S(1)}, u32[]{:S(2)}, u32[]{:S(2)}) async-start(bf16[64,32,256]{2,1,0:T(8,128)(2,1)} %broadcast_in_dim.23), calls=%async_computation.2 | async-start | bytes 2097152 | tf_op jit(solution)/shard_map/all_to_all | solution.py:17
  58.5 5.0 %collective-permute-start = (bf16[1024,256]{1,0:T(8,128)(2,1)S(1)}, bf16[1024,256]{1,0:T(8,128)(2,1)}, u32[]{:S(2)}, u32[]{:S(2)}) collective-permute-start(bf16[1024,256]{1,0:T(8,128)(2,1)S(1)} %constant_dynamic-slice_fusion), channel_id=1, source_target_pairs={{0,4},{4,0},{1,5},{5,1},{2,6},{6,2},{3,7},{7,3},{8,12},{12,8},{9,1... | collective-permute-start | bytes 1572872 | tf_op jit(solution)/shard_map/ppermute | solution.py:258
  63.7 0.6 pad_add_fusion.where_ref
  64.3 19.5 %all-to-all-done.2.spread_ref = bf16[64,32,256]{2,1,0:T(8,128)(2,1)S(1)} async-done(((bf16[64,32,256]{2,1,0:T(8,128)(2,1)}), bf16[64,32,256]{2,1,0:T(8,128)(2,1)S(1)}, u32[]{:S(2)}, u32[]{:S(2)}) %all-to-all-start.2) | async-done | bytes 1048608 | tf_op jit(solution)/shard_map/all_to_all | solution.py:17
  83.8 1.0 copy-done.1
  84.8 4.3 %attend_part.1 = bf16[4,32,1152]{2,1,0:T(8,128)(2,1)} custom-call(s32[2]{0:T(128)} %pad_add_fusion.where_ref, bf16[4,160,256]{2,1,0:T(8,128)(2,1)} %copy-done.2, bf16[64,32,256]{2,1,0:T(8,128)(2,1)} %copy-done.1), custom_call_target="tpu_custom_call" | custom-call | tf_op jit(solution)/shard_map/attend_part/pallas_call | solution.py:127
  89.1 3.6 %all-to-all-start.3 = ((bf16[4,32,1152]{2,1,0:T(8,128)(2,1)}), bf16[4,32,1152]{2,1,0:T(8,128)(2,1)S(1)}, u32[]{:S(2)}, u32[]{:S(2)}) async-start(bf16[4,32,1152]{2,1,0:T(8,128)(2,1)} %attend_part.1), calls=%async_computation.3 | async-start | bytes 589824 | tf_op jit(solution)/shard_map/all_to_all | solution.py:17
  92.7 0.2 convert_reduce_fusion
  93.1 8.7 %all-to-all-done.3 = bf16[4,32,1152]{2,1,0:T(8,128)(2,1)S(1)} async-done(((bf16[4,32,1152]{2,1,0:T(8,128)(2,1)}), bf16[4,32,1152]{2,1,0:T(8,128)(2,1)S(1)}, u32[]{:S(2)}, u32[]{:S(2)}) %all-to-all-start.3) | async-done | bytes 294944 | tf_op jit(solution)/shard_map/all_to_all | solution.py:17
  102.0 0.2 mul.185
  102.4 0.7 broadcast_in_dim.24
  103.1 3.4 %all-to-all-start.4 = ((bf16[4,32,1024]{2,1,0:T(8,128)(2,1)}), bf16[4,32,1024]{2,1,0:T(8,128)(2,1)S(1)}, u32[]{:S(2)}, u32[]{:S(2)}) async-start(bf16[4,32,1024]{2,1,0:T(8,128)(2,1)} %broadcast_in_dim.24), calls=%async_computation.4 | async-start | bytes 524288 | tf_op jit(solution)/shard_map/all_to_all | solution.py:17
  106.6 8.4 %all-to-all-done.4 = bf16[4,32,1024]{2,1,0:T(8,128)(2,1)S(1)} async-done(((bf16[4,32,1024]{2,1,0:T(8,128)(2,1)}), bf16[4,32,1024]{2,1,0:T(8,128)(2,1)S(1)}, u32[]{:S(2)}, u32[]{:S(2)}) %all-to-all-start.4) | async-done | bytes 262176 | tf_op jit(solution)/shard_map/all_to_all | solution.py:17
  115.0 0.2 fusion.1
  115.3 1.3 fusion.2
  116.6 0.7 copy.52
  117.2 9.8 %all-to-all-start.5 = ((bf16[8,32,256]{2,1,0:T(8,128)(2,1)}), bf16[8,32,256]{2,1,0:T(8,128)(2,1)S(1)}, u32[]{:S(2)}, u32[]{:S(2)}) async-start(bf16[8,32,256]{2,1,0:T(8,128)(2,1)} %bitcast.22), calls=%async_computation.5 | async-start | bytes 262144 | tf_op jit(solution)/shard_map/all_to_all | solution.py:17
  127.1 0.1 fusion.22
  127.2 5.1 %all-to-all-done.5 = bf16[8,32,256]{2,1,0:T(8,128)(2,1)S(1)} async-done(((bf16[8,32,256]{2,1,0:T(8,128)(2,1)}), bf16[8,32,256]{2,1,0:T(8,128)(2,1)S(1)}, u32[]{:S(2)}, u32[]{:S(2)}) %all-to-all-start.5) | async-done | bytes 131104 | tf_op jit(solution)/shard_map/all_to_all | solution.py:17
  132.3 0.1 fusion.16
  132.5 0.5 convolution_convert_fusion
  133.0 0.7 reshape.155
  133.7 38.9 %all_to_all.40 = bf16[128,2,2048]{2,1,0:T(2,128)(2,1)S(1)} all-to-all(bf16[128,2,2048]{2,1,0:T(2,128)(2,1)S(1)} %reshape.155), channel_id=1, replica_groups=mesh['ctx'=64,'head'=2,'pair'=4] {'ctx','head'}, dimensions={0} | all-to-all | bytes 2097152 | tf_op jit(solution)/shard_map/all_to_all | solution.py:17
  172.6 1.2 reshape.156.rows_ref
  173.8 8.0 %experts_forward.1 = bf16[256,2048]{1,0:T(8,128)(2,1)} custom-call(bf16[256,2048]{1,0:T(8,128)(2,1)} %reshape.156.rows_ref, bf16[768,6144]{1,0:T(8,128)(2,1)} %all-gather.2.cloned.1.call-done.gate_ref.up_ref.down_ref, bf16[768,6144]{1,0:T(8,128)(2,1)} %all-gather.2.cloned.1.call-done.gate_ref.up_ref.down_ref, ...), custom_call_target="tpu_custom_call" | custom-call | tf_op jit(solution)/shard_map/experts_forward/pallas_call | solution.py:161
  181.8 2.5 %reshape.157 = bf16[128,2,2048]{2,1,0:T(2,128)(2,1)} reshape(bf16[256,2048]{1,0:T(8,128)(2,1)} %experts_forward.1) | data formatting | bytes 2097152 | tf_op jit(solution)/shard_map/reshape | solution.py:319
  184.3 6.4 %all-to-all-start.7 = ((bf16[128,2,2048]{2,1,0:T(2,128)(2,1)}), bf16[128,2,2048]{2,1,0:T(2,128)(2,1)S(1)}, u32[]{:S(2)}, u32[]{:S(2)}) async-start(bf16[128,2,2048]{2,1,0:T(2,128)(2,1)} %reshape.157), calls=%async_computation.7 | async-start | bytes 2097152 | tf_op jit(solution)/shard_map/all_to_all | solution.py:17
  190.8 0.1 select_reduce_fusion
  191.0 30.7 %all-to-all-done.7 = bf16[128,2,2048]{2,1,0:T(2,128)(2,1)S(1)} async-done(((bf16[128,2,2048]{2,1,0:T(2,128)(2,1)}), bf16[128,2,2048]{2,1,0:T(2,128)(2,1)S(1)}, u32[]{:S(2)}, u32[]{:S(2)}) %all-to-all-start.7) | async-done | bytes 1048608 | tf_op jit(solution)/shard_map/all_to_all | solution.py:17
  221.7 0.4 reshape.158
  222.1 0.3 fusion.53
  222.4 0.7 fusion.23
  (62 shorter events, 1.7 us)
Async XLA Ops:
  6.5 51.9 %copy-start = (bf16[2048,256]{1,0:T(8,128)(2,1)S(1)}, bf16[2048,256]{1,0:T(8,128)(2,1)}, u32[]{:S(2)}) copy-start(bf16[2048,256]{1,0:T(8,128)(2,1)} %param.17) | copy-start | bytes 3145732
  6.5 3.5 %copy-start.4 = (bf16[2,16,2048]{2,1,0:T(8,128)(2,1)S(1)}, bf16[2,16,2048]{2,1,0:T(8,128)(2,1)}, u32[]{:S(2)}) copy-start(bf16[2,16,2048]{2,1,0:T(8,128)(2,1)} %param.12) | copy-start | bytes 393220
  6.5 3.6 %copy-start.7 = (f32[2048]{0:T(1024)S(1)}, f32[2048]{0:T(1024)}, u32[]{:S(2)}) copy-start(f32[2048]{0:T(1024)} %param.13) | copy-start | bytes 24580
  6.5 16.3 %copy-start.3 = (bf16[2048,256]{1,0:T(8,128)(2,1)S(1)}, bf16[2048,256]{1,0:T(8,128)(2,1)}, u32[]{:S(2)}) copy-start(bf16[2048,256]{1,0:T(8,128)(2,1)} %param.14) | copy-start | bytes 3145732
  6.5 167.3 %all-gather.2.cloned.1.call-start = ((), (), s32[]{:S(2)}) async-start(), calls=%async_computation.8 | async-start | bytes 11796480 | tf_op jit(solution)/shard_map/all_gather | solution.py:206
  6.6 17.2 %copy-start.9 = (bf16[32,2048]{1,0:T(8,128)(2,1)S(1)}, bf16[32,2048]{1,0:T(8,128)(2,1)}, u32[]{:S(2)}) copy-start(bf16[32,2048]{1,0:T(8,128)(2,1)} %param.16) | copy-start | bytes 393220
  6.6 17.2 %copy-start.10 = (bf16[32,2048]{1,0:T(8,128)(2,1)S(1)}, bf16[32,2048]{1,0:T(8,128)(2,1)}, u32[]{:S(2)}) copy-start(bf16[32,2048]{1,0:T(8,128)(2,1)} %param.15) | copy-start | bytes 393220
  11.1 11.8 %all-to-all-start = ((bf16[4,2,16,2048]{3,2,1,0:T(8,128)(2,1)}), bf16[4,2,16,2048]{3,2,1,0:T(8,128)(2,1)S(1)}, u32[]{:S(2)}, u32[]{:S(2)}) async-start(bf16[4,2,16,2048]{3,2,1,0:T(8,128)(2,1)} %broadcast_in_dim.21), calls=%async_computation | async-start | bytes 1048576 | tf_op jit(solution)/shard_map/all_to_all | solution.py:17
  15.9 47.6 %copy-start.5 = (s32[1,16,8]{1,2,0:T(8,128)S(1)}, s32[1,16,8]{1,2,0:T(8,128)}, u32[]{:S(2)}) copy-start(s32[1,16,8]{1,2,0:T(8,128)} %param.19) | copy-start | bytes 1540
  25.0 9.3 %all-to-all-start.1 = ((bf16[4,160,256]{2,1,0:T(8,128)(2,1)}), bf16[4,160,256]{2,1,0:T(8,128)(2,1)S(1)}, u32[]{:S(2)}, u32[]{:S(2)}) async-start(bf16[4,160,256]{2,1,0:T(8,128)(2,1)} %fusion.9), calls=%async_computation.1 | async-start | bytes 655360 | tf_op jit(solution)/shard_map/all_to_all | solution.py:17
  34.3 49.5 %copy-start.2 = (bf16[4,160,256]{2,1,0:T(8,128)(2,1)}, bf16[4,160,256]{2,1,0:T(8,128)(2,1)S(1)}, u32[]{:S(2)}) copy-start(bf16[4,160,256]{2,1,0:T(8,128)(2,1)S(1)} %all-to-all-done.1.swapped_ref) | copy-start | bytes 983044
  35.8 48.0 %all-to-all-start.2 = ((bf16[64,32,256]{2,1,0:T(8,128)(2,1)}), bf16[64,32,256]{2,1,0:T(8,128)(2,1)S(1)}, u32[]{:S(2)}, u32[]{:S(2)}) async-start(bf16[64,32,256]{2,1,0:T(8,128)(2,1)} %broadcast_in_dim.23), calls=%async_computation.2 | async-start | bytes 2097152 | tf_op jit(solution)/shard_map/all_to_all | solution.py:17
  58.5 56.8 %collective-permute-start = (bf16[1024,256]{1,0:T(8,128)(2,1)S(1)}, bf16[1024,256]{1,0:T(8,128)(2,1)}, u32[]{:S(2)}, u32[]{:S(2)}) collective-permute-start(bf16[1024,256]{1,0:T(8,128)(2,1)S(1)} %constant_dynamic-slice_fusion), channel_id=1, source_target_pairs={{0,4},{4,0},{1,5},{5,1},{2,6},{6,2},{3,7},{7,3},{8,12},{12,8},{9,1... | collective-permute-start | bytes 1572872 | tf_op jit(solution)/shard_map/ppermute | solution.py:258
  83.8 1.0 copy-start.1
  89.1 43.4 %copy-start.6 = (f32[2048]{0:T(1024)S(1)}, f32[2048]{0:T(1024)}, u32[]{:S(2)}) copy-start(f32[2048]{0:T(1024)} %param.18) | copy-start | bytes 24580
  89.1 12.6 %all-to-all-start.3 = ((bf16[4,32,1152]{2,1,0:T(8,128)(2,1)}), bf16[4,32,1152]{2,1,0:T(8,128)(2,1)S(1)}, u32[]{:S(2)}, u32[]{:S(2)}) async-start(bf16[4,32,1152]{2,1,0:T(8,128)(2,1)} %attend_part.1), calls=%async_computation.3 | async-start | bytes 589824 | tf_op jit(solution)/shard_map/all_to_all | solution.py:17
  103.1 11.9 %all-to-all-start.4 = ((bf16[4,32,1024]{2,1,0:T(8,128)(2,1)}), bf16[4,32,1024]{2,1,0:T(8,128)(2,1)S(1)}, u32[]{:S(2)}, u32[]{:S(2)}) async-start(bf16[4,32,1024]{2,1,0:T(8,128)(2,1)} %broadcast_in_dim.24), calls=%async_computation.4 | async-start | bytes 524288 | tf_op jit(solution)/shard_map/all_to_all | solution.py:17
  117.2 15.0 %all-to-all-start.5 = ((bf16[8,32,256]{2,1,0:T(8,128)(2,1)}), bf16[8,32,256]{2,1,0:T(8,128)(2,1)S(1)}, u32[]{:S(2)}, u32[]{:S(2)}) async-start(bf16[8,32,256]{2,1,0:T(8,128)(2,1)} %bitcast.22), calls=%async_computation.5 | async-start | bytes 262144 | tf_op jit(solution)/shard_map/all_to_all | solution.py:17
  173.8 16.9 %copy-start.8 = (f32[1,16,8]{1,2,0:T(8,128)S(1)}, f32[1,16,8]{1,2,0:T(8,128)}, u32[]{:S(2)}) copy-start(f32[1,16,8]{1,2,0:T(8,128)} %param.20) | copy-start | bytes 1540
  184.3 37.4 %all-to-all-start.7 = ((bf16[128,2,2048]{2,1,0:T(2,128)(2,1)}), bf16[128,2,2048]{2,1,0:T(2,128)(2,1)S(1)}, u32[]{:S(2)}, u32[]{:S(2)}) async-start(bf16[128,2,2048]{2,1,0:T(2,128)(2,1)} %reshape.157), calls=%async_computation.7 | async-start | bytes 2097152 | tf_op jit(solution)/shard_map/all_to_all | solution.py:17
Sparse Core Ops, SparseCore 0:
  10.1 109.9 all-gather.1

commit v4 on v3

--- a/solution.py
+++ b/solution.py
@@ -133,46 +133,59 @@
     )(where, swapped, spread)
 
 
-def experts_forward(incoming, weights):
+def experts_forward(incoming, pieces):
     slots, width = incoming.shape
-    hidden_units = weights.shape[0]
+    counts = [piece.shape[0] for piece in pieces]
+    offsets = [sum(counts[:n]) for n in range(len(pieces))]
+    hidden_units = sum(counts)
     step_units = 256 if hidden_units % 256 == 0 else hidden_units
 
-    def kernel(rows_ref, gate_ref, up_ref, down_ref, out_ref, sum_ref):
-        step = pl.program_id(0)
-        gate_part = dot(rows_ref[...], gate_ref[...], 1, 1)
-        up_part = dot(rows_ref[...], up_ref[...], 1, 1)
-        hidden = (gate_part / (1.0 + jnp.exp(-gate_part)) * up_part).astype(BF16)
-        part = dot(hidden, down_ref[...], 1, 0)
-
-        @pl.when(step == 0)
-        def _():
-            sum_ref[...] = part
-
-        @pl.when(step > 0)
-        def _():
-            sum_ref[...] += part
-
-        @pl.when(step == pl.num_programs(0) - 1)
-        def _():
-            out_ref[...] = sum_ref[...].astype(BF16)
-
-    whole = pl.BlockSpec((slots, width), lambda i: (0, 0))
+    def kernel(rows_ref, *refs):
+        piece_refs = refs[: len(pieces)]
+        out_ref, sum_ref, gate_ref, up_ref, down_ref, sems = refs[len(pieces) :]
+        copies = [
+            [
+                pltpu.make_async_copy(
+                    ref.at[:, pl.ds(n * width, width)],
+                    target.at[pl.ds(offset, count), :],
+                    sems.at[i * 3 + n],
+                )
+                for n, target in enumerate((gate_ref, up_ref, down_ref))
+            ]
+            for i, (ref, offset, count) in enumerate(zip(piece_refs, offsets, counts))
+        ]
+        for group in copies:
+            for copy in group:
+                copy.start()
+        arrived = 0
+        for low in range(0, hidden_units, step_units):
+            while arrived < len(pieces) and offsets[arrived] < low + step_units:
+                for copy in copies[arrived]:
+                    copy.wait()
+                arrived += 1
+            span = slice(low, low + step_units)
+            gate_part = dot(rows_ref[...], gate_ref[span, :], 1, 1)
+            up_part = dot(rows_ref[...], up_ref[span, :], 1, 1)
+            hidden = (gate_part / (1.0 + jnp.exp(-gate_part)) * up_part).astype(BF16)
+            part = dot(hidden, down_ref[span, :], 1, 0)
+            if low > 0:
+                part = sum_ref[...] + part
+            if low + step_units < hidden_units:
+                sum_ref[...] = part
+            else:
+                out_ref[...] = part.astype(BF16)
+
+    vmem = pl.BlockSpec(memory_space=pltpu.VMEM)
     return pl.pallas_call(
         kernel,
-        grid=(hidden_units // step_units,),
         out_shape=jax.ShapeDtypeStruct((slots, width), BF16),
-        in_specs=[
-            whole,
-            pl.BlockSpec((step_units, width), lambda i: (i, 0)),
-            pl.BlockSpec((step_units, width), lambda i: (i, 1)),
-            pl.BlockSpec((step_units, width), lambda i: (i, 2)),
-        ],
-        out_specs=whole,
-        scratch_shapes=[pltpu.VMEM((slots, width), F32)],
-        compiler_params=pltpu.CompilerParams(dimension_semantics=("arbitrary",)),
+        in_specs=[vmem] + [pl.BlockSpec(memory_space=pl.ANY)] * len(pieces),
+        out_specs=vmem,
+        scratch_shapes=[pltpu.VMEM((slots, width), F32)]
+        + [pltpu.VMEM((hidden_units, width), BF16)] * 3
+        + [pltpu.SemaphoreType.DMA((3 * len(pieces),))],
         name="experts_forward",
-    )(incoming, weights, weights, weights)
+    )(incoming, *pieces)
 
 
 def body(
@@ -202,8 +215,11 @@
     local_heads = q_cols // head_dim
     group = local_heads * pairs
 
+    up_ring = [(i, (i + 1) % pairs) for i in range(pairs)]
+    down_ring = [(i, (i - 1) % pairs) for i in range(pairs)]
     joined = jnp.concatenate([gate_weight[0], up_weight[0], down_weight[0]], axis=1)
-    weights = lax.all_gather(joined, "pair", axis=0, tiled=True)
+    from_below = lax.ppermute(joined, "pair", up_ring)
+    from_above = lax.ppermute(joined, "pair", down_ring)
 
     normed = normalize(tokens_in, attn_gain)
     token_send = for_each(normed, pairs)
@@ -226,19 +242,17 @@
         ],
         axis=1,
     )
-    swapped = exchange(
-        jnp.concatenate(
-            [
-                for_each(query, pairs),
-                jnp.pad(
-                    key_value.reshape(pairs, own_rows, 2 * part_cols),
-                    ((0, 0), (0, 0), (0, q_cols - 2 * part_cols)),
-                ),
-            ],
-            axis=1,
-        ),
-        "pair",
-    )
+    swap_send = jnp.concatenate(
+        [
+            for_each(query, pairs),
+            jnp.pad(
+                key_value.reshape(pairs, own_rows, 2 * part_cols),
+                ((0, 0), (0, 0), (0, q_cols - 2 * part_cols)),
+            ),
+        ],
+        axis=1,
+    )
+    swapped = exchange(swap_send, "pair")
     own_pos = (own_start + jnp.zeros((seqs, 1), jnp.int32) + places).reshape(own_rows)
     key_own = jnp.concatenate([swapped[p, rows:, :part_cols] for p in range(pairs)], axis=1)
     value_own = jnp.concatenate(
@@ -313,9 +327,14 @@
     chosen_slot = slot_ids[..., None] == jnp.arange(slots)[None, None, :]
     placing = jnp.any(chosen_slot, axis=1).astype(BF16)
     outgoing = dot(placing, moe_in, 0, 0).astype(BF16)
-    incoming = exchange(outgoing.reshape(experts, capacity, width), ("ctx", "head"))
+    outgoing = outgoing.reshape(experts, capacity, width)
+    incoming = exchange(outgoing, ("ctx", "head"))
     incoming = incoming.reshape(slots, width)
-    expert_out = experts_forward(incoming, weights)
+
+    half = joined.shape[0] // 2
+    far_low = lax.ppermute(from_below[:half], "pair", up_ring)
+    far_high = lax.ppermute(from_above[half:], "pair", down_ring)
+    expert_out = experts_forward(incoming, [joined, from_below, from_above, far_low, far_high])
     returned = exchange(expert_out.reshape(experts, capacity, width), ("ctx", "head"))
     returned = returned.reshape(slots, width)
     share = jnp.sum(

time: 231 us -> 256 us (1.11)
  blocking collectives: 38.9 us -> 0 us
  starting transfers between devices: 59.2 us -> 93.5 us
  waiting for transfers between devices: 84.9 us -> 108 us
  between operations: 13.8 us -> 0.44 us
  local copies, waits for them, and re-layouts: 10.9 us -> 21.9 us
  matrix products: 3.09 us -> 7.03 us
  other arithmetic: 6.93 us -> 10.5 us
    all_to_all x1 -> x0, blocking collectives: 38.9 us -> none  [exchange(): return lax.all_to_all(tiles, axis, 0, 0, tiled=True)]
    all_to_all x7 -> x8, waiting for transfers between devices: 84.9 us -> 107 us  [exchange(): return lax.all_to_all(tiles, axis, 0, 0, tiled=True)]
    all_to_all x7 -> x8, starting transfers between devices: 54.1 us -> 74.3 us  [exchange(): return lax.all_to_all(tiles, axis, 0, 0, tiled=True)]
    ppermute x0 -> x4, starting transfers between devices: none -> 13.2 us  [the longest x1 4.3 us: body(): from_above = lax.ppermute(joined, 'pair', down_ring)]
    dot_general x6, matrix products: 3.09 us -> 7.03 us  [dot(): lax.dot_general(a, b, (((a_dim,), (b_dim,)), ((), ())), preferred_element...]
    slice x0 -> x2, local copies, waits for them, and re-layouts: none -> 3.81 us  [the longest x1 2.46 us: body(): far_low = lax.ppermute(from_below[:half], 'pair', up_ring)]
    mul x2, local copies, waits for them, and re-layouts: 0.29 us -> 2.92 us  [body(): scale[..., None] * part_mixed.astype(F32)]
  transfers between devices with their start and end apart: 9 -> 13, of which waited for: 7 -> 9; matrix products, arithmetic and copies ran while one was open for 5% -> 10% of each run, Pallas kernels for 2% -> 2%
where the time goes in v4:
time: 256 us; the launch traced here: 254 us
  waiting for transfers between devices  108 us (42%)
  starting transfers between devices  93.5 us (37%)
  local copies, waits for them, and re-layouts  21.9 us (9%)
  Pallas kernels  12.3 us (5%)
  other arithmetic  10.5 us (4%)
  matrix products  7.03 us (3%)
    all_to_all x8, waiting for transfers between devices, exchange(): return lax.all_to_all(tiles, axis, 0, 0, tiled=True)  107 us
    all_to_all x8, starting transfers between devices, exchange(): return lax.all_to_all(tiles, axis, 0, 0, tiled=True)  74.3 us
    pallas_call x1, Pallas kernels, experts_forward(): pl.pallas_call(kernel, out_shape=jax.ShapeDtypeStruct((slots, width), BF1...  7.92 us
    dot_general x6, matrix products, dot(): lax.dot_general(a, b, (((a_dim,), (b_dim,)), ((), ())), preferred_element...  7.03 us
    ppermute x1, starting transfers between devices, body(): lax.ppermute(out_theirs, 'head', [(h, heads - 1 - h) for h in range(heads)])  5.99 us
  transfers between devices with their start and end apart: 13, of which 9 were waited for; matrix products, arithmetic and copies ran while one was open for 10% of the time, Pallas kernels for 2%

profile of v4, /device:TPU:1, one launch (start us, length us, event | category | flops | bytes accessed | tf_op | source)
XLA Modules:
  0.0 254.0 jit_solution(12891108947632265522)
XLA Ops:
  0.0 1.1 fusion.10
  1.1 1.0 fusion.12
  2.2 0.8 broadcast_in_dim.21
  3.0 4.8 %all-to-all-start = ((bf16[4,2,16,2048]{3,2,1,0:T(8,128)(2,1)}), bf16[4,2,16,2048]{3,2,1,0:T(8,128)(2,1)S(1)}, u32[]{:S(2)}, u32[]{:S(2)}) async-start(bf16[4,2,16,2048]{3,2,1,0:T(8,128)(2,1)} %broadcast_in_dim.21), calls=%async_computation | async-start | bytes 1048576 | tf_op jit(solution)/shard_map/all_to_all | solution.py:17
  8.0 6.8 %all-to-all-done = bf16[4,2,16,2048]{3,2,1,0:T(8,128)(2,1)S(1)} async-done(((bf16[4,2,16,2048]{3,2,1,0:T(8,128)(2,1)}), bf16[4,2,16,2048]{3,2,1,0:T(8,128)(2,1)S(1)}, u32[]{:S(2)}, u32[]{:S(2)}) %all-to-all-start) | async-done | bytes 524320 | tf_op jit(solution)/shard_map/all_to_all | solution.py:17
  14.8 1.7 fusion.61
  17.4 0.8 fusion.9
  18.1 3.5 %all-to-all-start.1 = ((bf16[4,160,256]{2,1,0:T(8,128)(2,1)}), bf16[4,160,256]{2,1,0:T(8,128)(2,1)S(1)}, u32[]{:S(2)}, u32[]{:S(2)}) async-start(bf16[4,160,256]{2,1,0:T(8,128)(2,1)} %fusion.9), calls=%async_computation.1 | async-start | bytes 655360 | tf_op jit(solution)/shard_map/all_to_all | solution.py:17
  21.7 5.7 %all-to-all-done.1.swapped_ref = bf16[4,160,256]{2,1,0:T(8,128)(2,1)S(1)} async-done(((bf16[4,160,256]{2,1,0:T(8,128)(2,1)}), bf16[4,160,256]{2,1,0:T(8,128)(2,1)S(1)}, u32[]{:S(2)}, u32[]{:S(2)}) %all-to-all-start.1) | async-done | bytes 327712 | tf_op jit(solution)/shard_map/all_to_all | solution.py:17
  27.8 1.2 broadcast_in_dim.23
  29.0 18.0 %all-to-all-start.2 = ((bf16[64,32,256]{2,1,0:T(8,128)(2,1)}), bf16[64,32,256]{2,1,0:T(8,128)(2,1)}, u32[]{:S(2)}, u32[]{:S(2)}) async-start(bf16[64,32,256]{2,1,0:T(8,128)(2,1)} %broadcast_in_dim.23), calls=%async_computation.2 | async-start | bytes 2097152 | tf_op jit(solution)/shard_map/all_to_all | solution.py:17
  47.0 1.8 pad_maximum_fusion.refs_0_
  48.8 2.2 collective-permute-start.1
  51.0 4.3 %collective-permute-start.2 = (bf16[192,6144]{1,0:T(8,128)(2,1)S(1)}, bf16[192,6144]{1,0:T(8,128)(2,1)}, u32[]{:S(2)}, u32[]{:S(2)}) collective-permute-start(bf16[192,6144]{1,0:T(8,128)(2,1)S(1)} %pad_maximum_fusion.refs_0_), channel_id=1, source_target_pairs={{0,3},{1,0},{2,1},{3,2},{4,7},{5,4},{6,5},{7,6},{8,11},{9,8},{10,9... | collective-permute-start | bytes 7077896 | tf_op jit(solution)/shard_map/ppermute | solution.py:222
  55.3 0.8 constant_dynamic-slice_fusion
  56.2 6.0 %collective-permute-start = (bf16[1024,256]{1,0:T(8,128)(2,1)}, bf16[1024,256]{1,0:T(8,128)(2,1)}, u32[]{:S(2)}, u32[]{:S(2)}) collective-permute-start(bf16[1024,256]{1,0:T(8,128)(2,1)} %constant_dynamic-slice_fusion), channel_id=1, source_target_pairs={{0,4},{4,0},{1,5},{5,1},{2,6},{6,2},{3,7},{7,3},{8,12},{12,8},{9,1... | collective-permute-start | bytes 1572872 | tf_op jit(solution)/shard_map/ppermute | solution.py:272
  62.9 8.8 %all-to-all-done.2.spread_ref = bf16[64,32,256]{2,1,0:T(8,128)(2,1)} async-done(((bf16[64,32,256]{2,1,0:T(8,128)(2,1)}), bf16[64,32,256]{2,1,0:T(8,128)(2,1)}, u32[]{:S(2)}, u32[]{:S(2)}) %all-to-all-start.2) | async-done | bytes 1048608 | tf_op jit(solution)/shard_map/all_to_all | solution.py:17
  71.7 4.3 %attend_part.1 = bf16[4,32,1152]{2,1,0:T(8,128)(2,1)} custom-call(s32[2]{0:T(128)} %pad_add_fusion.where_ref, bf16[4,160,256]{2,1,0:T(8,128)(2,1)} %copy-done.2, bf16[64,32,256]{2,1,0:T(8,128)(2,1)} %all-to-all-done.2.spread_ref), custom_call_target="tpu_custom_call" | custom-call | tf_op jit(solution)/shard_map/attend_part/pallas_call | solution.py:127
  76.0 4.1 %all-to-all-start.3 = ((bf16[4,32,1152]{2,1,0:T(8,128)(2,1)}), bf16[4,32,1152]{2,1,0:T(8,128)(2,1)}, u32[]{:S(2)}, u32[]{:S(2)}) async-start(bf16[4,32,1152]{2,1,0:T(8,128)(2,1)} %attend_part.1), calls=%async_computation.3 | async-start | bytes 589824 | tf_op jit(solution)/shard_map/all_to_all | solution.py:17
  80.5 23.9 %all-to-all-done.3 = bf16[4,32,1152]{2,1,0:T(8,128)(2,1)} async-done(((bf16[4,32,1152]{2,1,0:T(8,128)(2,1)}), bf16[4,32,1152]{2,1,0:T(8,128)(2,1)}, u32[]{:S(2)}, u32[]{:S(2)}) %all-to-all-start.3) | async-done | bytes 294944 | tf_op jit(solution)/shard_map/all_to_all | solution.py:17
  104.4 1.4 slice_convert_fusion
  105.8 0.9 copy.50
  106.9 1.0 mul.185
  107.9 1.9 mul.186
  109.8 1.2 multiply_reduce_fusion
  111.0 0.7 broadcast_in_dim.24
  111.7 4.8 %all-to-all-start.4 = ((bf16[4,32,1024]{2,1,0:T(8,128)(2,1)}), bf16[4,32,1024]{2,1,0:T(8,128)(2,1)}, u32[]{:S(2)}, u32[]{:S(2)}) async-start(bf16[4,32,1024]{2,1,0:T(8,128)(2,1)} %broadcast_in_dim.24), calls=%async_computation.4 | async-start | bytes 524288 | tf_op jit(solution)/shard_map/all_to_all | solution.py:17
  116.6 5.6 %all-to-all-done.4 = bf16[4,32,1024]{2,1,0:T(8,128)(2,1)} async-done(((bf16[4,32,1024]{2,1,0:T(8,128)(2,1)}), bf16[4,32,1024]{2,1,0:T(8,128)(2,1)}, u32[]{:S(2)}, u32[]{:S(2)}) %all-to-all-start.4) | async-done | bytes 262176 | tf_op jit(solution)/shard_map/all_to_all | solution.py:17
  122.2 1.2 fusion.1
  123.4 1.4 fusion.2
  125.4 10.2 %all-to-all-start.5 = ((bf16[8,32,256]{2,1,0:T(8,128)(2,1)}), bf16[8,32,256]{2,1,0:T(8,128)(2,1)S(1)}, u32[]{:S(2)}, u32[]{:S(2)}) async-start(bf16[8,32,256]{2,1,0:T(8,128)(2,1)} %bitcast.77), calls=%async_computation.5 | async-start | bytes 262144 | tf_op jit(solution)/shard_map/all_to_all | solution.py:17
  135.8 5.1 %all-to-all-done.5 = bf16[8,32,256]{2,1,0:T(8,128)(2,1)S(1)} async-done(((bf16[8,32,256]{2,1,0:T(8,128)(2,1)}), bf16[8,32,256]{2,1,0:T(8,128)(2,1)S(1)}, u32[]{:S(2)}, u32[]{:S(2)}) %all-to-all-start.5) | async-done | bytes 131104 | tf_op jit(solution)/shard_map/all_to_all | solution.py:17
  140.9 1.0 fusion.16
  141.9 2.2 convolution_convert_fusion
  144.1 2.5 reshape.155
  146.6 13.5 %all-to-all-start.6 = ((bf16[128,2,2048]{2,1,0:T(2,128)(2,1)}), bf16[128,2,2048]{2,1,0:T(2,128)(2,1)}, u32[]{:S(2)}, u32[]{:S(2)}) async-start(bf16[128,2,2048]{2,1,0:T(2,128)(2,1)} %reshape.155), calls=%async_computation.6 | async-start | bytes 2097152 | tf_op jit(solution)/shard_map/all_to_all | solution.py:17
  160.1 2.5 slice.122
  162.6 2.5 collective-permute-start.3
  165.1 1.3 slice.123
  166.5 4.1 %collective-permute-start.4 = (bf16[96,6144]{1,0:T(8,128)(2,1)S(1)}, bf16[96,6144]{1,0:T(8,128)(2,1)S(1)}, u32[]{:S(2)}, u32[]{:S(2)}) collective-permute-start(bf16[96,6144]{1,0:T(8,128)(2,1)S(1)} %slice.123), channel_id=1, source_target_pairs={{0,3},{1,0},{2,1},{3,2},{4,7},{5,4},{6,5},{7,6},{8,11},{9,8},{10,9... | collective-permute-start | bytes 3538952 | tf_op jit(solution)/shard_map/ppermute | solution.py:336
  170.6 20.1 %all-to-all-done.6 = bf16[128,2,2048]{2,1,0:T(2,128)(2,1)} async-done(((bf16[128,2,2048]{2,1,0:T(2,128)(2,1)}), bf16[128,2,2048]{2,1,0:T(2,128)(2,1)}, u32[]{:S(2)}, u32[]{:S(2)}) %all-to-all-start.6) | async-done | bytes 1048608 | tf_op jit(solution)/shard_map/all_to_all | solution.py:17
  190.7 2.2 reshape.156.rows_ref
  193.0 1.7 collective-permute-done.4.refs_4_
  194.7 1.1 copy-done.3
  195.8 7.9 %experts_forward.1 = bf16[256,2048]{1,0:T(8,128)(2,1)} custom-call(bf16[256,2048]{1,0:T(8,128)(2,1)} %reshape.156.rows_ref, bf16[192,6144]{1,0:T(8,128)(2,1)} %copy-done.1, bf16[192,6144]{1,0:T(8,128)(2,1)} %collective-permute-done.1.refs_1_, bf16[192,6144]{1,0:T(8,128)(2,1)} %collective-permute-done.2.refs_2_, ...), custom_call_target="tpu_custom_call" | custom-call | tf_op jit(solution)/shard_map/experts_forward/pallas_call | solution.py:179
  203.7 2.5 reshape.157
  206.3 15.4 %all-to-all-start.7 = ((bf16[128,2,2048]{2,1,0:T(2,128)(2,1)}), bf16[128,2,2048]{2,1,0:T(2,128)(2,1)S(1)}, u32[]{:S(2)}, u32[]{:S(2)}) async-start(bf16[128,2,2048]{2,1,0:T(2,128)(2,1)} %reshape.157), calls=%async_computation.7 | async-start | bytes 2097152 | tf_op jit(solution)/shard_map/all_to_all | solution.py:17
  221.9 30.7 %all-to-all-done.7 = bf16[128,2,2048]{2,1,0:T(2,128)(2,1)S(1)} async-done(((bf16[128,2,2048]{2,1,0:T(2,128)(2,1)}), bf16[128,2,2048]{2,1,0:T(2,128)(2,1)S(1)}, u32[]{:S(2)}, u32[]{:S(2)}) %all-to-all-start.7) | async-done | bytes 1048608 | tf_op jit(solution)/shard_map/all_to_all | solution.py:17
  (64 shorter events, 5.2 us)
Async XLA Ops:
  0.0 55.3 %copy-start = (bf16[2048,256]{1,0:T(8,128)(2,1)S(1)}, bf16[2048,256]{1,0:T(8,128)(2,1)}, u32[]{:S(2)}) copy-start(bf16[2048,256]{1,0:T(8,128)(2,1)} %param.17) | copy-start | bytes 3145732
  0.0 16.9 %copy-start.7 = (bf16[32,2048]{1,0:T(8,128)(2,1)S(1)}, bf16[32,2048]{1,0:T(8,128)(2,1)}, u32[]{:S(2)}) copy-start(bf16[32,2048]{1,0:T(8,128)(2,1)} %param.15) | copy-start | bytes 393220
  0.0 16.9 %copy-start.6 = (bf16[32,2048]{1,0:T(8,128)(2,1)S(1)}, bf16[32,2048]{1,0:T(8,128)(2,1)}, u32[]{:S(2)}) copy-start(bf16[32,2048]{1,0:T(8,128)(2,1)} %param.16) | copy-start | bytes 393220
  3.0 11.8 %all-to-all-start = ((bf16[4,2,16,2048]{3,2,1,0:T(8,128)(2,1)}), bf16[4,2,16,2048]{3,2,1,0:T(8,128)(2,1)S(1)}, u32[]{:S(2)}, u32[]{:S(2)}) async-start(bf16[4,2,16,2048]{3,2,1,0:T(8,128)(2,1)} %broadcast_in_dim.21), calls=%async_computation | async-start | bytes 1048576 | tf_op jit(solution)/shard_map/all_to_all | solution.py:17
  18.1 9.3 %all-to-all-start.1 = ((bf16[4,160,256]{2,1,0:T(8,128)(2,1)}), bf16[4,160,256]{2,1,0:T(8,128)(2,1)S(1)}, u32[]{:S(2)}, u32[]{:S(2)}) async-start(bf16[4,160,256]{2,1,0:T(8,128)(2,1)} %fusion.9), calls=%async_computation.1 | async-start | bytes 655360 | tf_op jit(solution)/shard_map/all_to_all | solution.py:17
  27.4 19.6 %copy-start.2 = (bf16[4,160,256]{2,1,0:T(8,128)(2,1)}, bf16[4,160,256]{2,1,0:T(8,128)(2,1)S(1)}, u32[]{:S(2)}) copy-start(bf16[4,160,256]{2,1,0:T(8,128)(2,1)S(1)} %all-to-all-done.1.swapped_ref) | copy-start | bytes 983044
  29.0 42.6 %all-to-all-start.2 = ((bf16[64,32,256]{2,1,0:T(8,128)(2,1)}), bf16[64,32,256]{2,1,0:T(8,128)(2,1)}, u32[]{:S(2)}, u32[]{:S(2)}) async-start(bf16[64,32,256]{2,1,0:T(8,128)(2,1)} %broadcast_in_dim.23), calls=%async_computation.2 | async-start | bytes 2097152 | tf_op jit(solution)/shard_map/all_to_all | solution.py:17
  47.0 15.2 %copy-start.4 = (s32[1,16,8]{1,2,0:T(8,128)S(1)}, s32[1,16,8]{1,2,0:T(8,128)}, u32[]{:S(2)}) copy-start(s32[1,16,8]{1,2,0:T(8,128)} %param.19) | copy-start | bytes 1540
  48.8 61.1 %copy-start.1 = (bf16[192,6144]{1,0:T(8,128)(2,1)}, bf16[192,6144]{1,0:T(8,128)(2,1)S(1)}, u32[]{:S(2)}) copy-start(bf16[192,6144]{1,0:T(8,128)(2,1)S(1)} %pad_maximum_fusion.refs_0_) | copy-start | bytes 7077892
  48.8 111.3 %collective-permute-start.1 = (bf16[192,6144]{1,0:T(8,128)(2,1)S(1)}, bf16[192,6144]{1,0:T(8,128)(2,1)}, u32[]{:S(2)}, u32[]{:S(2)}) collective-permute-start(bf16[192,6144]{1,0:T(8,128)(2,1)S(1)} %pad_maximum_fusion.refs_0_), channel_id=1, source_target_pairs={{0,1},{1,2},{2,3},{3,0},{4,5},{5,6},{6,7},{7,4},{8,9},{9,10},{10,1... | collective-permute-start | bytes 7077896 | tf_op jit(solution)/shard_map/ppermute | solution.py:221
  51.0 114.1 %collective-permute-start.2 = (bf16[192,6144]{1,0:T(8,128)(2,1)S(1)}, bf16[192,6144]{1,0:T(8,128)(2,1)}, u32[]{:S(2)}, u32[]{:S(2)}) collective-permute-start(bf16[192,6144]{1,0:T(8,128)(2,1)S(1)} %pad_maximum_fusion.refs_0_), channel_id=1, source_target_pairs={{0,3},{1,0},{2,1},{3,2},{4,7},{5,4},{6,5},{7,6},{8,11},{9,8},{10,9... | collective-permute-start | bytes 7077896 | tf_op jit(solution)/shard_map/ppermute | solution.py:222
  56.2 67.2 %collective-permute-start = (bf16[1024,256]{1,0:T(8,128)(2,1)}, bf16[1024,256]{1,0:T(8,128)(2,1)}, u32[]{:S(2)}, u32[]{:S(2)}) collective-permute-start(bf16[1024,256]{1,0:T(8,128)(2,1)} %constant_dynamic-slice_fusion), channel_id=1, source_target_pairs={{0,4},{4,0},{1,5},{5,1},{2,6},{6,2},{3,7},{7,3},{8,12},{12,8},{9,1... | collective-permute-start | bytes 1572872 | tf_op jit(solution)/shard_map/ppermute | solution.py:272
  76.0 28.4 %all-to-all-start.3 = ((bf16[4,32,1152]{2,1,0:T(8,128)(2,1)}), bf16[4,32,1152]{2,1,0:T(8,128)(2,1)}, u32[]{:S(2)}, u32[]{:S(2)}) async-start(bf16[4,32,1152]{2,1,0:T(8,128)(2,1)} %attend_part.1), calls=%async_computation.3 | async-start | bytes 589824 | tf_op jit(solution)/shard_map/all_to_all | solution.py:17
  111.7 10.5 %all-to-all-start.4 = ((bf16[4,32,1024]{2,1,0:T(8,128)(2,1)}), bf16[4,32,1024]{2,1,0:T(8,128)(2,1)}, u32[]{:S(2)}, u32[]{:S(2)}) async-start(bf16[4,32,1024]{2,1,0:T(8,128)(2,1)} %broadcast_in_dim.24), calls=%async_computation.4 | async-start | bytes 524288 | tf_op jit(solution)/shard_map/all_to_all | solution.py:17
  125.4 15.4 %all-to-all-start.5 = ((bf16[8,32,256]{2,1,0:T(8,128)(2,1)}), bf16[8,32,256]{2,1,0:T(8,128)(2,1)S(1)}, u32[]{:S(2)}, u32[]{:S(2)}) async-start(bf16[8,32,256]{2,1,0:T(8,128)(2,1)} %bitcast.77), calls=%async_computation.5 | async-start | bytes 262144 | tf_op jit(solution)/shard_map/all_to_all | solution.py:17
  146.6 44.1 %all-to-all-start.6 = ((bf16[128,2,2048]{2,1,0:T(2,128)(2,1)}), bf16[128,2,2048]{2,1,0:T(2,128)(2,1)}, u32[]{:S(2)}, u32[]{:S(2)}) async-start(bf16[128,2,2048]{2,1,0:T(2,128)(2,1)} %reshape.155), calls=%async_computation.6 | async-start | bytes 2097152 | tf_op jit(solution)/shard_map/all_to_all | solution.py:17
  162.6 30.4 %collective-permute-start.3 = (bf16[96,6144]{1,0:T(8,128)(2,1)}, bf16[96,6144]{1,0:T(8,128)(2,1)}, u32[]{:S(2)}, u32[]{:S(2)}) collective-permute-start(bf16[96,6144]{1,0:T(8,128)(2,1)} %slice.122), channel_id=1, source_target_pairs={{0,1},{1,2},{2,3},{3,0},{4,5},{5,6},{6,7},{7,4},{8,9},{9,10},{10,1... | collective-permute-start | bytes 3538952 | tf_op jit(solution)/shard_map/ppermute | solution.py:335
  166.5 28.2 %collective-permute-start.4 = (bf16[96,6144]{1,0:T(8,128)(2,1)S(1)}, bf16[96,6144]{1,0:T(8,128)(2,1)S(1)}, u32[]{:S(2)}, u32[]{:S(2)}) collective-permute-start(bf16[96,6144]{1,0:T(8,128)(2,1)S(1)} %slice.123), channel_id=1, source_target_pairs={{0,3},{1,0},{2,1},{3,2},{4,7},{5,4},{6,5},{7,6},{8,11},{9,8},{10,9... | collective-permute-start | bytes 3538952 | tf_op jit(solution)/shard_map/ppermute | solution.py:336
  194.7 1.1 copy-start.3
  203.7 18.0 %copy-start.5 = (f32[1,16,8]{1,2,0:T(8,128)S(1)}, f32[1,16,8]{1,2,0:T(8,128)}, u32[]{:S(2)}) copy-start(f32[1,16,8]{1,2,0:T(8,128)} %param.20) | copy-start | bytes 1540
  206.3 46.4 %all-to-all-start.7 = ((bf16[128,2,2048]{2,1,0:T(2,128)(2,1)}), bf16[128,2,2048]{2,1,0:T(2,128)(2,1)S(1)}, u32[]{:S(2)}, u32[]{:S(2)}) async-start(bf16[128,2,2048]{2,1,0:T(2,128)(2,1)} %reshape.157), calls=%async_computation.7 | async-start | bytes 2097152 | tf_op jit(solution)/shard_map/all_to_all | solution.py:17

commit v5 on v4

--- a/solution.py
+++ b/solution.py
@@ -59,6 +59,7 @@
 STATS = 6
 LOG2_E = 1.4426950408889634
 GROUP_ROWS = 256
+WHOLE_VMEM = 66_500_000
 
 
 def attend_part(where, swapped, spread, seqs, own_len, local_heads, head_dim):
@@ -129,6 +130,7 @@
         out_shape=jax.ShapeDtypeStruct((pairs, own_rows, lanes + head_dim), BF16),
         in_specs=[pl.BlockSpec(memory_space=pltpu.SMEM), vmem, vmem],
         out_specs=vmem,
+        compiler_params=pltpu.CompilerParams(vmem_limit_bytes=WHOLE_VMEM),
         name="attend_part",
     )(where, swapped, spread)
 
@@ -179,13 +181,68 @@
     return pl.pallas_call(
         kernel,
         out_shape=jax.ShapeDtypeStruct((slots, width), BF16),
-        in_specs=[vmem] + [pl.BlockSpec(memory_space=pl.ANY)] * len(pieces),
+        in_specs=[vmem] + [pl.BlockSpec(memory_space=pltpu.HBM)] * len(pieces),
         out_specs=vmem,
         scratch_shapes=[pltpu.VMEM((slots, width), F32)]
         + [pltpu.VMEM((hidden_units, width), BF16)] * 3
         + [pltpu.SemaphoreType.DMA((3 * len(pieces),))],
         name="experts_forward",
     )(incoming, *pieces)
+
+
+def side_by_side(arrays, after):
+    count, width = arrays[0].shape
+
+    def kernel(*refs):
+        out_ref, sems = refs[len(arrays) + 1 :]
+        copies = [
+            pltpu.make_async_copy(ref, out_ref.at[:, pl.ds(n * width, width)], sems.at[n])
+            for n, ref in enumerate(refs[: len(arrays)])
+        ]
+        for copy in copies:
+            copy.start()
+        for copy in copies:
+            copy.wait()
+
+    hbm = pl.BlockSpec(memory_space=pltpu.HBM)
+    return pl.pallas_call(
+        kernel,
+        out_shape=jax.ShapeDtypeStruct((count, width * len(arrays)), arrays[0].dtype),
+        in_specs=[hbm] * (len(arrays) + 1),
+        out_specs=hbm,
+        scratch_shapes=[pltpu.SemaphoreType.DMA((len(arrays),))],
+        name="side_by_side",
+    )(*arrays, after)
+
+
+def halves(low_source, high_source):
+    count, width = low_source.shape
+    half = count // 2
+
+    def kernel(low_ref, high_ref, low_out, high_out, sems):
+        copies = [
+            pltpu.make_async_copy(low_ref.at[pl.ds(0, half), :], low_out, sems.at[0]),
+            pltpu.make_async_copy(
+                high_ref.at[pl.ds(half, count - half), :], high_out, sems.at[1]
+            ),
+        ]
+        for copy in copies:
+            copy.start()
+        for copy in copies:
+            copy.wait()
+
+    hbm = pl.BlockSpec(memory_space=pltpu.HBM)
+    return pl.pallas_call(
+        kernel,
+        out_shape=(
+            jax.ShapeDtypeStruct((half, width), low_source.dtype),
+            jax.ShapeDtypeStruct((count - half, width), high_source.dtype),
+        ),
+        in_specs=[hbm, hbm],
+        out_specs=(hbm, hbm),
+        scratch_shapes=[pltpu.SemaphoreType.DMA((2,))],
+        name="halves",
+    )(low_source, high_source)
 
 
 def body(
@@ -215,12 +272,6 @@
     local_heads = q_cols // head_dim
     group = local_heads * pairs
 
-    up_ring = [(i, (i + 1) % pairs) for i in range(pairs)]
-    down_ring = [(i, (i - 1) % pairs) for i in range(pairs)]
-    joined = jnp.concatenate([gate_weight[0], up_weight[0], down_weight[0]], axis=1)
-    from_below = lax.ppermute(joined, "pair", up_ring)
-    from_above = lax.ppermute(joined, "pair", down_ring)
-
     normed = normalize(tokens_in, attn_gain)
     token_send = for_each(normed, pairs)
     block_rows = exchange(token_send, "pair").reshape(rows, width)
@@ -252,6 +303,12 @@
         ],
         axis=1,
     )
+    up_ring = [(i, (i + 1) % pairs) for i in range(pairs)]
+    down_ring = [(i, (i - 1) % pairs) for i in range(pairs)]
+    joined = side_by_side([gate_weight[0], up_weight[0], down_weight[0]], swap_send)
+    from_below = lax.ppermute(joined, "pair", up_ring)
+    from_above = lax.ppermute(joined, "pair", down_ring)
+
     swapped = exchange(swap_send, "pair")
     own_pos = (own_start + jnp.zeros((seqs, 1), jnp.int32) + places).reshape(own_rows)
     key_own = jnp.concatenate([swapped[p, rows:, :part_cols] for p in range(pairs)], axis=1)
@@ -296,7 +353,8 @@
     attended = jnp.sum(scale[..., None] * part_mixed.astype(F32), axis=0).astype(BF16)
     attended = attended.reshape(own_rows, group * head_dim)
 
-    gathered_heads = exchange(for_each(attended, pairs), "pair").reshape(rows, group_cols)
+    heads_send = for_each(attended, pairs)
+    gathered_heads = exchange(heads_send, "pair").reshape(rows, group_cols)
     projected = jnp.stack(
         [dot(gathered_heads, out_mine, 1, 0), dot(gathered_heads, out_other, 1, 0)]
     ).astype(BF16)
@@ -306,9 +364,8 @@
         .transpose(2, 1, 0, 3, 4)
         .reshape(seqs * pairs, 2 * own_len, out_cols)
     )
-    owned = exchange(projected, ("head", "pair")).reshape(
-        heads, pairs, 2, own_len, out_cols
-    ).astype(F32)
+    owned = exchange(projected, ("head", "pair"))
+    owned = owned.reshape(heads, pairs, 2, own_len, out_cols).astype(F32)
     owned = (owned[:, :, 0] + owned[::-1, :, 1]).reshape(heads * pairs, own_len, out_cols)
     owned = jnp.moveaxis(owned, 0, 1).reshape(own_len, width)
     own_tokens = lax.dynamic_index_in_dim(tokens_in, lax.axis_index("head"), 0, keepdims=False)
@@ -331,9 +388,9 @@
     incoming = exchange(outgoing, ("ctx", "head"))
     incoming = incoming.reshape(slots, width)
 
-    half = joined.shape[0] // 2
-    far_low = lax.ppermute(from_below[:half], "pair", up_ring)
-    far_high = lax.ppermute(from_above[half:], "pair", down_ring)
+    low_half, high_half = halves(from_below, from_above)
+    far_low = lax.ppermute(low_half, "pair", up_ring)
+    far_high = lax.ppermute(high_half, "pair", down_ring)
     expert_out = experts_forward(incoming, [joined, from_below, from_above, far_low, far_high])
     returned = exchange(expert_out.reshape(experts, capacity, width), ("ctx", "head"))
     returned = returned.reshape(slots, width)

time: 256 us -> 404 us (1.58)
  Pallas kernels: 12.3 us -> 157 us
  waiting for transfers between devices: 108 us -> 130 us
  local copies, waits for them, and re-layouts: 21.9 us -> 14.4 us
  other arithmetic: 10.5 us -> 6.46 us
    pallas_call x0 -> x2, Pallas kernels: none -> 145 us  [the longest x1 72.6 us: side_by_side(): pl.pallas_call(kernel, out_shape=jax.ShapeDtypeStruct((count, width * len...]
    ppermute x2, waiting for transfers between devices: 1.7 us -> 23.1 us  [the longest x1 22 us: body(): far_low = lax.ppermute(low_half, 'pair', up_ring)]
  transfers between devices with their start and end apart: 13 -> 13, of which waited for: 9 -> 8; matrix products, arithmetic and copies ran while one was open for 10% -> 3% of each run, Pallas kernels for 2% -> 37%
where the time goes in v5:
time: 404 us; the launch traced here: 402 us
  Pallas kernels  157 us (39%)
  waiting for transfers between devices  130 us (32%)
  starting transfers between devices  89.6 us (22%)
  local copies, waits for them, and re-layouts  14.4 us (4%)
  other arithmetic  6.46 us (2%)
  matrix products  4.13 us (1%)
    all_to_all x8, waiting for transfers between devices, exchange(): return lax.all_to_all(tiles, axis, 0, 0, tiled=True)  107 us
    pallas_call x1, Pallas kernels, side_by_side(): pl.pallas_call(kernel, out_shape=jax.ShapeDtypeStruct((count, width * len...  72.6 us
    pallas_call x1, Pallas kernels, halves(): pl.pallas_call(kernel, out_shape=(jax.ShapeDtypeStruct((half, width), low...  72.6 us
    all_to_all x8, starting transfers between devices, exchange(): return lax.all_to_all(tiles, axis, 0, 0, tiled=True)  71 us
    ppermute x1, waiting for transfers between devices, body(): far_low = lax.ppermute(low_half, 'pair', up_ring)  22 us
  transfers between devices with their start and end apart: 13, of which 8 were waited for; matrix products, arithmetic and copies ran while one was open for 3% of the time, Pallas kernels for 37%

profile of v5, /device:TPU:1, one launch (start us, length us, event | category | flops | bytes accessed | tf_op | source)
XLA Modules:
  0.0 402.2 jit_solution(7851196970427954454)
XLA Ops:
  0.0 1.1 fusion.10
  1.1 1.0 fusion.12
  2.2 0.9 broadcast_in_dim.21
  3.0 4.8 %all-to-all-start = ((bf16[4,2,16,2048]{3,2,1,0:T(8,128)(2,1)}), bf16[4,2,16,2048]{3,2,1,0:T(8,128)(2,1)S(1)}, u32[]{:S(2)}, u32[]{:S(2)}) async-start(bf16[4,2,16,2048]{3,2,1,0:T(8,128)(2,1)} %broadcast_in_dim.21), calls=%async_computation | async-start | bytes 1048576 | tf_op jit(solution)/shard_map/all_to_all | solution.py:17
  8.0 6.8 %all-to-all-done = bf16[4,2,16,2048]{3,2,1,0:T(8,128)(2,1)S(1)} async-done(((bf16[4,2,16,2048]{3,2,1,0:T(8,128)(2,1)}), bf16[4,2,16,2048]{3,2,1,0:T(8,128)(2,1)S(1)}, u32[]{:S(2)}, u32[]{:S(2)}) %all-to-all-start) | async-done | bytes 524320 | tf_op jit(solution)/shard_map/all_to_all | solution.py:17
  14.8 0.5 fusion.61
  15.7 0.3 convolution_convert_fusion.3
  16.2 0.8 fusion.9.refs_3_
  16.9 3.6 all-to-all-start.1
  20.6 5.7 %all-to-all-done.1.swapped_ref = bf16[4,160,256]{2,1,0:T(8,128)(2,1)S(1)} async-done(((bf16[4,160,256]{2,1,0:T(8,128)(2,1)}), bf16[4,160,256]{2,1,0:T(8,128)(2,1)S(1)}, u32[]{:S(2)}, u32[]{:S(2)}) %all-to-all-start.1) | async-done | bytes 327712 | tf_op jit(solution)/shard_map/all_to_all | solution.py:17
  26.8 1.1 broadcast_in_dim.23
  27.9 18.0 %all-to-all-start.2 = ((bf16[64,32,256]{2,1,0:T(8,128)(2,1)}), bf16[64,32,256]{2,1,0:T(8,128)(2,1)}, u32[]{:S(2)}, u32[]{:S(2)}) async-start(bf16[64,32,256]{2,1,0:T(8,128)(2,1)} %broadcast_in_dim.23), calls=%async_computation.2 | async-start | bytes 2097152 | tf_op jit(solution)/shard_map/all_to_all | solution.py:17
  45.9 0.8 constant_dynamic-slice_fusion
  46.7 5.4 %collective-permute-start = (bf16[1024,256]{1,0:T(8,128)(2,1)}, bf16[1024,256]{1,0:T(8,128)(2,1)}, u32[]{:S(2)}, u32[]{:S(2)}) collective-permute-start(bf16[1024,256]{1,0:T(8,128)(2,1)} %constant_dynamic-slice_fusion), channel_id=1, source_target_pairs={{0,4},{4,0},{1,5},{5,1},{2,6},{6,2},{3,7},{7,3},{8,12},{12,8},{9,1... | collective-permute-start | bytes 1572872 | tf_op jit(solution)/shard_map/ppermute | solution.py:329
  52.3 0.6 pad_add_fusion.where_ref
  53.0 17.6 %all-to-all-done.2.spread_ref = bf16[64,32,256]{2,1,0:T(8,128)(2,1)} async-done(((bf16[64,32,256]{2,1,0:T(8,128)(2,1)}), bf16[64,32,256]{2,1,0:T(8,128)(2,1)}, u32[]{:S(2)}, u32[]{:S(2)}) %all-to-all-start.2) | async-done | bytes 1048608 | tf_op jit(solution)/shard_map/all_to_all | solution.py:17
  70.6 4.3 %attend_part.1 = bf16[4,32,1152]{2,1,0:T(8,128)(2,1)} custom-call(s32[2]{0:T(128)} %pad_add_fusion.where_ref, bf16[4,160,256]{2,1,0:T(8,128)(2,1)} %copy-done.1, bf16[64,32,256]{2,1,0:T(8,128)(2,1)} %all-to-all-done.2.spread_ref), custom_call_target="tpu_custom_call" | custom-call | tf_op jit(solution)/shard_map/attend_part/pallas_call | solution.py:128
  74.9 3.5 all-to-all-start.3
  78.7 72.6 %side_by_side.1.refs_0_ = bf16[192,6144]{1,0:T(8,128)(2,1)} custom-call(bf16[192,2048]{1,0:T(8,128)(2,1)} %bitcast.75, bf16[192,2048]{1,0:T(8,128)(2,1)} %bitcast.76, bf16[192,2048]{1,0:T(8,128)(2,1)} %bitcast.77, bf16[4,160,256]{2,1,0:T(8,128)(2,1)} %fusion.9.refs_3_), custom_call_target="tpu_custom_call" | custom-call | tf_op jit(solution)/shard_map/side_by_side/pallas_call | solution.py:208
  151.3 3.3 collective-permute-start.1
  154.6 3.2 collective-permute-start.2
  158.1 0.4 copy-done.2
  158.8 1.0 multiply_reduce_fusion
  159.9 0.7 broadcast_in_dim.24
  160.6 3.5 all-to-all-start.4
  164.2 40.6 %all-to-all-done.4 = bf16[4,32,1024]{2,1,0:T(8,128)(2,1)S(1)} async-done(((bf16[4,32,1024]{2,1,0:T(8,128)(2,1)}), bf16[4,32,1024]{2,1,0:T(8,128)(2,1)S(1)}, u32[]{:S(2)}, u32[]{:S(2)}) %all-to-all-start.4) | async-done | bytes 262176 | tf_op jit(solution)/shard_map/all_to_all | solution.py:17
  204.8 1.3 fusion.1
  206.1 1.3 fusion.2
  207.4 0.7 copy.52
  208.1 12.4 %all-to-all-start.5 = ((bf16[8,32,256]{2,1,0:T(8,128)(2,1)}), bf16[8,32,256]{2,1,0:T(8,128)(2,1)S(1)}, u32[]{:S(2)}, u32[]{:S(2)}) async-start(bf16[8,32,256]{2,1,0:T(8,128)(2,1)} %bitcast.22), calls=%async_computation.5 | async-start | bytes 262144 | tf_op jit(solution)/shard_map/all_to_all | solution.py:17
  220.6 5.1 %all-to-all-done.5 = bf16[8,32,256]{2,1,0:T(8,128)(2,1)S(1)} async-done(((bf16[8,32,256]{2,1,0:T(8,128)(2,1)}), bf16[8,32,256]{2,1,0:T(8,128)(2,1)S(1)}, u32[]{:S(2)}, u32[]{:S(2)}) %all-to-all-start.5) | async-done | bytes 131104 | tf_op jit(solution)/shard_map/all_to_all | solution.py:17
  226.0 0.5 convolution_convert_fusion
  226.4 1.5 reshape.155
  228.0 9.9 %all-to-all-start.6 = ((bf16[128,2,2048]{2,1,0:T(2,128)(2,1)}), bf16[128,2,2048]{2,1,0:T(2,128)(2,1)S(1)}, u32[]{:S(2)}, u32[]{:S(2)}) async-start(bf16[128,2,2048]{2,1,0:T(2,128)(2,1)} %reshape.155), calls=%async_computation.6 | async-start | bytes 2097152 | tf_op jit(solution)/shard_map/all_to_all | solution.py:17
  237.9 1.4 copy-done
  239.3 72.6 %halves.1 = (bf16[96,6144]{1,0:T(8,128)(2,1)}, bf16[96,6144]{1,0:T(8,128)(2,1)}) custom-call(bf16[192,6144]{1,0:T(8,128)(2,1)} %copy-done, bf16[192,6144]{1,0:T(8,128)(2,1)} %collective-permute-done.2.high_ref.refs_2_), custom_call_target="tpu_custom_call" | custom-call | tf_op jit(solution)/shard_map/halves/pallas_call | solution.py:235
  311.9 2.5 collective-permute-start.3
  314.4 4.1 %collective-permute-start.4 = (bf16[96,6144]{1,0:T(8,128)(2,1)}, bf16[96,6144]{1,0:T(8,128)(2,1)S(1)}, u32[]{:S(2)}, u32[]{:S(2)}) collective-permute-start(bf16[96,6144]{1,0:T(8,128)(2,1)} %get-tuple-element.8), channel_id=1, source_target_pairs={{0,3},{1,0},{2,1},{3,2},{4,7},{5,4},{6,5},{7,6},{8,11},{9,8},{10,9... | collective-permute-start | bytes 3538952 | tf_op jit(solution)/shard_map/ppermute | solution.py:393
  318.6 1.2 reshape.156.rows_ref
  319.8 22.0 %collective-permute-done.3.refs_3_ = bf16[96,6144]{1,0:T(8,128)(2,1)S(1)} collective-permute-done((bf16[96,6144]{1,0:T(8,128)(2,1)}, bf16[96,6144]{1,0:T(8,128)(2,1)S(1)}, u32[]{:S(2)}, u32[]{:S(2)}) %collective-permute-start.3) | collective-permute-done | bytes 1179680 | tf_op jit(solution)/shard_map/ppermute | solution.py:392
  341.8 1.1 collective-permute-done.4.refs_4_
  342.9 1.1 copy-done.4
  344.0 7.9 %experts_forward.1 = bf16[256,2048]{1,0:T(8,128)(2,1)} custom-call(bf16[256,2048]{1,0:T(8,128)(2,1)} %reshape.156.rows_ref, bf16[192,6144]{1,0:T(8,128)(2,1)} %side_by_side.1.refs_0_, bf16[192,6144]{1,0:T(8,128)(2,1)} %copy-done, bf16[192,6144]{1,0:T(8,128)(2,1)} %collective-permute-done.2.high_ref.refs_2_, bf16[96,6144]{1,0:T(8,128)(2,1)} %copy-done.3, ...), custom_call_target="tpu_custom_call" | custom-call | tf_op jit(solution)/shard_map/experts_forward/pallas_call | solution.py:181
  352.0 2.5 reshape.157
  354.5 15.4 %all-to-all-start.7 = ((bf16[128,2,2048]{2,1,0:T(2,128)(2,1)}), bf16[128,2,2048]{2,1,0:T(2,128)(2,1)S(1)}, u32[]{:S(2)}, u32[]{:S(2)}) async-start(bf16[128,2,2048]{2,1,0:T(2,128)(2,1)} %reshape.157), calls=%async_computation.7 | async-start | bytes 2097152 | tf_op jit(solution)/shard_map/all_to_all | solution.py:17
  370.1 30.7 %all-to-all-done.7 = bf16[128,2,2048]{2,1,0:T(2,128)(2,1)S(1)} async-done(((bf16[128,2,2048]{2,1,0:T(2,128)(2,1)}), bf16[128,2,2048]{2,1,0:T(2,128)(2,1)S(1)}, u32[]{:S(2)}, u32[]{:S(2)}) %all-to-all-start.7) | async-done | bytes 1048608 | tf_op jit(solution)/shard_map/all_to_all | solution.py:17
  400.8 0.4 reshape.158
  401.6 0.7 fusion.23
  (73 shorter events, 3.1 us)
Async XLA Ops:
  0.0 14.8 %copy-start.6 = (bf16[2048,256]{1,0:T(8,128)(2,1)S(1)}, bf16[2048,256]{1,0:T(8,128)(2,1)}, u32[]{:S(2)}) copy-start(bf16[2048,256]{1,0:T(8,128)(2,1)} %param.14) | copy-start | bytes 3145732
  1.1 14.6 %copy-start.11 = (bf16[32,2048]{1,0:T(8,128)(2,1)S(1)}, bf16[32,2048]{1,0:T(8,128)(2,1)}, u32[]{:S(2)}) copy-start(bf16[32,2048]{1,0:T(8,128)(2,1)} %param.16) | copy-start | bytes 393220
  1.1 14.6 %copy-start.12 = (bf16[32,2048]{1,0:T(8,128)(2,1)S(1)}, bf16[32,2048]{1,0:T(8,128)(2,1)}, u32[]{:S(2)}) copy-start(bf16[32,2048]{1,0:T(8,128)(2,1)} %param.15) | copy-start | bytes 393220
  3.0 11.8 %all-to-all-start = ((bf16[4,2,16,2048]{3,2,1,0:T(8,128)(2,1)}), bf16[4,2,16,2048]{3,2,1,0:T(8,128)(2,1)S(1)}, u32[]{:S(2)}, u32[]{:S(2)}) async-start(bf16[4,2,16,2048]{3,2,1,0:T(8,128)(2,1)} %broadcast_in_dim.21), calls=%async_computation | async-start | bytes 1048576 | tf_op jit(solution)/shard_map/all_to_all | solution.py:17
  16.9 29.0 %copy-start.5 = (bf16[2048,256]{1,0:T(8,128)(2,1)S(1)}, bf16[2048,256]{1,0:T(8,128)(2,1)}, u32[]{:S(2)}) copy-start(bf16[2048,256]{1,0:T(8,128)(2,1)} %param.17) | copy-start | bytes 3145732
  16.9 9.4 %all-to-all-start.1 = ((bf16[4,160,256]{2,1,0:T(8,128)(2,1)}), bf16[4,160,256]{2,1,0:T(8,128)(2,1)S(1)}, u32[]{:S(2)}, u32[]{:S(2)}) async-start(bf16[4,160,256]{2,1,0:T(8,128)(2,1)} %fusion.9.refs_3_), calls=%async_computation.1 | async-start | bytes 655360 | tf_op jit(solution)/shard_map/all_to_all | solution.py:17
  26.4 20.4 %copy-start.1 = (bf16[4,160,256]{2,1,0:T(8,128)(2,1)}, bf16[4,160,256]{2,1,0:T(8,128)(2,1)S(1)}, u32[]{:S(2)}) copy-start(bf16[4,160,256]{2,1,0:T(8,128)(2,1)S(1)} %all-to-all-done.1.swapped_ref) | copy-start | bytes 983044
  26.8 25.4 %copy-start.8 = (s32[1,16,8]{1,2,0:T(8,128)S(1)}, s32[1,16,8]{1,2,0:T(8,128)}, u32[]{:S(2)}) copy-start(s32[1,16,8]{1,2,0:T(8,128)} %param.19) | copy-start | bytes 1540
  27.9 42.7 %all-to-all-start.2 = ((bf16[64,32,256]{2,1,0:T(8,128)(2,1)}), bf16[64,32,256]{2,1,0:T(8,128)(2,1)}, u32[]{:S(2)}, u32[]{:S(2)}) async-start(bf16[64,32,256]{2,1,0:T(8,128)(2,1)} %broadcast_in_dim.23), calls=%async_computation.2 | async-start | bytes 2097152 | tf_op jit(solution)/shard_map/all_to_all | solution.py:17
  46.7 159.4 %collective-permute-start = (bf16[1024,256]{1,0:T(8,128)(2,1)}, bf16[1024,256]{1,0:T(8,128)(2,1)}, u32[]{:S(2)}, u32[]{:S(2)}) collective-permute-start(bf16[1024,256]{1,0:T(8,128)(2,1)} %constant_dynamic-slice_fusion), channel_id=1, source_target_pairs={{0,4},{4,0},{1,5},{5,1},{2,6},{6,2},{3,7},{7,3},{8,12},{12,8},{9,1... | collective-permute-start | bytes 1572872 | tf_op jit(solution)/shard_map/ppermute | solution.py:329
  74.9 82.9 %all-to-all-start.3 = ((bf16[4,32,1152]{2,1,0:T(8,128)(2,1)}), bf16[4,32,1152]{2,1,0:T(8,128)(2,1)S(1)}, u32[]{:S(2)}, u32[]{:S(2)}) async-start(bf16[4,32,1152]{2,1,0:T(8,128)(2,1)} %attend_part.1), calls=%async_computation.3 | async-start | bytes 589824 | tf_op jit(solution)/shard_map/all_to_all | solution.py:17
  151.3 86.6 %collective-permute-start.1 = (bf16[192,6144]{1,0:T(8,128)(2,1)}, bf16[192,6144]{1,0:T(8,128)(2,1)S(1)}, u32[]{:S(2)}, u32[]{:S(2)}) collective-permute-start(bf16[192,6144]{1,0:T(8,128)(2,1)} %side_by_side.1.refs_0_), channel_id=1, source_target_pairs={{0,1},{1,2},{2,3},{3,0},{4,5},{5,6},{6,7},{7,4},{8,9},{9,10},{10,1... | collective-permute-start | bytes 7077896 | tf_op jit(solution)/shard_map/ppermute | solution.py:309
  154.6 83.2 %collective-permute-start.2 = (bf16[192,6144]{1,0:T(8,128)(2,1)}, bf16[192,6144]{1,0:T(8,128)(2,1)}, u32[]{:S(2)}, u32[]{:S(2)}) collective-permute-start(bf16[192,6144]{1,0:T(8,128)(2,1)} %side_by_side.1.refs_0_), channel_id=1, source_target_pairs={{0,3},{1,0},{2,1},{3,2},{4,7},{5,4},{6,5},{7,6},{8,11},{9,8},{10,9... | collective-permute-start | bytes 7077896 | tf_op jit(solution)/shard_map/ppermute | solution.py:310
  157.8 0.7 copy-start.2
  160.6 65.2 %copy-start.7 = (bf16[2,16,2048]{2,1,0:T(8,128)(2,1)S(1)}, bf16[2,16,2048]{2,1,0:T(8,128)(2,1)}, u32[]{:S(2)}) copy-start(bf16[2,16,2048]{2,1,0:T(8,128)(2,1)} %param.12) | copy-start | bytes 393220
  160.6 44.3 %all-to-all-start.4 = ((bf16[4,32,1024]{2,1,0:T(8,128)(2,1)}), bf16[4,32,1024]{2,1,0:T(8,128)(2,1)S(1)}, u32[]{:S(2)}, u32[]{:S(2)}) async-start(bf16[4,32,1024]{2,1,0:T(8,128)(2,1)} %broadcast_in_dim.24), calls=%async_computation.4 | async-start | bytes 524288 | tf_op jit(solution)/shard_map/all_to_all | solution.py:17
  164.1 61.8 %copy-start.9 = (f32[2048]{0:T(1024)S(1)}, f32[2048]{0:T(1024)}, u32[]{:S(2)}) copy-start(f32[2048]{0:T(1024)} %param.18) | copy-start | bytes 24580
  208.1 17.6 %all-to-all-start.5 = ((bf16[8,32,256]{2,1,0:T(8,128)(2,1)}), bf16[8,32,256]{2,1,0:T(8,128)(2,1)S(1)}, u32[]{:S(2)}, u32[]{:S(2)}) async-start(bf16[8,32,256]{2,1,0:T(8,128)(2,1)} %bitcast.22), calls=%async_computation.5 | async-start | bytes 262144 | tf_op jit(solution)/shard_map/all_to_all | solution.py:17
  228.0 90.6 %all-to-all-start.6 = ((bf16[128,2,2048]{2,1,0:T(2,128)(2,1)}), bf16[128,2,2048]{2,1,0:T(2,128)(2,1)S(1)}, u32[]{:S(2)}, u32[]{:S(2)}) async-start(bf16[128,2,2048]{2,1,0:T(2,128)(2,1)} %reshape.155), calls=%async_computation.6 | async-start | bytes 2097152 | tf_op jit(solution)/shard_map/all_to_all | solution.py:17
  237.9 1.4 copy-start
  311.9 29.9 %collective-permute-start.3 = (bf16[96,6144]{1,0:T(8,128)(2,1)}, bf16[96,6144]{1,0:T(8,128)(2,1)S(1)}, u32[]{:S(2)}, u32[]{:S(2)}) collective-permute-start(bf16[96,6144]{1,0:T(8,128)(2,1)} %get-tuple-element.7), channel_id=1, source_target_pairs={{0,1},{1,2},{2,3},{3,0},{4,5},{5,6},{6,7},{7,4},{8,9},{9,10},{10,1... | collective-permute-start | bytes 3538952 | tf_op jit(solution)/shard_map/ppermute | solution.py:392
  314.4 28.5 %collective-permute-start.4 = (bf16[96,6144]{1,0:T(8,128)(2,1)}, bf16[96,6144]{1,0:T(8,128)(2,1)S(1)}, u32[]{:S(2)}, u32[]{:S(2)}) collective-permute-start(bf16[96,6144]{1,0:T(8,128)(2,1)} %get-tuple-element.8), channel_id=1, source_target_pairs={{0,3},{1,0},{2,1},{3,2},{4,7},{5,4},{6,5},{7,6},{8,11},{9,8},{10,9... | collective-permute-start | bytes 3538952 | tf_op jit(solution)/shard_map/ppermute | solution.py:393
  341.8 1.1 copy-start.3
  342.9 1.1 copy-start.4
  352.0 17.9 %copy-start.10 = (f32[1,16,8]{1,2,0:T(8,128)S(1)}, f32[1,16,8]{1,2,0:T(8,128)}, u32[]{:S(2)}) copy-start(f32[1,16,8]{1,2,0:T(8,128)} %param.20) | copy-start | bytes 1540
  354.5 46.3 %all-to-all-start.7 = ((bf16[128,2,2048]{2,1,0:T(2,128)(2,1)}), bf16[128,2,2048]{2,1,0:T(2,128)(2,1)S(1)}, u32[]{:S(2)}, u32[]{:S(2)}) async-start(bf16[128,2,2048]{2,1,0:T(2,128)(2,1)} %reshape.157), calls=%async_computation.7 | async-start | bytes 2097152 | tf_op jit(solution)/shard_map/all_to_all | solution.py:17

commit v6 on v4

--- a/solution.py
+++ b/solution.py
@@ -59,6 +59,7 @@
 STATS = 6
 LOG2_E = 1.4426950408889634
 GROUP_ROWS = 256
+WHOLE_VMEM = 66_500_000
 
 
 def attend_part(where, swapped, spread, seqs, own_len, local_heads, head_dim):
@@ -129,6 +130,7 @@
         out_shape=jax.ShapeDtypeStruct((pairs, own_rows, lanes + head_dim), BF16),
         in_specs=[pl.BlockSpec(memory_space=pltpu.SMEM), vmem, vmem],
         out_specs=vmem,
+        compiler_params=pltpu.CompilerParams(vmem_limit_bytes=WHOLE_VMEM),
         name="attend_part",
     )(where, swapped, spread)
 
@@ -179,7 +181,7 @@
     return pl.pallas_call(
         kernel,
         out_shape=jax.ShapeDtypeStruct((slots, width), BF16),
-        in_specs=[vmem] + [pl.BlockSpec(memory_space=pl.ANY)] * len(pieces),
+        in_specs=[vmem] + [pl.BlockSpec(memory_space=pltpu.HBM)] * len(pieces),
         out_specs=vmem,
         scratch_shapes=[pltpu.VMEM((slots, width), F32)]
         + [pltpu.VMEM((hidden_units, width), BF16)] * 3
@@ -296,7 +298,8 @@
     attended = jnp.sum(scale[..., None] * part_mixed.astype(F32), axis=0).astype(BF16)
     attended = attended.reshape(own_rows, group * head_dim)
 
-    gathered_heads = exchange(for_each(attended, pairs), "pair").reshape(rows, group_cols)
+    heads_send = for_each(attended, pairs)
+    gathered_heads = exchange(heads_send, "pair").reshape(rows, group_cols)
     projected = jnp.stack(
         [dot(gathered_heads, out_mine, 1, 0), dot(gathered_heads, out_other, 1, 0)]
     ).astype(BF16)
@@ -306,9 +309,8 @@
         .transpose(2, 1, 0, 3, 4)
         .reshape(seqs * pairs, 2 * own_len, out_cols)
     )
-    owned = exchange(projected, ("head", "pair")).reshape(
-        heads, pairs, 2, own_len, out_cols
-    ).astype(F32)
+    owned = exchange(projected, ("head", "pair"))
+    owned = owned.reshape(heads, pairs, 2, own_len, out_cols).astype(F32)
     owned = (owned[:, :, 0] + owned[::-1, :, 1]).reshape(heads * pairs, own_len, out_cols)
     owned = jnp.moveaxis(owned, 0, 1).reshape(own_len, width)
     own_tokens = lax.dynamic_index_in_dim(tokens_in, lax.axis_index("head"), 0, keepdims=False)
@@ -332,8 +334,10 @@
     incoming = incoming.reshape(slots, width)
 
     half = joined.shape[0] // 2
-    far_low = lax.ppermute(from_below[:half], "pair", up_ring)
-    far_high = lax.ppermute(from_above[half:], "pair", down_ring)
+    low_half = from_below[:half]
+    high_half = from_above[half:]
+    far_low = lax.ppermute(low_half, "pair", up_ring)
+    far_high = lax.ppermute(high_half, "pair", down_ring)
     expert_out = experts_forward(incoming, [joined, from_below, from_above, far_low, far_high])
     returned = exchange(expert_out.reshape(experts, capacity, width), ("ctx", "head"))
     returned = returned.reshape(slots, width)

time: 256 us -> 244 us (0.953)
  local copies, waits for them, and re-layouts: 21.9 us -> 13.4 us
  waiting for transfers between devices: 108 us -> 111 us
  matrix products: 7.03 us -> 4.32 us
    all_to_all x8, waiting for transfers between devices: 107 us -> 109 us  [exchange(): return lax.all_to_all(tiles, axis, 0, 0, tiled=True)]
    dot_general x6, matrix products: 7.03 us -> 4.32 us  [dot(): lax.dot_general(a, b, (((a_dim,), (b_dim,)), ((), ())), preferred_element...]
    mul x2, local copies, waits for them, and re-layouts: 2.92 us -> 0.29 us  [body(): scale[..., None] * part_mixed.astype(F32)]
  transfers between devices with their start and end apart: 13 -> 13, of which waited for: 9 -> 9; matrix products, arithmetic and copies ran while one was open for 10% -> 6% of each run, Pallas kernels for 2% -> 2%
where the time goes in v6:
time: 244 us; the launch traced here: 242 us
  waiting for transfers between devices  111 us (45%)
  starting transfers between devices  92.5 us (38%)
  local copies, waits for them, and re-layouts  13.4 us (5%)
  Pallas kernels  12.3 us (5%)
  other arithmetic  8.27 us (3%)
  matrix products  4.32 us (2%)
    all_to_all x8, waiting for transfers between devices, exchange(): return lax.all_to_all(tiles, axis, 0, 0, tiled=True)  109 us
    all_to_all x8, starting transfers between devices, exchange(): return lax.all_to_all(tiles, axis, 0, 0, tiled=True)  73.3 us
    pallas_call x1, Pallas kernels, experts_forward(): pl.pallas_call(kernel, out_shape=jax.ShapeDtypeStruct((slots, width), BF1...  7.91 us
    ppermute x1, starting transfers between devices, body(): lax.ppermute(out_theirs, 'head', [(h, heads - 1 - h) for h in range(heads)])  6 us
  transfers between devices with their start and end apart: 13, of which 9 were waited for; matrix products, arithmetic and copies ran while one was open for 6% of the time, Pallas kernels for 2%

profile of v6, /device:TPU:1, one launch (start us, length us, event | category | flops | bytes accessed | tf_op | source)
XLA Modules:
  0.0 242.1 jit_solution(6501144269450277655)
XLA Ops:
  0.0 1.1 fusion.10
  1.1 1.0 fusion.12
  2.1 0.9 broadcast_in_dim.21
  2.9 4.8 %all-to-all-start = ((bf16[4,2,16,2048]{3,2,1,0:T(8,128)(2,1)}), bf16[4,2,16,2048]{3,2,1,0:T(8,128)(2,1)S(1)}, u32[]{:S(2)}, u32[]{:S(2)}) async-start(bf16[4,2,16,2048]{3,2,1,0:T(8,128)(2,1)} %broadcast_in_dim.21), calls=%async_computation | async-start | bytes 1048576 | tf_op jit(solution)/shard_map/all_to_all | solution.py:17
  7.9 6.8 %all-to-all-done = bf16[4,2,16,2048]{3,2,1,0:T(8,128)(2,1)S(1)} async-done(((bf16[4,2,16,2048]{3,2,1,0:T(8,128)(2,1)}), bf16[4,2,16,2048]{3,2,1,0:T(8,128)(2,1)S(1)}, u32[]{:S(2)}, u32[]{:S(2)}) %all-to-all-start) | async-done | bytes 524320 | tf_op jit(solution)/shard_map/all_to_all | solution.py:17
  14.7 1.7 fusion.61
  16.5 0.2 fusion.37
  16.8 0.3 convolution_convert_fusion.3
  17.3 0.7 fusion.9
  18.0 3.5 %all-to-all-start.1 = ((bf16[4,160,256]{2,1,0:T(8,128)(2,1)}), bf16[4,160,256]{2,1,0:T(8,128)(2,1)S(1)}, u32[]{:S(2)}, u32[]{:S(2)}) async-start(bf16[4,160,256]{2,1,0:T(8,128)(2,1)} %fusion.9), calls=%async_computation.1 | async-start | bytes 655360 | tf_op jit(solution)/shard_map/all_to_all | solution.py:17
  21.6 5.7 %all-to-all-done.1.swapped_ref = bf16[4,160,256]{2,1,0:T(8,128)(2,1)S(1)} async-done(((bf16[4,160,256]{2,1,0:T(8,128)(2,1)}), bf16[4,160,256]{2,1,0:T(8,128)(2,1)S(1)}, u32[]{:S(2)}, u32[]{:S(2)}) %all-to-all-start.1) | async-done | bytes 327712 | tf_op jit(solution)/shard_map/all_to_all | solution.py:17
  27.8 1.2 broadcast_in_dim.23
  28.9 18.0 %all-to-all-start.2 = ((bf16[64,32,256]{2,1,0:T(8,128)(2,1)}), bf16[64,32,256]{2,1,0:T(8,128)(2,1)}, u32[]{:S(2)}, u32[]{:S(2)}) async-start(bf16[64,32,256]{2,1,0:T(8,128)(2,1)} %broadcast_in_dim.23), calls=%async_computation.2 | async-start | bytes 2097152 | tf_op jit(solution)/shard_map/all_to_all | solution.py:17
  47.0 2.8 %pad_maximum_fusion.refs_0_ = bf16[192,6144]{1,0:T(8,128)(2,1)} fusion(bf16[192,2048]{1,0:T(8,128)(2,1)S(1)} %bitcast.75, bf16[192,2048]{1,0:T(8,128)(2,1)S(1)} %bitcast.76, bf16[192,2048]{1,0:T(8,128)(2,1)} %bitcast.77), kind=kLoop, calls=%fused_computation.2 | loop fusion | flops 7077888 | bytes 4718592 | tf_op jit(solution)/shard_map/concatenate | solution.py:222
  49.8 2.2 collective-permute-start.1
  52.0 4.3 %collective-permute-start.2 = (bf16[192,6144]{1,0:T(8,128)(2,1)}, bf16[192,6144]{1,0:T(8,128)(2,1)}, u32[]{:S(2)}, u32[]{:S(2)}) collective-permute-start(bf16[192,6144]{1,0:T(8,128)(2,1)} %pad_maximum_fusion.refs_0_), channel_id=1, source_target_pairs={{0,3},{1,0},{2,1},{3,2},{4,7},{5,4},{6,5},{7,6},{8,11},{9,8},{10,9... | collective-permute-start | bytes 7077896 | tf_op jit(solution)/shard_map/ppermute | solution.py:224
  56.3 6.0 %collective-permute-start = (bf16[1024,256]{1,0:T(8,128)(2,1)S(1)}, bf16[1024,256]{1,0:T(8,128)(2,1)}, u32[]{:S(2)}, u32[]{:S(2)}) collective-permute-start(bf16[1024,256]{1,0:T(8,128)(2,1)S(1)} %constant_dynamic-slice_fusion), channel_id=1, source_target_pairs={{0,4},{4,0},{1,5},{5,1},{2,6},{6,2},{3,7},{7,3},{8,12},{12,8},{9,1... | collective-permute-start | bytes 1572872 | tf_op jit(solution)/shard_map/ppermute | solution.py:274
  62.5 0.7 pad_add_fusion.where_ref
  63.2 8.4 %all-to-all-done.2.spread_ref = bf16[64,32,256]{2,1,0:T(8,128)(2,1)} async-done(((bf16[64,32,256]{2,1,0:T(8,128)(2,1)}), bf16[64,32,256]{2,1,0:T(8,128)(2,1)}, u32[]{:S(2)}, u32[]{:S(2)}) %all-to-all-start.2) | async-done | bytes 1048608 | tf_op jit(solution)/shard_map/all_to_all | solution.py:17
  71.6 4.4 %attend_part.1 = bf16[4,32,1152]{2,1,0:T(8,128)(2,1)} custom-call(s32[2]{0:T(128)} %pad_add_fusion.where_ref, bf16[4,160,256]{2,1,0:T(8,128)(2,1)} %copy-done, bf16[64,32,256]{2,1,0:T(8,128)(2,1)} %all-to-all-done.2.spread_ref), custom_call_target="tpu_custom_call" | custom-call | tf_op jit(solution)/shard_map/attend_part/pallas_call | solution.py:128
  76.0 3.6 %all-to-all-start.3 = ((bf16[4,32,1152]{2,1,0:T(8,128)(2,1)}), bf16[4,32,1152]{2,1,0:T(8,128)(2,1)S(1)}, u32[]{:S(2)}, u32[]{:S(2)}) async-start(bf16[4,32,1152]{2,1,0:T(8,128)(2,1)} %attend_part.1), calls=%async_computation.3 | async-start | bytes 589824 | tf_op jit(solution)/shard_map/all_to_all | solution.py:17
  79.9 25.7 %all-to-all-done.3 = bf16[4,32,1152]{2,1,0:T(8,128)(2,1)S(1)} async-done(((bf16[4,32,1152]{2,1,0:T(8,128)(2,1)}), bf16[4,32,1152]{2,1,0:T(8,128)(2,1)S(1)}, u32[]{:S(2)}, u32[]{:S(2)}) %all-to-all-start.3) | async-done | bytes 294944 | tf_op jit(solution)/shard_map/all_to_all | solution.py:17
  105.9 0.2 mul.185
  106.2 0.7 broadcast_in_dim.24
  107.0 5.0 %all-to-all-start.4 = ((bf16[4,32,1024]{2,1,0:T(8,128)(2,1)}), bf16[4,32,1024]{2,1,0:T(8,128)(2,1)S(1)}, u32[]{:S(2)}, u32[]{:S(2)}) async-start(bf16[4,32,1024]{2,1,0:T(8,128)(2,1)} %broadcast_in_dim.24), calls=%async_computation.4 | async-start | bytes 524288 | tf_op jit(solution)/shard_map/all_to_all | solution.py:17
  112.0 5.5 %all-to-all-done.4 = bf16[4,32,1024]{2,1,0:T(8,128)(2,1)S(1)} async-done(((bf16[4,32,1024]{2,1,0:T(8,128)(2,1)}), bf16[4,32,1024]{2,1,0:T(8,128)(2,1)S(1)}, u32[]{:S(2)}, u32[]{:S(2)}) %all-to-all-start.4) | async-done | bytes 262176 | tf_op jit(solution)/shard_map/all_to_all | solution.py:17
  117.5 0.2 fusion.1
  117.7 1.3 fusion.2
  119.0 0.7 copy.52
  119.7 10.1 %all-to-all-start.5 = ((bf16[8,32,256]{2,1,0:T(8,128)(2,1)}), bf16[8,32,256]{2,1,0:T(8,128)(2,1)S(1)}, u32[]{:S(2)}, u32[]{:S(2)}) async-start(bf16[8,32,256]{2,1,0:T(8,128)(2,1)} %bitcast.22), calls=%async_computation.5 | async-start | bytes 262144 | tf_op jit(solution)/shard_map/all_to_all | solution.py:17
  129.9 5.1 %all-to-all-done.5 = bf16[8,32,256]{2,1,0:T(8,128)(2,1)S(1)} async-done(((bf16[8,32,256]{2,1,0:T(8,128)(2,1)}), bf16[8,32,256]{2,1,0:T(8,128)(2,1)S(1)}, u32[]{:S(2)}, u32[]{:S(2)}) %all-to-all-start.5) | async-done | bytes 131104 | tf_op jit(solution)/shard_map/all_to_all | solution.py:17
  135.2 0.5 convolution_convert_fusion
  135.7 1.5 reshape.155
  137.2 13.1 %all-to-all-start.6 = ((bf16[128,2,2048]{2,1,0:T(2,128)(2,1)}), bf16[128,2,2048]{2,1,0:T(2,128)(2,1)S(1)}, u32[]{:S(2)}, u32[]{:S(2)}) async-start(bf16[128,2,2048]{2,1,0:T(2,128)(2,1)} %reshape.155), calls=%async_computation.6 | async-start | bytes 2097152 | tf_op jit(solution)/shard_map/all_to_all | solution.py:17
  150.3 1.3 slice.122
  151.7 2.5 %collective-permute-start.3 = (bf16[96,6144]{1,0:T(8,128)(2,1)S(1)}, bf16[96,6144]{1,0:T(8,128)(2,1)}, u32[]{:S(2)}, u32[]{:S(2)}) collective-permute-start(bf16[96,6144]{1,0:T(8,128)(2,1)S(1)} %slice.122), channel_id=1, source_target_pairs={{0,1},{1,2},{2,3},{3,0},{4,5},{5,6},{6,7},{7,4},{8,9},{9,10},{10,1... | collective-permute-start | bytes 3538952 | tf_op jit(solution)/shard_map/ppermute | solution.py:339
  154.2 1.3 slice.123
  155.6 4.1 %collective-permute-start.4 = (bf16[96,6144]{1,0:T(8,128)(2,1)S(1)}, bf16[96,6144]{1,0:T(8,128)(2,1)}, u32[]{:S(2)}, u32[]{:S(2)}) collective-permute-start(bf16[96,6144]{1,0:T(8,128)(2,1)S(1)} %slice.123), channel_id=1, source_target_pairs={{0,3},{1,0},{2,1},{3,2},{4,7},{5,4},{6,5},{7,6},{8,11},{9,8},{10,9... | collective-permute-start | bytes 3538952 | tf_op jit(solution)/shard_map/ppermute | solution.py:340
  159.7 21.5 %all-to-all-done.6 = bf16[128,2,2048]{2,1,0:T(2,128)(2,1)S(1)} async-done(((bf16[128,2,2048]{2,1,0:T(2,128)(2,1)}), bf16[128,2,2048]{2,1,0:T(2,128)(2,1)S(1)}, u32[]{:S(2)}, u32[]{:S(2)}) %all-to-all-start.6) | async-done | bytes 1048608 | tf_op jit(solution)/shard_map/all_to_all | solution.py:17
  181.3 1.2 reshape.156.rows_ref
  182.5 1.5 collective-permute-done.4.refs_4_
  183.9 7.9 %experts_forward.1 = bf16[256,2048]{1,0:T(8,128)(2,1)} custom-call(bf16[256,2048]{1,0:T(8,128)(2,1)} %reshape.156.rows_ref, bf16[192,6144]{1,0:T(8,128)(2,1)} %pad_maximum_fusion.refs_0_, bf16[192,6144]{1,0:T(8,128)(2,1)} %collective-permute-done.1.refs_1_, bf16[192,6144]{1,0:T(8,128)(2,1)} %collective-permute-done.2.refs_2_, ...), custom_call_target="tpu_custom_call" | custom-call | tf_op jit(solution)/shard_map/experts_forward/pallas_call | solution.py:181
  191.9 2.5 %reshape.157 = bf16[128,2,2048]{2,1,0:T(2,128)(2,1)} reshape(bf16[256,2048]{1,0:T(8,128)(2,1)} %experts_forward.1) | data formatting | bytes 2097152 | tf_op jit(solution)/shard_map/reshape | solution.py:342
  194.4 15.4 %all-to-all-start.7 = ((bf16[128,2,2048]{2,1,0:T(2,128)(2,1)}), bf16[128,2,2048]{2,1,0:T(2,128)(2,1)S(1)}, u32[]{:S(2)}, u32[]{:S(2)}) async-start(bf16[128,2,2048]{2,1,0:T(2,128)(2,1)} %reshape.157), calls=%async_computation.7 | async-start | bytes 2097152 | tf_op jit(solution)/shard_map/all_to_all | solution.py:17
  210.0 30.7 %all-to-all-done.7 = bf16[128,2,2048]{2,1,0:T(2,128)(2,1)S(1)} async-done(((bf16[128,2,2048]{2,1,0:T(2,128)(2,1)}), bf16[128,2,2048]{2,1,0:T(2,128)(2,1)S(1)}, u32[]{:S(2)}, u32[]{:S(2)}) %all-to-all-start.7) | async-done | bytes 1048608 | tf_op jit(solution)/shard_map/all_to_all | solution.py:17
  240.7 0.4 reshape.158
  241.1 0.3 fusion.53
  241.4 0.7 fusion.23
  (70 shorter events, 2.5 us)
Async XLA Ops:
  0.0 16.8 %copy-start.10 = (bf16[32,2048]{1,0:T(8,128)(2,1)S(1)}, bf16[32,2048]{1,0:T(8,128)(2,1)}, u32[]{:S(2)}) copy-start(bf16[32,2048]{1,0:T(8,128)(2,1)} %param.15) | copy-start | bytes 393220
  0.0 16.8 %copy-start.9 = (bf16[32,2048]{1,0:T(8,128)(2,1)S(1)}, bf16[32,2048]{1,0:T(8,128)(2,1)}, u32[]{:S(2)}) copy-start(bf16[32,2048]{1,0:T(8,128)(2,1)} %param.16) | copy-start | bytes 393220
  2.9 11.8 %all-to-all-start = ((bf16[4,2,16,2048]{3,2,1,0:T(8,128)(2,1)}), bf16[4,2,16,2048]{3,2,1,0:T(8,128)(2,1)S(1)}, u32[]{:S(2)}, u32[]{:S(2)}) async-start(bf16[4,2,16,2048]{3,2,1,0:T(8,128)(2,1)} %broadcast_in_dim.21), calls=%async_computation | async-start | bytes 1048576 | tf_op jit(solution)/shard_map/all_to_all | solution.py:17
  17.3 29.6 %copy-start.4 = (bf16[1,192,2048]{2,1,0:T(8,128)(2,1)S(1)}, bf16[1,192,2048]{2,1,0:T(8,128)(2,1)}, u32[]{:S(2)}) copy-start(bf16[1,192,2048]{2,1,0:T(8,128)(2,1)} %param.23) | copy-start | bytes 2359300
  17.3 29.6 %copy-start.5 = (bf16[1,192,2048]{2,1,0:T(8,128)(2,1)S(1)}, bf16[1,192,2048]{2,1,0:T(8,128)(2,1)}, u32[]{:S(2)}) copy-start(bf16[1,192,2048]{2,1,0:T(8,128)(2,1)} %param.22) | copy-start | bytes 2359300
  18.0 9.3 %all-to-all-start.1 = ((bf16[4,160,256]{2,1,0:T(8,128)(2,1)}), bf16[4,160,256]{2,1,0:T(8,128)(2,1)S(1)}, u32[]{:S(2)}, u32[]{:S(2)}) async-start(bf16[4,160,256]{2,1,0:T(8,128)(2,1)} %fusion.9), calls=%async_computation.1 | async-start | bytes 655360 | tf_op jit(solution)/shard_map/all_to_all | solution.py:17
  27.4 22.4 %copy-start = (bf16[4,160,256]{2,1,0:T(8,128)(2,1)}, bf16[4,160,256]{2,1,0:T(8,128)(2,1)S(1)}, u32[]{:S(2)}) copy-start(bf16[4,160,256]{2,1,0:T(8,128)(2,1)S(1)} %all-to-all-done.1.swapped_ref) | copy-start | bytes 983044
  28.9 42.6 %all-to-all-start.2 = ((bf16[64,32,256]{2,1,0:T(8,128)(2,1)}), bf16[64,32,256]{2,1,0:T(8,128)(2,1)}, u32[]{:S(2)}, u32[]{:S(2)}) async-start(bf16[64,32,256]{2,1,0:T(8,128)(2,1)} %broadcast_in_dim.23), calls=%async_computation.2 | async-start | bytes 2097152 | tf_op jit(solution)/shard_map/all_to_all | solution.py:17
  46.9 9.3 %copy-start.1 = (bf16[2048,256]{1,0:T(8,128)(2,1)S(1)}, bf16[2048,256]{1,0:T(8,128)(2,1)}, u32[]{:S(2)}) copy-start(bf16[2048,256]{1,0:T(8,128)(2,1)} %param.17) | copy-start | bytes 3145732
  46.9 15.4 %copy-start.6 = (s32[1,16,8]{1,2,0:T(8,128)S(1)}, s32[1,16,8]{1,2,0:T(8,128)}, u32[]{:S(2)}) copy-start(s32[1,16,8]{1,2,0:T(8,128)} %param.19) | copy-start | bytes 1540
  49.8 100.5 %collective-permute-start.1 = (bf16[192,6144]{1,0:T(8,128)(2,1)}, bf16[192,6144]{1,0:T(8,128)(2,1)}, u32[]{:S(2)}, u32[]{:S(2)}) collective-permute-start(bf16[192,6144]{1,0:T(8,128)(2,1)} %pad_maximum_fusion.refs_0_), channel_id=1, source_target_pairs={{0,1},{1,2},{2,3},{3,0},{4,5},{5,6},{6,7},{7,4},{8,9},{9,10},{10,1... | collective-permute-start | bytes 7077896 | tf_op jit(solution)/shard_map/ppermute | solution.py:223
  52.0 102.3 %collective-permute-start.2 = (bf16[192,6144]{1,0:T(8,128)(2,1)}, bf16[192,6144]{1,0:T(8,128)(2,1)}, u32[]{:S(2)}, u32[]{:S(2)}) collective-permute-start(bf16[192,6144]{1,0:T(8,128)(2,1)} %pad_maximum_fusion.refs_0_), channel_id=1, source_target_pairs={{0,3},{1,0},{2,1},{3,2},{4,7},{5,4},{6,5},{7,6},{8,11},{9,8},{10,9... | collective-permute-start | bytes 7077896 | tf_op jit(solution)/shard_map/ppermute | solution.py:224
  56.3 61.4 %collective-permute-start = (bf16[1024,256]{1,0:T(8,128)(2,1)S(1)}, bf16[1024,256]{1,0:T(8,128)(2,1)}, u32[]{:S(2)}, u32[]{:S(2)}) collective-permute-start(bf16[1024,256]{1,0:T(8,128)(2,1)S(1)} %constant_dynamic-slice_fusion), channel_id=1, source_target_pairs={{0,4},{4,0},{1,5},{5,1},{2,6},{6,2},{3,7},{7,3},{8,12},{12,8},{9,1... | collective-permute-start | bytes 1572872 | tf_op jit(solution)/shard_map/ppermute | solution.py:274
  76.0 41.5 %copy-start.2 = (bf16[2048,256]{1,0:T(8,128)(2,1)S(1)}, bf16[2048,256]{1,0:T(8,128)(2,1)}, u32[]{:S(2)}) copy-start(bf16[2048,256]{1,0:T(8,128)(2,1)} %param.17) | copy-start | bytes 3145732
  76.0 29.6 %all-to-all-start.3 = ((bf16[4,32,1152]{2,1,0:T(8,128)(2,1)}), bf16[4,32,1152]{2,1,0:T(8,128)(2,1)S(1)}, u32[]{:S(2)}, u32[]{:S(2)}) async-start(bf16[4,32,1152]{2,1,0:T(8,128)(2,1)} %attend_part.1), calls=%async_computation.3 | async-start | bytes 589824 | tf_op jit(solution)/shard_map/all_to_all | solution.py:17
  106.2 28.8 %copy-start.3 = (bf16[2,16,2048]{2,1,0:T(8,128)(2,1)S(1)}, bf16[2,16,2048]{2,1,0:T(8,128)(2,1)}, u32[]{:S(2)}) copy-start(bf16[2,16,2048]{2,1,0:T(8,128)(2,1)} %param.12) | copy-start | bytes 393220
  107.0 28.2 %copy-start.7 = (f32[2048]{0:T(1024)S(1)}, f32[2048]{0:T(1024)}, u32[]{:S(2)}) copy-start(f32[2048]{0:T(1024)} %param.18) | copy-start | bytes 24580
  107.0 10.5 %all-to-all-start.4 = ((bf16[4,32,1024]{2,1,0:T(8,128)(2,1)}), bf16[4,32,1024]{2,1,0:T(8,128)(2,1)S(1)}, u32[]{:S(2)}, u32[]{:S(2)}) async-start(bf16[4,32,1024]{2,1,0:T(8,128)(2,1)} %broadcast_in_dim.24), calls=%async_computation.4 | async-start | bytes 524288 | tf_op jit(solution)/shard_map/all_to_all | solution.py:17
  119.7 15.3 %all-to-all-start.5 = ((bf16[8,32,256]{2,1,0:T(8,128)(2,1)}), bf16[8,32,256]{2,1,0:T(8,128)(2,1)S(1)}, u32[]{:S(2)}, u32[]{:S(2)}) async-start(bf16[8,32,256]{2,1,0:T(8,128)(2,1)} %bitcast.22), calls=%async_computation.5 | async-start | bytes 262144 | tf_op jit(solution)/shard_map/all_to_all | solution.py:17
  137.2 44.0 %all-to-all-start.6 = ((bf16[128,2,2048]{2,1,0:T(2,128)(2,1)}), bf16[128,2,2048]{2,1,0:T(2,128)(2,1)S(1)}, u32[]{:S(2)}, u32[]{:S(2)}) async-start(bf16[128,2,2048]{2,1,0:T(2,128)(2,1)} %reshape.155), calls=%async_computation.6 | async-start | bytes 2097152 | tf_op jit(solution)/shard_map/all_to_all | solution.py:17
  151.7 30.8 %collective-permute-start.3 = (bf16[96,6144]{1,0:T(8,128)(2,1)S(1)}, bf16[96,6144]{1,0:T(8,128)(2,1)}, u32[]{:S(2)}, u32[]{:S(2)}) collective-permute-start(bf16[96,6144]{1,0:T(8,128)(2,1)S(1)} %slice.122), channel_id=1, source_target_pairs={{0,1},{1,2},{2,3},{3,0},{4,5},{5,6},{6,7},{7,4},{8,9},{9,10},{10,1... | collective-permute-start | bytes 3538952 | tf_op jit(solution)/shard_map/ppermute | solution.py:339
  155.6 28.4 %collective-permute-start.4 = (bf16[96,6144]{1,0:T(8,128)(2,1)S(1)}, bf16[96,6144]{1,0:T(8,128)(2,1)}, u32[]{:S(2)}, u32[]{:S(2)}) collective-permute-start(bf16[96,6144]{1,0:T(8,128)(2,1)S(1)} %slice.123), channel_id=1, source_target_pairs={{0,3},{1,0},{2,1},{3,2},{4,7},{5,4},{6,5},{7,6},{8,11},{9,8},{10,9... | collective-permute-start | bytes 3538952 | tf_op jit(solution)/shard_map/ppermute | solution.py:340
  191.9 17.9 %copy-start.8 = (f32[1,16,8]{1,2,0:T(8,128)S(1)}, f32[1,16,8]{1,2,0:T(8,128)}, u32[]{:S(2)}) copy-start(f32[1,16,8]{1,2,0:T(8,128)} %param.20) | copy-start | bytes 1540
  194.4 46.3 %all-to-all-start.7 = ((bf16[128,2,2048]{2,1,0:T(2,128)(2,1)}), bf16[128,2,2048]{2,1,0:T(2,128)(2,1)S(1)}, u32[]{:S(2)}, u32[]{:S(2)}) async-start(bf16[128,2,2048]{2,1,0:T(2,128)(2,1)} %reshape.157), calls=%async_computation.7 | async-start | bytes 2097152 | tf_op jit(solution)/shard_map/all_to_all | solution.py:17

commit v7 on v6

--- a/solution.py
+++ b/solution.py
@@ -1,3 +1,5 @@
+import math
+
 import jax
 import jax.numpy as jnp
 from jax import lax
@@ -13,8 +15,8 @@
 BF16 = jnp.bfloat16
 
 
-def exchange(tiles, axis):
-    return lax.all_to_all(tiles, axis, 0, 0, tiled=True)
+def exchange(tiles, axis, groups=None):
+    return lax.all_to_all(tiles, axis, 0, 0, tiled=True, axis_index_groups=groups)
 
 
 def for_each(shard, count):
@@ -180,14 +182,15 @@
     vmem = pl.BlockSpec(memory_space=pltpu.VMEM)
     return pl.pallas_call(
         kernel,
-        out_shape=jax.ShapeDtypeStruct((slots, width), BF16),
+        out_shape=pltpu.VMEM((slots, width), BF16),
         in_specs=[vmem] + [pl.BlockSpec(memory_space=pltpu.HBM)] * len(pieces),
         out_specs=vmem,
         scratch_shapes=[pltpu.VMEM((slots, width), F32)]
         + [pltpu.VMEM((hidden_units, width), BF16)] * 3
         + [pltpu.SemaphoreType.DMA((3 * len(pieces),))],
+        compiler_params=pltpu.CompilerParams(vmem_limit_bytes=24 << 20),
         name="experts_forward",
-    )(incoming, *pieces)
+    )(pltpu.with_memory_space_constraint(incoming, pltpu.VMEM), *pieces)
 
 
 def body(
@@ -262,8 +265,14 @@
     )
     key_own = rotate(key_own.astype(F32), rope_tables(own_pos.astype(F32), head_dim))
     both = jnp.concatenate([key_own, value_own], axis=1)
-    kv_send = for_each(both, blocks)
-    spread = exchange(kv_send, "ctx")
+    inner = math.isqrt(blocks)
+    outer = blocks // inner
+    near_groups = [[a * inner + b for b in range(inner)] for a in range(outer)]
+    far_groups = [[a * inner + b for a in range(outer)] for b in range(inner)]
+    kv_send = for_each(both, inner)
+    near = exchange(kv_send, "ctx", near_groups)
+    spread = exchange(for_each(near, outer).reshape(outer, -1, near.shape[-1]), "ctx", far_groups)
+    spread = spread.reshape(blocks, own_rows, 2 * head_dim)
 
     head = lax.axis_index("head")
     group_cols = group * head_dim

time: 244 us -> 246 us (level)
  blocking collectives: 0 us -> 15.9 us
  starting transfers between devices: 92.5 us -> 83.1 us
    all_to_all x0 -> x1, blocking collectives: none -> 15.9 us  [exchange(): lax.all_to_all(tiles, axis, 0, 0, tiled=True, axis_index_groups=groups)]
    all_to_all x8, starting transfers between devices: 73.3 us -> 62.5 us  [exchange(): lax.all_to_all(tiles, axis, 0, 0, tiled=True, axis_index_groups=groups)]
    all_to_all x8, waiting for transfers between devices: 109 us -> 104 us  [exchange(): lax.all_to_all(tiles, axis, 0, 0, tiled=True, axis_index_groups=groups)]
  transfers between devices with their start and end apart: 13 -> 13, of which waited for: 9 -> 10; matrix products, arithmetic and copies ran while one was open for 6% -> 6% of each run, Pallas kernels for 2% -> 2%
where the time goes in v7:
time: 246 us; the launch traced here: 245 us
  waiting for transfers between devices  109 us (44%)
  starting transfers between devices  83.1 us (34%)
  blocking collectives  15.9 us (6%)
  local copies, waits for them, and re-layouts  13.7 us (6%)
  Pallas kernels  10.1 us (4%)
  other arithmetic  8.27 us (3%)
  matrix products  4.32 us (2%)
    all_to_all x8, waiting for transfers between devices, exchange(): lax.all_to_all(tiles, axis, 0, 0, tiled=True, axis_index_groups=groups)  104 us
    all_to_all x8, starting transfers between devices, exchange(): lax.all_to_all(tiles, axis, 0, 0, tiled=True, axis_index_groups=groups)  62.5 us
    all_to_all x1, blocking collectives, exchange(): lax.all_to_all(tiles, axis, 0, 0, tiled=True, axis_index_groups=groups)  15.9 us
    ppermute x1, starting transfers between devices, body(): lax.ppermute(out_theirs, 'head', [(h, heads - 1 - h) for h in range(heads)])  7.43 us
    pallas_call x1, Pallas kernels, experts_forward(): pl.pallas_call(kernel, out_shape=pltpu.VMEM((slots, width), BF16), in_spe...  5.73 us
  transfers between devices with their start and end apart: 13, of which 10 were waited for; matrix products, arithmetic and copies ran while one was open for 6% of the time, Pallas kernels for 2%

profile of v7, /device:TPU:1, one launch (start us, length us, event | category | flops | bytes accessed | tf_op | source)
XLA Modules:
  0.0 244.8 jit_solution(5343102608668142021)
XLA Ops:
  0.0 1.1 fusion.10
  1.1 1.0 fusion.12
  2.1 0.9 broadcast_in_dim.25
  2.9 4.8 %all-to-all-start = ((bf16[4,2,16,2048]{3,2,1,0:T(8,128)(2,1)}), bf16[4,2,16,2048]{3,2,1,0:T(8,128)(2,1)S(1)}, u32[]{:S(2)}, u32[]{:S(2)}) async-start(bf16[4,2,16,2048]{3,2,1,0:T(8,128)(2,1)} %broadcast_in_dim.25), calls=%async_computation | async-start | bytes 1048576 | tf_op jit(solution)/shard_map/all_to_all | solution.py:19
  7.9 6.8 %all-to-all-done = bf16[4,2,16,2048]{3,2,1,0:T(8,128)(2,1)S(1)} async-done(((bf16[4,2,16,2048]{3,2,1,0:T(8,128)(2,1)}), bf16[4,2,16,2048]{3,2,1,0:T(8,128)(2,1)S(1)}, u32[]{:S(2)}, u32[]{:S(2)}) %all-to-all-start) | async-done | bytes 524320 | tf_op jit(solution)/shard_map/all_to_all | solution.py:19
  14.7 1.7 fusion.61
  16.8 0.3 convolution_convert_fusion.3
  17.3 0.7 fusion.9
  18.0 3.6 %all-to-all-start.1 = ((bf16[4,160,256]{2,1,0:T(8,128)(2,1)}), bf16[4,160,256]{2,1,0:T(8,128)(2,1)S(1)}, u32[]{:S(2)}, u32[]{:S(2)}) async-start(bf16[4,160,256]{2,1,0:T(8,128)(2,1)} %fusion.9), calls=%async_computation.1 | async-start | bytes 655360 | tf_op jit(solution)/shard_map/all_to_all | solution.py:19
  21.7 5.7 %all-to-all-done.1.swapped_ref = bf16[4,160,256]{2,1,0:T(8,128)(2,1)S(1)} async-done(((bf16[4,160,256]{2,1,0:T(8,128)(2,1)}), bf16[4,160,256]{2,1,0:T(8,128)(2,1)S(1)}, u32[]{:S(2)}, u32[]{:S(2)}) %all-to-all-start.1) | async-done | bytes 327712 | tf_op jit(solution)/shard_map/all_to_all | solution.py:19
  27.9 15.9 %all_to_all.45 = bf16[8,32,256]{2,1,0:T(8,128)(2,1)S(1)} all-to-all(bf16[8,32,256]{2,1,0:T(8,128)(2,1)S(1)} %broadcast_in_dim.27), channel_id=1, replica_groups={{0,8,16,24,32,40,48,56},{64,72,80,88,96,104,112,120},{128,136,144,152,1..., dimensions={0} | all-to-all | bytes 262144 | tf_op jit(solution)/shard_map/all_to_all | solution.py:19
  43.8 1.1 broadcast_in_dim.29
  45.0 10.0 %all-to-all-start.3 = ((bf16[8,256,256]{2,1,0:T(8,128)(2,1)}), bf16[8,256,256]{2,1,0:T(8,128)(2,1)}, u32[]{:S(2)}, u32[]{:S(2)}) async-start(bf16[8,256,256]{2,1,0:T(8,128)(2,1)} %broadcast_in_dim.29), calls=%async_computation.3 | async-start | bytes 2097152 | tf_op jit(solution)/shard_map/all_to_all | solution.py:19
  55.0 2.8 %pad_maximum_fusion.refs_0_ = bf16[192,6144]{1,0:T(8,128)(2,1)} fusion(bf16[192,2048]{1,0:T(8,128)(2,1)S(1)} %bitcast.77, bf16[192,2048]{1,0:T(8,128)(2,1)S(1)} %bitcast.78, bf16[192,2048]{1,0:T(8,128)(2,1)} %bitcast.79), kind=kLoop, calls=%fused_computation.2 | loop fusion | flops 7077888 | bytes 4718592 | tf_op jit(solution)/shard_map/concatenate | solution.py:225
  57.8 2.2 collective-permute-start.1
  60.0 4.3 %collective-permute-start.2 = (bf16[192,6144]{1,0:T(8,128)(2,1)}, bf16[192,6144]{1,0:T(8,128)(2,1)}, u32[]{:S(2)}, u32[]{:S(2)}) collective-permute-start(bf16[192,6144]{1,0:T(8,128)(2,1)} %pad_maximum_fusion.refs_0_), channel_id=1, source_target_pairs={{0,3},{1,0},{2,1},{3,2},{4,7},{5,4},{6,5},{7,6},{8,11},{9,8},{10,9... | collective-permute-start | bytes 7077896 | tf_op jit(solution)/shard_map/ppermute | solution.py:227
  64.4 7.4 %collective-permute-start = (bf16[1024,256]{1,0:T(8,128)(2,1)S(1)}, bf16[1024,256]{1,0:T(8,128)(2,1)}, u32[]{:S(2)}, u32[]{:S(2)}) collective-permute-start(bf16[1024,256]{1,0:T(8,128)(2,1)S(1)} %constant_dynamic-slice_fusion), channel_id=1, source_target_pairs={{0,4},{4,0},{1,5},{5,1},{2,6},{6,2},{3,7},{7,3},{8,12},{12,8},{9,1... | collective-permute-start | bytes 1572872 | tf_op jit(solution)/shard_map/ppermute | solution.py:283
  72.0 0.7 pad_add_fusion.where_ref
  72.7 7.7 %all-to-all-done.3 = bf16[8,256,256]{2,1,0:T(8,128)(2,1)} async-done(((bf16[8,256,256]{2,1,0:T(8,128)(2,1)}), bf16[8,256,256]{2,1,0:T(8,128)(2,1)}, u32[]{:S(2)}, u32[]{:S(2)}) %all-to-all-start.3) | async-done | bytes 1048608 | tf_op jit(solution)/shard_map/all_to_all | solution.py:19
  80.4 4.4 %attend_part.1 = bf16[4,32,1152]{2,1,0:T(8,128)(2,1)} custom-call(s32[2]{0:T(128)} %pad_add_fusion.where_ref, bf16[4,160,256]{2,1,0:T(8,128)(2,1)} %copy-done, bf16[64,32,256]{2,1,0:T(8,128)(2,1)} %bitcast.14.spread_ref), custom_call_target="tpu_custom_call" | custom-call | tf_op jit(solution)/shard_map/attend_part/pallas_call | solution.py:130
  84.7 3.6 %all-to-all-start.4 = ((bf16[4,32,1152]{2,1,0:T(8,128)(2,1)}), bf16[4,32,1152]{2,1,0:T(8,128)(2,1)S(1)}, u32[]{:S(2)}, u32[]{:S(2)}) async-start(bf16[4,32,1152]{2,1,0:T(8,128)(2,1)} %attend_part.1), calls=%async_computation.4 | async-start | bytes 589824 | tf_op jit(solution)/shard_map/all_to_all | solution.py:19
  88.7 23.6 %all-to-all-done.4 = bf16[4,32,1152]{2,1,0:T(8,128)(2,1)S(1)} async-done(((bf16[4,32,1152]{2,1,0:T(8,128)(2,1)}), bf16[4,32,1152]{2,1,0:T(8,128)(2,1)S(1)}, u32[]{:S(2)}, u32[]{:S(2)}) %all-to-all-start.4) | async-done | bytes 294944 | tf_op jit(solution)/shard_map/all_to_all | solution.py:19
  112.9 0.7 broadcast_in_dim.30
  113.6 5.0 %all-to-all-start.5 = ((bf16[4,32,1024]{2,1,0:T(8,128)(2,1)}), bf16[4,32,1024]{2,1,0:T(8,128)(2,1)S(1)}, u32[]{:S(2)}, u32[]{:S(2)}) async-start(bf16[4,32,1024]{2,1,0:T(8,128)(2,1)} %broadcast_in_dim.30), calls=%async_computation.5 | async-start | bytes 524288 | tf_op jit(solution)/shard_map/all_to_all | solution.py:19
  118.7 5.5 %all-to-all-done.5 = bf16[4,32,1024]{2,1,0:T(8,128)(2,1)S(1)} async-done(((bf16[4,32,1024]{2,1,0:T(8,128)(2,1)}), bf16[4,32,1024]{2,1,0:T(8,128)(2,1)S(1)}, u32[]{:S(2)}, u32[]{:S(2)}) %all-to-all-start.5) | async-done | bytes 262176 | tf_op jit(solution)/shard_map/all_to_all | solution.py:19
  124.1 0.2 fusion.1
  124.4 1.3 fusion.2
  125.7 0.7 copy.52
  126.3 11.5 %all-to-all-start.6 = ((bf16[8,32,256]{2,1,0:T(8,128)(2,1)}), bf16[8,32,256]{2,1,0:T(8,128)(2,1)S(1)}, u32[]{:S(2)}, u32[]{:S(2)}) async-start(bf16[8,32,256]{2,1,0:T(8,128)(2,1)} %bitcast.24), calls=%async_computation.6 | async-start | bytes 262144 | tf_op jit(solution)/shard_map/all_to_all | solution.py:19
  138.0 5.1 %all-to-all-done.6 = bf16[8,32,256]{2,1,0:T(8,128)(2,1)S(1)} async-done(((bf16[8,32,256]{2,1,0:T(8,128)(2,1)}), bf16[8,32,256]{2,1,0:T(8,128)(2,1)S(1)}, u32[]{:S(2)}, u32[]{:S(2)}) %all-to-all-start.6) | async-done | bytes 131104 | tf_op jit(solution)/shard_map/all_to_all | solution.py:19
  143.3 0.5 convolution_convert_fusion
  143.8 1.5 reshape.163
  145.3 8.7 %all-to-all-start.7 = ((bf16[128,2,2048]{2,1,0:T(2,128)(2,1)}), bf16[128,2,2048]{2,1,0:T(2,128)(2,1)S(1)}, u32[]{:S(2)}, u32[]{:S(2)}) async-start(bf16[128,2,2048]{2,1,0:T(2,128)(2,1)} %reshape.163), calls=%async_computation.7 | async-start | bytes 2097152 | tf_op jit(solution)/shard_map/all_to_all | solution.py:19
  154.0 2.4 %slice.122 = bf16[96,6144]{1,0:T(8,128)(2,1)} slice(bf16[192,6144]{1,0:T(8,128)(2,1)} %collective-permute-done.1.refs_1_), slice={[0:96], [0:6144]} | slice | bytes 2359296 | tf_op jit(solution)/shard_map/slice | solution.py:346
  156.4 2.5 %collective-permute-start.3 = (bf16[96,6144]{1,0:T(8,128)(2,1)}, bf16[96,6144]{1,0:T(8,128)(2,1)S(1)}, u32[]{:S(2)}, u32[]{:S(2)}) collective-permute-start(bf16[96,6144]{1,0:T(8,128)(2,1)} %slice.122), channel_id=1, source_target_pairs={{0,1},{1,2},{2,3},{3,0},{4,5},{5,6},{6,7},{7,4},{8,9},{9,10},{10,1... | collective-permute-start | bytes 3538952 | tf_op jit(solution)/shard_map/ppermute | solution.py:348
  159.0 2.4 slice.123
  161.3 4.1 %collective-permute-start.4 = (bf16[96,6144]{1,0:T(8,128)(2,1)}, bf16[96,6144]{1,0:T(8,128)(2,1)}, u32[]{:S(2)}, u32[]{:S(2)}) collective-permute-start(bf16[96,6144]{1,0:T(8,128)(2,1)} %slice.123), channel_id=1, source_target_pairs={{0,3},{1,0},{2,1},{3,2},{4,7},{5,4},{6,5},{7,6},{8,11},{9,8},{10,9... | collective-permute-start | bytes 3538952 | tf_op jit(solution)/shard_map/ppermute | solution.py:349
  165.5 19.5 %all-to-all-done.7 = bf16[128,2,2048]{2,1,0:T(2,128)(2,1)S(1)} async-done(((bf16[128,2,2048]{2,1,0:T(2,128)(2,1)}), bf16[128,2,2048]{2,1,0:T(2,128)(2,1)S(1)}, u32[]{:S(2)}, u32[]{:S(2)}) %all-to-all-start.7) | async-done | bytes 1048608 | tf_op jit(solution)/shard_map/all_to_all | solution.py:19
  184.9 0.4 reshape.164.rows_ref
  185.4 1.0 collective-permute-done.3.refs_3_
  186.4 3.5 %collective-permute-done.4.refs_4_ = bf16[96,6144]{1,0:T(8,128)(2,1)} collective-permute-done((bf16[96,6144]{1,0:T(8,128)(2,1)}, bf16[96,6144]{1,0:T(8,128)(2,1)}, u32[]{:S(2)}, u32[]{:S(2)}) %collective-permute-start.4) | collective-permute-done | bytes 1179680 | tf_op jit(solution)/shard_map/ppermute | solution.py:349
  189.9 5.7 %experts_forward.1 = bf16[256,2048]{1,0:T(8,128)(2,1)S(1)} custom-call(bf16[256,2048]{1,0:T(8,128)(2,1)S(1)} %reshape.164.rows_ref, bf16[192,6144]{1,0:T(8,128)(2,1)} %pad_maximum_fusion.refs_0_, bf16[192,6144]{1,0:T(8,128)(2,1)} %collective-permute-done.1.refs_1_, bf16[192,6144]{1,0:T(8,128)(2,1)} %collective-permute-done.2.refs_2_, ...), custom_call_target="tpu_custom_call" | custom-call | tf_op jit(solution)/shard_map/experts_forward/pallas_call | solution.py:183
  195.6 1.5 reshape.165
  197.1 15.4 %all-to-all-start.8 = ((bf16[128,2,2048]{2,1,0:T(2,128)(2,1)}), bf16[128,2,2048]{2,1,0:T(2,128)(2,1)S(1)}, u32[]{:S(2)}, u32[]{:S(2)}) async-start(bf16[128,2,2048]{2,1,0:T(2,128)(2,1)} %reshape.165), calls=%async_computation.8 | async-start | bytes 2097152 | tf_op jit(solution)/shard_map/all_to_all | solution.py:19
  212.7 30.7 %all-to-all-done.8 = bf16[128,2,2048]{2,1,0:T(2,128)(2,1)S(1)} async-done(((bf16[128,2,2048]{2,1,0:T(2,128)(2,1)}), bf16[128,2,2048]{2,1,0:T(2,128)(2,1)S(1)}, u32[]{:S(2)}, u32[]{:S(2)}) %all-to-all-start.8) | async-done | bytes 1048608 | tf_op jit(solution)/shard_map/all_to_all | solution.py:19
  243.5 0.4 reshape.166
  243.9 0.3 fusion.53
  244.2 0.7 fusion.23
  (72 shorter events, 3.0 us)
Async XLA Ops:
  0.0 16.8 %copy-start.10 = (bf16[32,2048]{1,0:T(8,128)(2,1)S(1)}, bf16[32,2048]{1,0:T(8,128)(2,1)}, u32[]{:S(2)}) copy-start(bf16[32,2048]{1,0:T(8,128)(2,1)} %param.15) | copy-start | bytes 393220
  0.0 16.8 %copy-start.9 = (bf16[32,2048]{1,0:T(8,128)(2,1)S(1)}, bf16[32,2048]{1,0:T(8,128)(2,1)}, u32[]{:S(2)}) copy-start(bf16[32,2048]{1,0:T(8,128)(2,1)} %param.16) | copy-start | bytes 393220
  2.9 11.8 %all-to-all-start = ((bf16[4,2,16,2048]{3,2,1,0:T(8,128)(2,1)}), bf16[4,2,16,2048]{3,2,1,0:T(8,128)(2,1)S(1)}, u32[]{:S(2)}, u32[]{:S(2)}) async-start(bf16[4,2,16,2048]{3,2,1,0:T(8,128)(2,1)} %broadcast_in_dim.25), calls=%async_computation | async-start | bytes 1048576 | tf_op jit(solution)/shard_map/all_to_all | solution.py:19
  18.0 37.0 %copy-start.4 = (bf16[1,192,2048]{2,1,0:T(8,128)(2,1)S(1)}, bf16[1,192,2048]{2,1,0:T(8,128)(2,1)}, u32[]{:S(2)}) copy-start(bf16[1,192,2048]{2,1,0:T(8,128)(2,1)} %param.23) | copy-start | bytes 2359300
  18.0 37.0 %copy-start.5 = (bf16[1,192,2048]{2,1,0:T(8,128)(2,1)S(1)}, bf16[1,192,2048]{2,1,0:T(8,128)(2,1)}, u32[]{:S(2)}) copy-start(bf16[1,192,2048]{2,1,0:T(8,128)(2,1)} %param.22) | copy-start | bytes 2359300
  18.0 9.4 %all-to-all-start.1 = ((bf16[4,160,256]{2,1,0:T(8,128)(2,1)}), bf16[4,160,256]{2,1,0:T(8,128)(2,1)S(1)}, u32[]{:S(2)}, u32[]{:S(2)}) async-start(bf16[4,160,256]{2,1,0:T(8,128)(2,1)} %fusion.9), calls=%async_computation.1 | async-start | bytes 655360 | tf_op jit(solution)/shard_map/all_to_all | solution.py:19
  27.5 30.4 %copy-start = (bf16[4,160,256]{2,1,0:T(8,128)(2,1)}, bf16[4,160,256]{2,1,0:T(8,128)(2,1)S(1)}, u32[]{:S(2)}) copy-start(bf16[4,160,256]{2,1,0:T(8,128)(2,1)S(1)} %all-to-all-done.1.swapped_ref) | copy-start | bytes 983044
  45.0 35.4 %all-to-all-start.3 = ((bf16[8,256,256]{2,1,0:T(8,128)(2,1)}), bf16[8,256,256]{2,1,0:T(8,128)(2,1)}, u32[]{:S(2)}, u32[]{:S(2)}) async-start(bf16[8,256,256]{2,1,0:T(8,128)(2,1)} %broadcast_in_dim.29), calls=%async_computation.3 | async-start | bytes 2097152 | tf_op jit(solution)/shard_map/all_to_all | solution.py:19
  55.0 9.3 %copy-start.1 = (bf16[2048,256]{1,0:T(8,128)(2,1)S(1)}, bf16[2048,256]{1,0:T(8,128)(2,1)}, u32[]{:S(2)}) copy-start(bf16[2048,256]{1,0:T(8,128)(2,1)} %param.17) | copy-start | bytes 3145732
  55.0 16.8 %copy-start.6 = (s32[1,16,8]{1,2,0:T(8,128)S(1)}, s32[1,16,8]{1,2,0:T(8,128)}, u32[]{:S(2)}) copy-start(s32[1,16,8]{1,2,0:T(8,128)} %param.19) | copy-start | bytes 1540
  57.8 96.1 %collective-permute-start.1 = (bf16[192,6144]{1,0:T(8,128)(2,1)}, bf16[192,6144]{1,0:T(8,128)(2,1)}, u32[]{:S(2)}, u32[]{:S(2)}) collective-permute-start(bf16[192,6144]{1,0:T(8,128)(2,1)} %pad_maximum_fusion.refs_0_), channel_id=1, source_target_pairs={{0,1},{1,2},{2,3},{3,0},{4,5},{5,6},{6,7},{7,4},{8,9},{9,10},{10,1... | collective-permute-start | bytes 7077896 | tf_op jit(solution)/shard_map/ppermute | solution.py:226
  60.0 98.9 %collective-permute-start.2 = (bf16[192,6144]{1,0:T(8,128)(2,1)}, bf16[192,6144]{1,0:T(8,128)(2,1)}, u32[]{:S(2)}, u32[]{:S(2)}) collective-permute-start(bf16[192,6144]{1,0:T(8,128)(2,1)} %pad_maximum_fusion.refs_0_), channel_id=1, source_target_pairs={{0,3},{1,0},{2,1},{3,2},{4,7},{5,4},{6,5},{7,6},{8,11},{9,8},{10,9... | collective-permute-start | bytes 7077896 | tf_op jit(solution)/shard_map/ppermute | solution.py:227
  64.4 60.0 %collective-permute-start = (bf16[1024,256]{1,0:T(8,128)(2,1)S(1)}, bf16[1024,256]{1,0:T(8,128)(2,1)}, u32[]{:S(2)}, u32[]{:S(2)}) collective-permute-start(bf16[1024,256]{1,0:T(8,128)(2,1)S(1)} %constant_dynamic-slice_fusion), channel_id=1, source_target_pairs={{0,4},{4,0},{1,5},{5,1},{2,6},{6,2},{3,7},{7,3},{8,12},{12,8},{9,1... | collective-permute-start | bytes 1572872 | tf_op jit(solution)/shard_map/ppermute | solution.py:283
  84.7 39.4 %copy-start.2 = (bf16[2048,256]{1,0:T(8,128)(2,1)S(1)}, bf16[2048,256]{1,0:T(8,128)(2,1)}, u32[]{:S(2)}) copy-start(bf16[2048,256]{1,0:T(8,128)(2,1)} %param.17) | copy-start | bytes 3145732
  84.7 27.5 %all-to-all-start.4 = ((bf16[4,32,1152]{2,1,0:T(8,128)(2,1)}), bf16[4,32,1152]{2,1,0:T(8,128)(2,1)S(1)}, u32[]{:S(2)}, u32[]{:S(2)}) async-start(bf16[4,32,1152]{2,1,0:T(8,128)(2,1)} %attend_part.1), calls=%async_computation.4 | async-start | bytes 589824 | tf_op jit(solution)/shard_map/all_to_all | solution.py:19
  112.9 30.3 %copy-start.3 = (bf16[2,16,2048]{2,1,0:T(8,128)(2,1)S(1)}, bf16[2,16,2048]{2,1,0:T(8,128)(2,1)}, u32[]{:S(2)}) copy-start(bf16[2,16,2048]{2,1,0:T(8,128)(2,1)} %param.12) | copy-start | bytes 393220
  113.6 29.7 %copy-start.7 = (f32[2048]{0:T(1024)S(1)}, f32[2048]{0:T(1024)}, u32[]{:S(2)}) copy-start(f32[2048]{0:T(1024)} %param.18) | copy-start | bytes 24580
  113.6 10.5 %all-to-all-start.5 = ((bf16[4,32,1024]{2,1,0:T(8,128)(2,1)}), bf16[4,32,1024]{2,1,0:T(8,128)(2,1)S(1)}, u32[]{:S(2)}, u32[]{:S(2)}) async-start(bf16[4,32,1024]{2,1,0:T(8,128)(2,1)} %broadcast_in_dim.30), calls=%async_computation.5 | async-start | bytes 524288 | tf_op jit(solution)/shard_map/all_to_all | solution.py:19
  126.3 16.7 %all-to-all-start.6 = ((bf16[8,32,256]{2,1,0:T(8,128)(2,1)}), bf16[8,32,256]{2,1,0:T(8,128)(2,1)S(1)}, u32[]{:S(2)}, u32[]{:S(2)}) async-start(bf16[8,32,256]{2,1,0:T(8,128)(2,1)} %bitcast.24), calls=%async_computation.6 | async-start | bytes 262144 | tf_op jit(solution)/shard_map/all_to_all | solution.py:19
  145.3 39.6 %all-to-all-start.7 = ((bf16[128,2,2048]{2,1,0:T(2,128)(2,1)}), bf16[128,2,2048]{2,1,0:T(2,128)(2,1)S(1)}, u32[]{:S(2)}, u32[]{:S(2)}) async-start(bf16[128,2,2048]{2,1,0:T(2,128)(2,1)} %reshape.163), calls=%async_computation.7 | async-start | bytes 2097152 | tf_op jit(solution)/shard_map/all_to_all | solution.py:19
  156.4 29.9 %collective-permute-start.3 = (bf16[96,6144]{1,0:T(8,128)(2,1)}, bf16[96,6144]{1,0:T(8,128)(2,1)S(1)}, u32[]{:S(2)}, u32[]{:S(2)}) collective-permute-start(bf16[96,6144]{1,0:T(8,128)(2,1)} %slice.122), channel_id=1, source_target_pairs={{0,1},{1,2},{2,3},{3,0},{4,5},{5,6},{6,7},{7,4},{8,9},{9,10},{10,1... | collective-permute-start | bytes 3538952 | tf_op jit(solution)/shard_map/ppermute | solution.py:348
  161.3 28.6 %collective-permute-start.4 = (bf16[96,6144]{1,0:T(8,128)(2,1)}, bf16[96,6144]{1,0:T(8,128)(2,1)}, u32[]{:S(2)}, u32[]{:S(2)}) collective-permute-start(bf16[96,6144]{1,0:T(8,128)(2,1)} %slice.123), channel_id=1, source_target_pairs={{0,3},{1,0},{2,1},{3,2},{4,7},{5,4},{6,5},{7,6},{8,11},{9,8},{10,9... | collective-permute-start | bytes 3538952 | tf_op jit(solution)/shard_map/ppermute | solution.py:349
  195.6 16.9 %copy-start.8 = (f32[1,16,8]{1,2,0:T(8,128)S(1)}, f32[1,16,8]{1,2,0:T(8,128)}, u32[]{:S(2)}) copy-start(f32[1,16,8]{1,2,0:T(8,128)} %param.20) | copy-start | bytes 1540
  197.1 46.3 %all-to-all-start.8 = ((bf16[128,2,2048]{2,1,0:T(2,128)(2,1)}), bf16[128,2,2048]{2,1,0:T(2,128)(2,1)S(1)}, u32[]{:S(2)}, u32[]{:S(2)}) async-start(bf16[128,2,2048]{2,1,0:T(2,128)(2,1)} %reshape.165), calls=%async_computation.8 | async-start | bytes 2097152 | tf_op jit(solution)/shard_map/all_to_all | solution.py:19

commit v8 on v6

--- a/solution.py
+++ b/solution.py
@@ -180,14 +180,15 @@
     vmem = pl.BlockSpec(memory_space=pltpu.VMEM)
     return pl.pallas_call(
         kernel,
-        out_shape=jax.ShapeDtypeStruct((slots, width), BF16),
+        out_shape=pltpu.VMEM((slots, width), BF16),
         in_specs=[vmem] + [pl.BlockSpec(memory_space=pltpu.HBM)] * len(pieces),
         out_specs=vmem,
         scratch_shapes=[pltpu.VMEM((slots, width), F32)]
         + [pltpu.VMEM((hidden_units, width), BF16)] * 3
         + [pltpu.SemaphoreType.DMA((3 * len(pieces),))],
+        compiler_params=pltpu.CompilerParams(vmem_limit_bytes=24 << 20),
         name="experts_forward",
-    )(incoming, *pieces)
+    )(pltpu.with_memory_space_constraint(incoming, pltpu.VMEM), *pieces)
 
 
 def body(

time: 244 us -> 243 us (level)
  transfers between devices with their start and end apart: 13 -> 13, of which waited for: 9 -> 10; matrix products, arithmetic and copies ran while one was open for 6% -> 6% of each run, Pallas kernels for 2% -> 2%
where the time goes in v8:
time: 243 us; the launch traced here: 241 us
  waiting for transfers between devices  112 us (46%)
  starting transfers between devices  92.4 us (38%)
  local copies, waits for them, and re-layouts  13.7 us (6%)
  Pallas kernels  10.1 us (4%)
  other arithmetic  8.27 us (3%)
  matrix products  4.32 us (2%)
    all_to_all x8, waiting for transfers between devices, exchange(): return lax.all_to_all(tiles, axis, 0, 0, tiled=True)  107 us
    all_to_all x8, starting transfers between devices, exchange(): return lax.all_to_all(tiles, axis, 0, 0, tiled=True)  73.3 us
    ppermute x1, starting transfers between devices, body(): lax.ppermute(out_theirs, 'head', [(h, heads - 1 - h) for h in range(heads)])  6 us
    pallas_call x1, Pallas kernels, experts_forward(): pl.pallas_call(kernel, out_shape=pltpu.VMEM((slots, width), BF16), in_spe...  5.72 us
  transfers between devices with their start and end apart: 13, of which 10 were waited for; matrix products, arithmetic and copies ran while one was open for 6% of the time, Pallas kernels for 2%

profile of v8, /device:TPU:1, one launch (start us, length us, event | category | flops | bytes accessed | tf_op | source)
XLA Modules:
  0.0 241.2 jit_solution(867539498638336322)
XLA Ops:
  0.0 1.1 fusion.10
  1.1 1.0 fusion.12
  2.1 0.9 broadcast_in_dim.21
  2.9 4.8 %all-to-all-start = ((bf16[4,2,16,2048]{3,2,1,0:T(8,128)(2,1)}), bf16[4,2,16,2048]{3,2,1,0:T(8,128)(2,1)S(1)}, u32[]{:S(2)}, u32[]{:S(2)}) async-start(bf16[4,2,16,2048]{3,2,1,0:T(8,128)(2,1)} %broadcast_in_dim.21), calls=%async_computation | async-start | bytes 1048576 | tf_op jit(solution)/shard_map/all_to_all | solution.py:17
  7.9 6.8 %all-to-all-done = bf16[4,2,16,2048]{3,2,1,0:T(8,128)(2,1)S(1)} async-done(((bf16[4,2,16,2048]{3,2,1,0:T(8,128)(2,1)}), bf16[4,2,16,2048]{3,2,1,0:T(8,128)(2,1)S(1)}, u32[]{:S(2)}, u32[]{:S(2)}) %all-to-all-start) | async-done | bytes 524320 | tf_op jit(solution)/shard_map/all_to_all | solution.py:17
  14.7 1.7 fusion.61
  16.5 0.2 fusion.37
  16.8 0.3 convolution_convert_fusion.3
  17.3 0.7 fusion.9
  18.0 3.5 %all-to-all-start.1 = ((bf16[4,160,256]{2,1,0:T(8,128)(2,1)}), bf16[4,160,256]{2,1,0:T(8,128)(2,1)S(1)}, u32[]{:S(2)}, u32[]{:S(2)}) async-start(bf16[4,160,256]{2,1,0:T(8,128)(2,1)} %fusion.9), calls=%async_computation.1 | async-start | bytes 655360 | tf_op jit(solution)/shard_map/all_to_all | solution.py:17
  21.6 5.7 %all-to-all-done.1.swapped_ref = bf16[4,160,256]{2,1,0:T(8,128)(2,1)S(1)} async-done(((bf16[4,160,256]{2,1,0:T(8,128)(2,1)}), bf16[4,160,256]{2,1,0:T(8,128)(2,1)S(1)}, u32[]{:S(2)}, u32[]{:S(2)}) %all-to-all-start.1) | async-done | bytes 327712 | tf_op jit(solution)/shard_map/all_to_all | solution.py:17
  27.8 1.2 broadcast_in_dim.23
  28.9 18.0 %all-to-all-start.2 = ((bf16[64,32,256]{2,1,0:T(8,128)(2,1)}), bf16[64,32,256]{2,1,0:T(8,128)(2,1)}, u32[]{:S(2)}, u32[]{:S(2)}) async-start(bf16[64,32,256]{2,1,0:T(8,128)(2,1)} %broadcast_in_dim.23), calls=%async_computation.2 | async-start | bytes 2097152 | tf_op jit(solution)/shard_map/all_to_all | solution.py:17
  47.0 2.8 %pad_maximum_fusion.refs_0_ = bf16[192,6144]{1,0:T(8,128)(2,1)} fusion(bf16[192,2048]{1,0:T(8,128)(2,1)S(1)} %bitcast.75, bf16[192,2048]{1,0:T(8,128)(2,1)S(1)} %bitcast.76, bf16[192,2048]{1,0:T(8,128)(2,1)} %bitcast.77), kind=kLoop, calls=%fused_computation.2 | loop fusion | flops 7077888 | bytes 4718592 | tf_op jit(solution)/shard_map/concatenate | solution.py:223
  49.8 2.2 collective-permute-start.1
  52.0 4.3 %collective-permute-start.2 = (bf16[192,6144]{1,0:T(8,128)(2,1)}, bf16[192,6144]{1,0:T(8,128)(2,1)}, u32[]{:S(2)}, u32[]{:S(2)}) collective-permute-start(bf16[192,6144]{1,0:T(8,128)(2,1)} %pad_maximum_fusion.refs_0_), channel_id=1, source_target_pairs={{0,3},{1,0},{2,1},{3,2},{4,7},{5,4},{6,5},{7,6},{8,11},{9,8},{10,9... | collective-permute-start | bytes 7077896 | tf_op jit(solution)/shard_map/ppermute | solution.py:225
  56.3 6.0 %collective-permute-start = (bf16[1024,256]{1,0:T(8,128)(2,1)S(1)}, bf16[1024,256]{1,0:T(8,128)(2,1)}, u32[]{:S(2)}, u32[]{:S(2)}) collective-permute-start(bf16[1024,256]{1,0:T(8,128)(2,1)S(1)} %constant_dynamic-slice_fusion), channel_id=1, source_target_pairs={{0,4},{4,0},{1,5},{5,1},{2,6},{6,2},{3,7},{7,3},{8,12},{12,8},{9,1... | collective-permute-start | bytes 1572872 | tf_op jit(solution)/shard_map/ppermute | solution.py:275
  62.5 0.7 pad_add_fusion.where_ref
  63.2 8.4 %all-to-all-done.2.spread_ref = bf16[64,32,256]{2,1,0:T(8,128)(2,1)} async-done(((bf16[64,32,256]{2,1,0:T(8,128)(2,1)}), bf16[64,32,256]{2,1,0:T(8,128)(2,1)}, u32[]{:S(2)}, u32[]{:S(2)}) %all-to-all-start.2) | async-done | bytes 1048608 | tf_op jit(solution)/shard_map/all_to_all | solution.py:17
  71.6 4.4 %attend_part.1 = bf16[4,32,1152]{2,1,0:T(8,128)(2,1)} custom-call(s32[2]{0:T(128)} %pad_add_fusion.where_ref, bf16[4,160,256]{2,1,0:T(8,128)(2,1)} %copy-done, bf16[64,32,256]{2,1,0:T(8,128)(2,1)} %all-to-all-done.2.spread_ref), custom_call_target="tpu_custom_call" | custom-call | tf_op jit(solution)/shard_map/attend_part/pallas_call | solution.py:128
  76.0 3.6 %all-to-all-start.3 = ((bf16[4,32,1152]{2,1,0:T(8,128)(2,1)}), bf16[4,32,1152]{2,1,0:T(8,128)(2,1)S(1)}, u32[]{:S(2)}, u32[]{:S(2)}) async-start(bf16[4,32,1152]{2,1,0:T(8,128)(2,1)} %attend_part.1), calls=%async_computation.3 | async-start | bytes 589824 | tf_op jit(solution)/shard_map/all_to_all | solution.py:17
  79.9 25.7 %all-to-all-done.3 = bf16[4,32,1152]{2,1,0:T(8,128)(2,1)S(1)} async-done(((bf16[4,32,1152]{2,1,0:T(8,128)(2,1)}), bf16[4,32,1152]{2,1,0:T(8,128)(2,1)S(1)}, u32[]{:S(2)}, u32[]{:S(2)}) %all-to-all-start.3) | async-done | bytes 294944 | tf_op jit(solution)/shard_map/all_to_all | solution.py:17
  106.2 0.7 broadcast_in_dim.24
  107.0 5.0 %all-to-all-start.4 = ((bf16[4,32,1024]{2,1,0:T(8,128)(2,1)}), bf16[4,32,1024]{2,1,0:T(8,128)(2,1)S(1)}, u32[]{:S(2)}, u32[]{:S(2)}) async-start(bf16[4,32,1024]{2,1,0:T(8,128)(2,1)} %broadcast_in_dim.24), calls=%async_computation.4 | async-start | bytes 524288 | tf_op jit(solution)/shard_map/all_to_all | solution.py:17
  112.0 5.5 %all-to-all-done.4 = bf16[4,32,1024]{2,1,0:T(8,128)(2,1)S(1)} async-done(((bf16[4,32,1024]{2,1,0:T(8,128)(2,1)}), bf16[4,32,1024]{2,1,0:T(8,128)(2,1)S(1)}, u32[]{:S(2)}, u32[]{:S(2)}) %all-to-all-start.4) | async-done | bytes 262176 | tf_op jit(solution)/shard_map/all_to_all | solution.py:17
  117.5 0.2 fusion.1
  117.7 1.3 fusion.2
  119.0 0.7 copy.52
  119.7 10.1 %all-to-all-start.5 = ((bf16[8,32,256]{2,1,0:T(8,128)(2,1)}), bf16[8,32,256]{2,1,0:T(8,128)(2,1)S(1)}, u32[]{:S(2)}, u32[]{:S(2)}) async-start(bf16[8,32,256]{2,1,0:T(8,128)(2,1)} %bitcast.22), calls=%async_computation.5 | async-start | bytes 262144 | tf_op jit(solution)/shard_map/all_to_all | solution.py:17
  129.9 5.1 %all-to-all-done.5 = bf16[8,32,256]{2,1,0:T(8,128)(2,1)S(1)} async-done(((bf16[8,32,256]{2,1,0:T(8,128)(2,1)}), bf16[8,32,256]{2,1,0:T(8,128)(2,1)S(1)}, u32[]{:S(2)}, u32[]{:S(2)}) %all-to-all-start.5) | async-done | bytes 131104 | tf_op jit(solution)/shard_map/all_to_all | solution.py:17
  135.2 0.5 convolution_convert_fusion
  135.7 1.5 reshape.155
  137.2 13.1 %all-to-all-start.6 = ((bf16[128,2,2048]{2,1,0:T(2,128)(2,1)}), bf16[128,2,2048]{2,1,0:T(2,128)(2,1)S(1)}, u32[]{:S(2)}, u32[]{:S(2)}) async-start(bf16[128,2,2048]{2,1,0:T(2,128)(2,1)} %reshape.155), calls=%async_computation.6 | async-start | bytes 2097152 | tf_op jit(solution)/shard_map/all_to_all | solution.py:17
  150.3 2.4 %slice.122 = bf16[96,6144]{1,0:T(8,128)(2,1)} slice(bf16[192,6144]{1,0:T(8,128)(2,1)} %collective-permute-done.1.refs_1_), slice={[0:96], [0:6144]} | slice | bytes 2359296 | tf_op jit(solution)/shard_map/slice | solution.py:338
  152.8 2.5 %collective-permute-start.3 = (bf16[96,6144]{1,0:T(8,128)(2,1)}, bf16[96,6144]{1,0:T(8,128)(2,1)S(1)}, u32[]{:S(2)}, u32[]{:S(2)}) collective-permute-start(bf16[96,6144]{1,0:T(8,128)(2,1)} %slice.122), channel_id=1, source_target_pairs={{0,1},{1,2},{2,3},{3,0},{4,5},{5,6},{6,7},{7,4},{8,9},{9,10},{10,1... | collective-permute-start | bytes 3538952 | tf_op jit(solution)/shard_map/ppermute | solution.py:340
  155.3 2.4 slice.123
  157.7 4.1 %collective-permute-start.4 = (bf16[96,6144]{1,0:T(8,128)(2,1)}, bf16[96,6144]{1,0:T(8,128)(2,1)}, u32[]{:S(2)}, u32[]{:S(2)}) collective-permute-start(bf16[96,6144]{1,0:T(8,128)(2,1)} %slice.123), channel_id=1, source_target_pairs={{0,3},{1,0},{2,1},{3,2},{4,7},{5,4},{6,5},{7,6},{8,11},{9,8},{10,9... | collective-permute-start | bytes 3538952 | tf_op jit(solution)/shard_map/ppermute | solution.py:341
  161.8 19.5 %all-to-all-done.6 = bf16[128,2,2048]{2,1,0:T(2,128)(2,1)S(1)} async-done(((bf16[128,2,2048]{2,1,0:T(2,128)(2,1)}), bf16[128,2,2048]{2,1,0:T(2,128)(2,1)S(1)}, u32[]{:S(2)}, u32[]{:S(2)}) %all-to-all-start.6) | async-done | bytes 1048608 | tf_op jit(solution)/shard_map/all_to_all | solution.py:17
  181.3 0.4 reshape.156.rows_ref
  181.7 1.0 collective-permute-done.3.refs_3_
  182.7 3.5 %collective-permute-done.4.refs_4_ = bf16[96,6144]{1,0:T(8,128)(2,1)} collective-permute-done((bf16[96,6144]{1,0:T(8,128)(2,1)}, bf16[96,6144]{1,0:T(8,128)(2,1)}, u32[]{:S(2)}, u32[]{:S(2)}) %collective-permute-start.4) | collective-permute-done | bytes 1179680 | tf_op jit(solution)/shard_map/ppermute | solution.py:341
  186.2 5.7 %experts_forward.1 = bf16[256,2048]{1,0:T(8,128)(2,1)S(1)} custom-call(bf16[256,2048]{1,0:T(8,128)(2,1)S(1)} %reshape.156.rows_ref, bf16[192,6144]{1,0:T(8,128)(2,1)} %pad_maximum_fusion.refs_0_, bf16[192,6144]{1,0:T(8,128)(2,1)} %collective-permute-done.1.refs_1_, bf16[192,6144]{1,0:T(8,128)(2,1)} %collective-permute-done.2.refs_2_, ...), custom_call_target="tpu_custom_call" | custom-call | tf_op jit(solution)/shard_map/experts_forward/pallas_call | solution.py:181
  192.0 1.5 reshape.157
  193.5 15.4 %all-to-all-start.7 = ((bf16[128,2,2048]{2,1,0:T(2,128)(2,1)}), bf16[128,2,2048]{2,1,0:T(2,128)(2,1)S(1)}, u32[]{:S(2)}, u32[]{:S(2)}) async-start(bf16[128,2,2048]{2,1,0:T(2,128)(2,1)} %reshape.157), calls=%async_computation.7 | async-start | bytes 2097152 | tf_op jit(solution)/shard_map/all_to_all | solution.py:17
  209.1 30.7 %all-to-all-done.7 = bf16[128,2,2048]{2,1,0:T(2,128)(2,1)S(1)} async-done(((bf16[128,2,2048]{2,1,0:T(2,128)(2,1)}), bf16[128,2,2048]{2,1,0:T(2,128)(2,1)S(1)}, u32[]{:S(2)}, u32[]{:S(2)}) %all-to-all-start.7) | async-done | bytes 1048608 | tf_op jit(solution)/shard_map/all_to_all | solution.py:17
  239.8 0.4 reshape.158
  240.2 0.3 fusion.53
  240.5 0.7 fusion.23
  (70 shorter events, 2.7 us)
Async XLA Ops:
  0.0 16.8 %copy-start.10 = (bf16[32,2048]{1,0:T(8,128)(2,1)S(1)}, bf16[32,2048]{1,0:T(8,128)(2,1)}, u32[]{:S(2)}) copy-start(bf16[32,2048]{1,0:T(8,128)(2,1)} %param.15) | copy-start | bytes 393220
  0.0 16.8 %copy-start.9 = (bf16[32,2048]{1,0:T(8,128)(2,1)S(1)}, bf16[32,2048]{1,0:T(8,128)(2,1)}, u32[]{:S(2)}) copy-start(bf16[32,2048]{1,0:T(8,128)(2,1)} %param.16) | copy-start | bytes 393220
  2.9 11.8 %all-to-all-start = ((bf16[4,2,16,2048]{3,2,1,0:T(8,128)(2,1)}), bf16[4,2,16,2048]{3,2,1,0:T(8,128)(2,1)S(1)}, u32[]{:S(2)}, u32[]{:S(2)}) async-start(bf16[4,2,16,2048]{3,2,1,0:T(8,128)(2,1)} %broadcast_in_dim.21), calls=%async_computation | async-start | bytes 1048576 | tf_op jit(solution)/shard_map/all_to_all | solution.py:17
  17.3 29.6 %copy-start.4 = (bf16[1,192,2048]{2,1,0:T(8,128)(2,1)S(1)}, bf16[1,192,2048]{2,1,0:T(8,128)(2,1)}, u32[]{:S(2)}) copy-start(bf16[1,192,2048]{2,1,0:T(8,128)(2,1)} %param.23) | copy-start | bytes 2359300
  17.3 29.6 %copy-start.5 = (bf16[1,192,2048]{2,1,0:T(8,128)(2,1)S(1)}, bf16[1,192,2048]{2,1,0:T(8,128)(2,1)}, u32[]{:S(2)}) copy-start(bf16[1,192,2048]{2,1,0:T(8,128)(2,1)} %param.22) | copy-start | bytes 2359300
  18.0 9.3 %all-to-all-start.1 = ((bf16[4,160,256]{2,1,0:T(8,128)(2,1)}), bf16[4,160,256]{2,1,0:T(8,128)(2,1)S(1)}, u32[]{:S(2)}, u32[]{:S(2)}) async-start(bf16[4,160,256]{2,1,0:T(8,128)(2,1)} %fusion.9), calls=%async_computation.1 | async-start | bytes 655360 | tf_op jit(solution)/shard_map/all_to_all | solution.py:17
  27.4 22.4 %copy-start = (bf16[4,160,256]{2,1,0:T(8,128)(2,1)}, bf16[4,160,256]{2,1,0:T(8,128)(2,1)S(1)}, u32[]{:S(2)}) copy-start(bf16[4,160,256]{2,1,0:T(8,128)(2,1)S(1)} %all-to-all-done.1.swapped_ref) | copy-start | bytes 983044
  28.9 42.6 %all-to-all-start.2 = ((bf16[64,32,256]{2,1,0:T(8,128)(2,1)}), bf16[64,32,256]{2,1,0:T(8,128)(2,1)}, u32[]{:S(2)}, u32[]{:S(2)}) async-start(bf16[64,32,256]{2,1,0:T(8,128)(2,1)} %broadcast_in_dim.23), calls=%async_computation.2 | async-start | bytes 2097152 | tf_op jit(solution)/shard_map/all_to_all | solution.py:17
  46.9 9.3 %copy-start.1 = (bf16[2048,256]{1,0:T(8,128)(2,1)S(1)}, bf16[2048,256]{1,0:T(8,128)(2,1)}, u32[]{:S(2)}) copy-start(bf16[2048,256]{1,0:T(8,128)(2,1)} %param.17) | copy-start | bytes 3145732
  46.9 15.4 %copy-start.6 = (s32[1,16,8]{1,2,0:T(8,128)S(1)}, s32[1,16,8]{1,2,0:T(8,128)}, u32[]{:S(2)}) copy-start(s32[1,16,8]{1,2,0:T(8,128)} %param.19) | copy-start | bytes 1540
  49.8 100.5 %collective-permute-start.1 = (bf16[192,6144]{1,0:T(8,128)(2,1)}, bf16[192,6144]{1,0:T(8,128)(2,1)}, u32[]{:S(2)}, u32[]{:S(2)}) collective-permute-start(bf16[192,6144]{1,0:T(8,128)(2,1)} %pad_maximum_fusion.refs_0_), channel_id=1, source_target_pairs={{0,1},{1,2},{2,3},{3,0},{4,5},{5,6},{6,7},{7,4},{8,9},{9,10},{10,1... | collective-permute-start | bytes 7077896 | tf_op jit(solution)/shard_map/ppermute | solution.py:224
  52.0 103.4 %collective-permute-start.2 = (bf16[192,6144]{1,0:T(8,128)(2,1)}, bf16[192,6144]{1,0:T(8,128)(2,1)}, u32[]{:S(2)}, u32[]{:S(2)}) collective-permute-start(bf16[192,6144]{1,0:T(8,128)(2,1)} %pad_maximum_fusion.refs_0_), channel_id=1, source_target_pairs={{0,3},{1,0},{2,1},{3,2},{4,7},{5,4},{6,5},{7,6},{8,11},{9,8},{10,9... | collective-permute-start | bytes 7077896 | tf_op jit(solution)/shard_map/ppermute | solution.py:225
  56.3 61.4 %collective-permute-start = (bf16[1024,256]{1,0:T(8,128)(2,1)S(1)}, bf16[1024,256]{1,0:T(8,128)(2,1)}, u32[]{:S(2)}, u32[]{:S(2)}) collective-permute-start(bf16[1024,256]{1,0:T(8,128)(2,1)S(1)} %constant_dynamic-slice_fusion), channel_id=1, source_target_pairs={{0,4},{4,0},{1,5},{5,1},{2,6},{6,2},{3,7},{7,3},{8,12},{12,8},{9,1... | collective-permute-start | bytes 1572872 | tf_op jit(solution)/shard_map/ppermute | solution.py:275
  76.0 41.5 %copy-start.2 = (bf16[2048,256]{1,0:T(8,128)(2,1)S(1)}, bf16[2048,256]{1,0:T(8,128)(2,1)}, u32[]{:S(2)}) copy-start(bf16[2048,256]{1,0:T(8,128)(2,1)} %param.17) | copy-start | bytes 3145732
  76.0 29.6 %all-to-all-start.3 = ((bf16[4,32,1152]{2,1,0:T(8,128)(2,1)}), bf16[4,32,1152]{2,1,0:T(8,128)(2,1)S(1)}, u32[]{:S(2)}, u32[]{:S(2)}) async-start(bf16[4,32,1152]{2,1,0:T(8,128)(2,1)} %attend_part.1), calls=%async_computation.3 | async-start | bytes 589824 | tf_op jit(solution)/shard_map/all_to_all | solution.py:17
  106.2 28.8 %copy-start.3 = (bf16[2,16,2048]{2,1,0:T(8,128)(2,1)S(1)}, bf16[2,16,2048]{2,1,0:T(8,128)(2,1)}, u32[]{:S(2)}) copy-start(bf16[2,16,2048]{2,1,0:T(8,128)(2,1)} %param.12) | copy-start | bytes 393220
  107.0 28.2 %copy-start.7 = (f32[2048]{0:T(1024)S(1)}, f32[2048]{0:T(1024)}, u32[]{:S(2)}) copy-start(f32[2048]{0:T(1024)} %param.18) | copy-start | bytes 24580
  107.0 10.5 %all-to-all-start.4 = ((bf16[4,32,1024]{2,1,0:T(8,128)(2,1)}), bf16[4,32,1024]{2,1,0:T(8,128)(2,1)S(1)}, u32[]{:S(2)}, u32[]{:S(2)}) async-start(bf16[4,32,1024]{2,1,0:T(8,128)(2,1)} %broadcast_in_dim.24), calls=%async_computation.4 | async-start | bytes 524288 | tf_op jit(solution)/shard_map/all_to_all | solution.py:17
  119.7 15.3 %all-to-all-start.5 = ((bf16[8,32,256]{2,1,0:T(8,128)(2,1)}), bf16[8,32,256]{2,1,0:T(8,128)(2,1)S(1)}, u32[]{:S(2)}, u32[]{:S(2)}) async-start(bf16[8,32,256]{2,1,0:T(8,128)(2,1)} %bitcast.22), calls=%async_computation.5 | async-start | bytes 262144 | tf_op jit(solution)/shard_map/all_to_all | solution.py:17
  137.2 44.0 %all-to-all-start.6 = ((bf16[128,2,2048]{2,1,0:T(2,128)(2,1)}), bf16[128,2,2048]{2,1,0:T(2,128)(2,1)S(1)}, u32[]{:S(2)}, u32[]{:S(2)}) async-start(bf16[128,2,2048]{2,1,0:T(2,128)(2,1)} %reshape.155), calls=%async_computation.6 | async-start | bytes 2097152 | tf_op jit(solution)/shard_map/all_to_all | solution.py:17
  152.8 29.9 %collective-permute-start.3 = (bf16[96,6144]{1,0:T(8,128)(2,1)}, bf16[96,6144]{1,0:T(8,128)(2,1)S(1)}, u32[]{:S(2)}, u32[]{:S(2)}) collective-permute-start(bf16[96,6144]{1,0:T(8,128)(2,1)} %slice.122), channel_id=1, source_target_pairs={{0,1},{1,2},{2,3},{3,0},{4,5},{5,6},{6,7},{7,4},{8,9},{9,10},{10,1... | collective-permute-start | bytes 3538952 | tf_op jit(solution)/shard_map/ppermute | solution.py:340
  157.7 28.6 %collective-permute-start.4 = (bf16[96,6144]{1,0:T(8,128)(2,1)}, bf16[96,6144]{1,0:T(8,128)(2,1)}, u32[]{:S(2)}, u32[]{:S(2)}) collective-permute-start(bf16[96,6144]{1,0:T(8,128)(2,1)} %slice.123), channel_id=1, source_target_pairs={{0,3},{1,0},{2,1},{3,2},{4,7},{5,4},{6,5},{7,6},{8,11},{9,8},{10,9... | collective-permute-start | bytes 3538952 | tf_op jit(solution)/shard_map/ppermute | solution.py:341
  192.0 16.9 %copy-start.8 = (f32[1,16,8]{1,2,0:T(8,128)S(1)}, f32[1,16,8]{1,2,0:T(8,128)}, u32[]{:S(2)}) copy-start(f32[1,16,8]{1,2,0:T(8,128)} %param.20) | copy-start | bytes 1540
  193.5 46.3 %all-to-all-start.7 = ((bf16[128,2,2048]{2,1,0:T(2,128)(2,1)}), bf16[128,2,2048]{2,1,0:T(2,128)(2,1)S(1)}, u32[]{:S(2)}, u32[]{:S(2)}) async-start(bf16[128,2,2048]{2,1,0:T(2,128)(2,1)} %reshape.157), calls=%async_computation.7 | async-start | bytes 2097152 | tf_op jit(solution)/shard_map/all_to_all | solution.py:17
